TPU v7x, 32 devices: a whole 2x2x4 slice. The times are simulated.
32 devices in a mesh: seq: 8 (over z, y), head: 4 (over x, core).
Axes of the slice: x: 2, y: 2, z: 4, core: 2. Of those that a mesh axis runs over, the one named last changes fastest.
Arguments:
- hidden: bfloat16 [4096, 8192], P('seq', 'head'), may hold values from -6 to 6
- gain: float32 [8192], replicated, may hold values from 0.25 to 1.75
- key_matrix: bfloat16 [8192, 512], P(None, 'head'), may hold values from -0.0625 to 0.0625
- value_matrix: bfloat16 [8192, 512], P(None, 'head'), may hold values from -0.0625 to 0.0625
- queries: bfloat16 [64, 4096], P(None, 'head'), may hold values from -360 to 360
- window_len: int32 [4], P('head'), may hold values from 16 to 64, as said below
- kernel_width: int32 [4], P('head'), may hold values from 1 to 15, as said below
- kept_block_count: int32 [4], P('head'), may hold values from 1 to 16
Outputs:
- block_scores: float32 [4, 32], P('head', 'seq')
- kept_fraction: float32 [4], P('head')
Inputs may be any that keep to these rules, and one draw needn't show every extreme that they name: `window_len`: at least one key-value head uses all 64 window queries. `kernel_width`: odd; at least one key-value head has width 15.
All inputs are finite; a program needn't handle non-finite values.
Results may differ from a plain program's by a relative error of at most 0.0112.
The roundings to bfloat16 on the way count: a program that leaves them out, or rounds other values in their place, can miss the bound.
Values may be sent and summed in bfloat16 or wider, within the bound.
No kernel may reach another device: no remote copies, remote signals or barrier semaphores. Data moves between devices by JAX's collectives and lax.ppermute only.
A program may use at most 128 MiB of HBM per device.

v0:
```python
import jax
import jax.numpy as jnp
from jax import lax
from jax.sharding import PartitionSpec as P

BLK = 128
KERNEL_LIMIT = 15


def with_halo(x, sides, width):
    for axis, dim in sides:
        count, length = (lax.axis_size(axis), x.shape[dim])
        up = [(i, (i + 1) % count) for i in range(count - 1)]
        down = [(j, i) for i, j in up]
        last = lax.slice_in_dim(x, length - width, length, axis=dim)
        leading = lax.slice_in_dim(x, 0, width, axis=dim)
        before = lax.ppermute(last, axis, up)
        after = lax.ppermute(leading, axis, down)
        x = jnp.concatenate([before, x, after], axis=dim)
    return x


def rotate(raw, positions):
    half = raw.shape[1] // 2
    freq = 500000.0 ** (-(jnp.arange(half).astype(jnp.float32) * 2.0) / raw.shape[1])
    angle = positions[:, None] * freq[None, :]
    leading_part = raw[:, :half]
    trailing_part = raw[:, half:]
    return jnp.concatenate(
        [
            leading_part * jnp.cos(angle) - trailing_part * jnp.sin(angle),
            trailing_part * jnp.cos(angle) + leading_part * jnp.sin(angle),
        ],
        axis=1,
    )


def local(
    hidden, gain, key_matrix, value_matrix, queries, window_len, kernel_width, kept_block_count
):
    tok_rows = hidden.shape[0]
    full_width = gain.shape[0]
    head_size = key_matrix.shape[1]
    floats = hidden.astype(jnp.float32)
    sumsq = lax.psum(jnp.sum(floats * floats, axis=1), "head")
    inv_rms = lax.rsqrt(sumsq / full_width + 1e-05)
    joined = jnp.concatenate([key_matrix, value_matrix], axis=1)
    normed = (
        lax.all_gather(hidden, "head", axis=1, tiled=True).astype(jnp.float32) * gain[None, :]
    ).astype(jnp.bfloat16)
    projected = jnp.dot(normed, joined, preferred_element_type=jnp.float32)
    projected = projected * inv_rms[:, None]
    tok_index = lax.axis_index("seq") * tok_rows + jnp.arange(tok_rows)
    positions = tok_index.astype(jnp.float32)
    keys = rotate(projected[:, :head_size], positions).astype(jnp.bfloat16)
    vmag = jnp.mean(jnp.abs(projected[:, head_size:]), axis=1)
    window = queries.shape[0]
    group_heads = queries.shape[1] // head_size
    query_rows = queries.reshape(window * group_heads, head_size)
    scores = lax.dot_general(
        query_rows, keys, (((1,), (1,)), ((), ())), preferred_element_type=jnp.float32
    ) * head_size ** (-0.5)
    total_tokens = tok_rows * lax.axis_size("seq")
    limit = jnp.repeat(total_tokens - window + jnp.arange(window), group_heads)
    allowed = tok_index[None, :] <= limit[:, None]
    scores = jnp.where(allowed, scores, jnp.float32(-1e30))
    local_top = jnp.max(scores, axis=1)
    row_top = lax.pmax(local_top, "seq")
    expo = jnp.exp(scores - row_top[:, None])
    row_total = lax.psum(jnp.sum(expo, axis=1), "seq")
    rescale = jnp.ones_like(row_total)
    used = (jnp.arange(window) >= window - window_len[0]).astype(jnp.float32)
    row_weight = jnp.repeat(used, group_heads) * rescale / row_total
    column = jnp.dot(row_weight, expo, precision=lax.Precision.HIGHEST) * vmag
    reach = (KERNEL_LIMIT - 1) // 2
    padded = with_halo(column, (("seq", 0),), reach)
    kernel_halfspan = (kernel_width[0] - 1) // 2
    pooled = column
    for shift in range(1, reach + 1):
        wider = jnp.maximum(
            jnp.maximum(pooled, padded[reach + shift : reach + shift + tok_rows]),
            padded[reach - shift : reach - shift + tok_rows],
        )
        pooled = jnp.where(shift <= kernel_halfspan, wider, pooled)
    local_blocks = jnp.sum(pooled.reshape(tok_rows // BLK, BLK), axis=1)[None, :]
    everything = lax.all_gather(local_blocks, "seq", axis=1, tiled=True)[0]
    ordered = -jnp.sort(-everything)
    ranks = jnp.arange(ordered.shape[0])
    kept = jnp.sum(jnp.where(ranks < kept_block_count[0], ordered, jnp.float32(0.0)))
    fraction = (kept / jnp.sum(ordered)).reshape(1)
    return (local_blocks, fraction)


def solution(mesh):
    return jax.shard_map(
        local,
        mesh=mesh,
        in_specs=(
            P("seq", "head"),
            P(),
            P(None, "head"),
            P(None, "head"),
            P(None, "head"),
            P("head"),
            P("head"),
            P("head"),
        ),
        out_specs=(P("head", "seq"), P("head")),
        check_vma=False,
    )
```

profile of v0, /device:TPU:0, one launch (start us, length us, event | category | flops | bytes accessed | tf_op | source)
XLA Modules:
  0.0 157.1 jit_solution(7609627779435552544)
XLA Ops:
  7.2 0.7 all-gather.3.cloned.1.call-update
  8.6 1.0 reshape.43
  9.6 0.1 le.16
  10.5 0.1 reshape.42
  11.3 1.2 dynamic-slice
  13.1 2.1 %multiply_reduce_fusion = f32[512]{0:T(512)S(1)} fusion(bf16[512,2048]{1,0:T(8,128)(2,1)} %param.8), kind=kLoop, calls=%fused_computation.6 | loop fusion | flops 3145216 | bytes 2099200 | tf_op jit(solution)/shard_map/reduce_sum | solution.py:45
  15.2 8.4 %psum.14 = f32[512]{0:T(512)S(1)} all-reduce(f32[512]{0:T(512)S(1)} %multiply_reduce_fusion), channel_id=1, replica_groups=mesh['seq'=8,'head'=4] {'head'}, use_global_device_ids=true, to_apply=%region_1.0 | all-reduce | flops 512 | bytes 4096 | tf_op jit(solution)/shard_map/psum | solution.py:45
  23.6 46.9 %all-gather.3.cloned.1.call-done = bf16[512,8192]{1,0:T(8,128)(2,1)} async-done(((bf16[512,2048]{1,0:T(8,128)(2,1)}), bf16[512,8192]{1,0:T(8,128)(2,1)}) %all-gather.3.cloned.1.call-update) | async-done | bytes 8388624 | tf_op jit(solution)/shard_map/all_gather | solution.py:49
  70.6 6.3 %fusion.7 = f32[512,256]{0,1:T(8,128)S(1)} fusion(bf16[8192,128]{1,0:T(8,128)(2,1)S(1)} %copy-done.1, bf16[8192,128]{1,0:T(8,128)(2,1)} %param.10, bf16[512,8192]{1,0:T(8,128)(2,1)} %all-gather.3.cloned.1.call-done, f32[8192]{0:T(1024)S(1)} %copy-done.2, f32[512]{0:T(512)S(1)} %add_rsqrt_fusion), kind=kOutput, calls=%fused_computation.10 | convolution fusion | flops 2168586240 | bytes 13142016 | tf_op jit(solution)/shard_map/dot_general | solution.py:51
  77.0 0.6 fusion.19
  77.5 0.4 fusion.31
  77.9 21.4 %pmax.7 = f32[512]{0:T(512)S(1)} all-reduce(f32[512]{0:T(512)S(1)} %get-tuple-element.13), channel_id=1, replica_groups=mesh['seq'=8,'head'=4] {'seq'}, use_global_device_ids=true, to_apply=%region_3.4 | all-reduce | flops 512 | bytes 4096 | tf_op jit(solution)/shard_map/pmax | solution.py:68
  99.3 0.2 fusion.11
  99.5 17.1 %psum.15 = f32[512]{0:T(512)S(1)} all-reduce(f32[512]{0:T(512)S(1)} %fusion.11), channel_id=1, replica_groups=mesh['seq'=8,'head'=4] {'seq'}, use_global_device_ids=true, to_apply=%region_5.6 | all-reduce | flops 512 | bytes 4096 | tf_op jit(solution)/shard_map/psum | solution.py:70
  116.6 1.0 fusion.10
  117.6 0.1 fusion.30
  117.7 1.3 collective-permute-start
  119.0 4.5 %collective-permute-start.1 = (f32[7]{0:T(128)S(1)}, f32[7]{0:T(128)S(1)}, u32[]{:S(2)}, u32[]{:S(2)}) collective-permute-start(f32[7]{0:T(128)S(1)} %get-tuple-element.12), channel_id=1, source_target_pairs={{0,4},{4,8},{8,12},{12,16},{16,20},{20,24},{24,28},{1,5},{5,9},{9,... | collective-permute-start | bytes 92 | tf_op jit(solution)/shard_map/ppermute | solution.py:17
  123.6 1.3 collective-permute-done.1
  124.9 0.2 bitcast_reduce_fusion
  125.1 0.2 dynamic-update-slice
  125.4 20.0 %all-reduce = f32[32]{0:T(128)S(1)} all-reduce(f32[32]{0:T(128)S(1)} %dynamic-update-slice), channel_id=2, replica_groups=mesh['seq'=8,'head'=4] {'seq'}, use_global_device_ids=true, to_apply=%add | all-reduce | flops 32 | bytes 256
  145.4 1.6 %sort.15 = (f32[32]{0:T(128)S(1)}, s32[32]{0:T(128)}) sort(f32[32]{0:T(128)S(1)} %neg.23, s32[32]{0:T(128)S(1)} %iota.29), dimensions={0}, to_apply=%region_8.9 | sort | flops 160 | bytes 512 | tf_op jit(solution)/shard_map/jit(sort)/sort | solution.py:87
  147.0 0.7 fusion.29
  (23 shorter events, 0.4 us)
Async XLA Ops:
  7.2 63.4 %copy-start.1 = (bf16[8192,128]{1,0:T(8,128)(2,1)S(1)}, bf16[8192,128]{1,0:T(8,128)(2,1)}, u32[]{:S(2)}) copy-start(bf16[8192,128]{1,0:T(8,128)(2,1)} %param.11) | copy-start | bytes 6291460
  7.2 63.4 %copy-start.2 = (f32[8192]{0:T(1024)S(1)}, f32[8192]{0:T(1024)}, u32[]{:S(2)}) copy-start(f32[8192]{0:T(1024)} %param.9) | copy-start | bytes 98308
  7.2 63.4 %all-gather.3.cloned.1.call-start = ((), (), s32[]{:S(2)}) async-start(), calls=%async_computation | async-start | bytes 10485760 | tf_op jit(solution)/shard_map/all_gather | solution.py:49
  117.7 5.9 %collective-permute-start = (f32[7]{0:T(128)S(1)}, f32[7]{0:T(128)S(1)}, u32[]{:S(2)}, u32[]{:S(2)}) collective-permute-start(f32[7]{0:T(128)S(1)} %get-tuple-element.11), channel_id=1, source_target_pairs={{4,0},{8,4},{12,8},{16,12},{20,16},{24,20},{28,24},{5,1},{9,5},{13... | collective-permute-start | bytes 92 | tf_op jit(solution)/shard_map/ppermute | solution.py:18
  119.0 5.8 %collective-permute-start.1 = (f32[7]{0:T(128)S(1)}, f32[7]{0:T(128)S(1)}, u32[]{:S(2)}, u32[]{:S(2)}) collective-permute-start(f32[7]{0:T(128)S(1)} %get-tuple-element.12), channel_id=1, source_target_pairs={{0,4},{4,8},{8,12},{12,16},{16,20},{20,24},{24,28},{1,5},{5,9},{9,... | collective-permute-start | bytes 92 | tf_op jit(solution)/shard_map/ppermute | solution.py:17
  125.1 24.0 %copy-start = (f32[4]{0:T(128)}, f32[4]{0:T(128)S(1)}, u32[]{:S(2)}) copy-start(f32[4]{0:T(128)S(1)} %bitcast_reduce_fusion) | copy-start | bytes 52
Sparse Core Ops, SparseCore 0:
  9.6 60.9 all-gather.2
where the time goes:
time: 157 us
  blocking collectives  66.9 us (43%)
  waiting for transfers between devices  48.9 us (31%)
  between operations  19.3 us (12%)
  matrix products  7.68 us (5%)
  starting transfers between devices  5.88 us (4%)
  other arithmetic  5.53 us (4%)
  local copies, waits for them, and re-layouts  2.88 us (2%)
    all_gather x1, waiting for transfers between devices, local(): lax.all_gather(hidden, 'head', axis=1, tiled=True).astype(jnp.float32)  46.9 us
    pmax x1, blocking collectives, local(): row_top = lax.pmax(local_top, 'seq')  21.4 us
    unnamed x1, blocking collectives  20 us
    psum x1, blocking collectives, local(): row_total = lax.psum(jnp.sum(expo, axis=1), 'seq')  17.1 us
    psum x1, blocking collectives, local(): sumsq = lax.psum(jnp.sum(floats * floats, axis=1), 'head')  8.37 us
    dot_general x1, matrix products, local(): projected = jnp.dot(normed, joined, preferred_element_type=jnp.float32)  6.35 us
    ppermute x1, starting transfers between devices, with_halo(): before = lax.ppermute(last, axis, up)  4.55 us
  transfers between devices with their start and end apart: 3, of which 2 were waited for; matrix products, arithmetic and copies ran while one was open for 3% of the time, Pallas kernels for 0%

commit v1 on v0

v1 whole, which is shorter than its diff:
```python
import jax
import jax.numpy as jnp
from jax import lax
from jax.sharding import PartitionSpec as P

BLK = 128
KERNEL_LIMIT = 15
HALO = 8
CORES = 2
GROUP = 4


def rotary(head_size, positions):
    half = head_size // 2
    freq = 500000.0 ** (-(jnp.arange(half).astype(jnp.float32) * 2.0) / head_size)
    angle = positions[:, None] * freq[None, :]
    return jnp.cos(angle), jnp.sin(angle)


def local(
    hidden, gain, key_matrix, value_matrix, queries, window_len, kernel_width, kept_block_count
):
    tok_rows, feats = hidden.shape
    full_width = gain.shape[0]
    head_size = key_matrix.shape[1]
    n_seq, n_head = lax.axis_size("seq"), lax.axis_size("head")
    n_x = n_head // CORES
    s, h = lax.axis_index("seq"), lax.axis_index("head")
    x, c = h // CORES, h % CORES
    i = s % GROUP
    r = feats // 2
    total_tokens = tok_rows * n_seq

    def shift_x(offset):
        return [
            (a * CORES + b, (a + offset) % n_x * CORES + b) for a in range(n_x) for b in range(CORES)
        ]

    def flip(bit):
        return [(j, j ^ bit) for j in range(n_seq)]

    def rows_at(start, count):
        return jnp.concatenate(
            [
                lax.dynamic_slice_in_dim(key_matrix, start, count, axis=0),
                lax.dynamic_slice_in_dim(value_matrix, start, count, axis=0),
            ],
            axis=1,
        )

    def start_of(chip, j):
        return (chip * CORES + jnp.where(j >= 2, 1 - c, c)) * feats + (j % 2) * r

    crossing = []
    for o in range(1, n_x):
        chip = (x - o) % n_x
        first = lax.ppermute(rows_at(start_of(chip, i), r), "head", shift_x(-o))
        second = lax.ppermute(rows_at(start_of(chip, 3 - i), r), "head", shift_x(-o))
        by_y = lax.ppermute(first, "seq", flip(1))
        by_z = lax.ppermute(first, "seq", flip(2))
        crossing.append((first, by_y, by_z, second))

    before = lax.ppermute(hidden[tok_rows - HALO :], "seq", [(j, j + 1) for j in range(n_seq - 1)])
    after = lax.ppermute(hidden[:HALO], "seq", [(j + 1, j) for j in range(n_seq - 1)])
    mine = jnp.concatenate([before, hidden, after], axis=0)
    other = lax.ppermute(mine, "head", [(j, j ^ 1) for j in range(n_head)])

    mine_f, other_f = mine.astype(jnp.float32), other.astype(jnp.float32)
    sumsq = jnp.sum(mine_f * mine_f, axis=1) + jnp.sum(other_f * other_f, axis=1)
    total_sq = sumsq
    for o in range(1, n_x):
        total_sq = total_sq + lax.ppermute(sumsq, "head", shift_x(o))
    inv_rms = lax.rsqrt(total_sq / full_width + 1e-05)

    mine_at, other_at = h * feats, (h ^ 1) * feats
    mine_gain = lax.dynamic_slice_in_dim(gain, mine_at, feats)
    other_gain = lax.dynamic_slice_in_dim(gain, other_at, feats)
    normed = jnp.concatenate(
        [
            (mine_f * mine_gain[None, :]).astype(jnp.bfloat16),
            (other_f * other_gain[None, :]).astype(jnp.bfloat16),
        ],
        axis=1,
    )

    def dot(a, b):
        return jnp.dot(a, b, preferred_element_type=jnp.float32)

    projected = dot(normed[:, :feats], rows_at(mine_at, feats))
    projected = projected + dot(normed[:, feats:], rows_at(other_at, feats))
    slabs = [lax.dynamic_slice_in_dim(normed, (i ^ k) * r, r, axis=1) for k in range(GROUP)]
    for o in range(1, n_x):
        partial = sum(dot(a, b) for a, b in zip(slabs, crossing[o - 1]))
        projected = projected + lax.ppermute(
            partial.astype(jnp.bfloat16), "head", shift_x(o)
        ).astype(jnp.float32)

    projected = projected * inv_rms[:, None]
    span = tok_rows + 2 * HALO
    tok_index = s * tok_rows - HALO + jnp.arange(span)
    cos, sin = rotary(head_size, tok_index.astype(jnp.float32))
    half = head_size // 2
    lead, trail = projected[:, :half], projected[:, half:head_size]
    keys = jnp.concatenate([lead * cos - trail * sin, trail * cos + lead * sin], axis=1)
    keys = keys.astype(jnp.bfloat16)
    vmag = jnp.mean(jnp.abs(projected[:, head_size:]), axis=1)

    window = queries.shape[0]
    group_heads = queries.shape[1] // head_size
    query_rows = queries.reshape(window * group_heads, head_size)
    scores = lax.dot_general(
        keys, query_rows, (((1,), (1,)), ((), ())), preferred_element_type=jnp.float32
    ) * head_size ** (-0.5)
    row_window = jnp.arange(window * group_heads) // group_heads
    limit = total_tokens - window + row_window
    allowed = (tok_index[:, None] <= limit[None, :]) & (tok_index[:, None] >= 0)
    scores = jnp.where(allowed, scores, jnp.float32(-1e30))
    top = jnp.max(scores, axis=0)
    expo = jnp.exp(scores - top[None, :])
    own_total = jnp.sum(expo[HALO : HALO + tok_rows], axis=0)
    stats = jnp.broadcast_to(jnp.stack([top, own_total])[None], (n_seq, 2, top.shape[0]))
    stats = lax.all_to_all(stats, "seq", 0, 0, tiled=True)
    row_top = jnp.max(stats[:, 0], axis=0)
    row_total = jnp.sum(stats[:, 1] * jnp.exp(stats[:, 0] - row_top[None, :]), axis=0)
    used = (row_window >= window - window_len[0]).astype(jnp.float32)
    row_weight = used * jnp.exp(top - row_top) / row_total
    column = (
        lax.dot_general(
            row_weight[None, :], expo, (((1,), (1,)), ((), ())), precision=lax.Precision.HIGHEST
        )[0]
        * vmag
    )
    reach = (KERNEL_LIMIT - 1) // 2
    kernel_halfspan = (kernel_width[0] - 1) // 2
    pooled = column[HALO : HALO + tok_rows]
    for shift in range(1, reach + 1):
        wider = jnp.maximum(
            jnp.maximum(pooled, column[HALO + shift : HALO + shift + tok_rows]),
            column[HALO - shift : HALO - shift + tok_rows],
        )
        pooled = jnp.where(shift <= kernel_halfspan, wider, pooled)
    local_blocks = jnp.sum(pooled.reshape(tok_rows // BLK, BLK), axis=1)[None, :]
    spread = jnp.broadcast_to(local_blocks, (n_seq, local_blocks.shape[1]))
    everything = lax.all_to_all(spread, "seq", 0, 0, tiled=True).reshape(-1)
    ordered = -jnp.sort(-everything)
    ranks = jnp.arange(ordered.shape[0])
    kept = jnp.sum(jnp.where(ranks < kept_block_count[0], ordered, jnp.float32(0.0)))
    fraction = (kept / jnp.sum(ordered)).reshape(1)
    return (local_blocks, fraction)


def solution(mesh):
    return jax.shard_map(
        local,
        mesh=mesh,
        in_specs=(
            P("seq", "head"),
            P(),
            P(None, "head"),
            P(None, "head"),
            P(None, "head"),
            P("head"),
            P("head"),
            P("head"),
        ),
        out_specs=(P("head", "seq"), P("head")),
        check_vma=False,
    )
```

time: 157 us -> 83.2 us (0.53)
  blocking collectives: 66.9 us -> 0 us
  starting transfers between devices: 5.88 us -> 22.7 us
  waiting for transfers between devices: 48.9 us -> 32.7 us
  between operations: 19.3 us -> 5.41 us
  local copies, waits for them, and re-layouts: 2.88 us -> 6.96 us
  other arithmetic: 5.53 us -> 7.52 us
    all_gather x1 -> x0, waiting for transfers between devices: 46.9 us -> none  [local(): lax.all_gather(hidden, 'head', axis=1, tiled=True).astype(jnp.float32)]
    psum x2 -> x0, blocking collectives: 25.5 us -> none  [the longest x1 17.1 us: local(): row_total = lax.psum(jnp.sum(expo, axis=1), 'seq')]
    pmax x1 -> x0, blocking collectives: 21.4 us -> none  [local(): row_top = lax.pmax(local_top, 'seq')]
    unnamed x1 -> x0, blocking collectives: 20 us -> none
    ppermute x2 -> x9, waiting for transfers between devices: 1.27 us -> 20.4 us  [the longest x1 8.79 us: local(): first = lax.ppermute(rows_at(start_of(chip, i), r), 'head', shift_x(-o))]
    all_to_all x0 -> x2, waiting for transfers between devices: none -> 12.3 us  [the longest x1 6.51 us: local(): stats = lax.all_to_all(stats, 'seq', 0, 0, tiled=True)]
    ppermute x2 -> x9, starting transfers between devices: 5.84 us -> 14.4 us  [the longest x1 4.89 us: local(): lax.ppermute(hidden[tok_rows - HALO:], 'seq', [(j, j + 1) for j in range(...]
    all_to_all x0 -> x2, starting transfers between devices: none -> 8.28 us  [the longest x1 4.95 us: local(): stats = lax.all_to_all(stats, 'seq', 0, 0, tiled=True)]
  transfers between devices with their start and end apart: 3 -> 11, of which waited for: 2 -> 9; matrix products, arithmetic and copies ran while one was open for 3% -> 15% of each run, Pallas kernels for 0% -> 0%
where the time goes in v1:
time: 83.2 us; the launch traced here: 82.6 us
  waiting for transfers between devices  32.7 us (39%)
  starting transfers between devices  22.7 us (27%)
  other arithmetic  7.52 us (9%)
  matrix products  7.28 us (9%)
  local copies, waits for them, and re-layouts  6.96 us (8%)
  between operations  5.41 us (7%)
    ppermute x1, waiting for transfers between devices, local(): first = lax.ppermute(rows_at(start_of(chip, i), r), 'head', shift_x(-o))  8.79 us
    all_to_all x1, waiting for transfers between devices, local(): stats = lax.all_to_all(stats, 'seq', 0, 0, tiled=True)  6.51 us
    dot_general x6, matrix products, dot(): return jnp.dot(a, b, preferred_element_type=jnp.float32)  5.81 us
    all_to_all x1, waiting for transfers between devices, local(): everything = lax.all_to_all(spread, 'seq', 0, 0, tiled=True).reshape(-1)  5.78 us
    all_to_all x1, starting transfers between devices, local(): stats = lax.all_to_all(stats, 'seq', 0, 0, tiled=True)  4.95 us
    ppermute x1, starting transfers between devices, local(): lax.ppermute(hidden[tok_rows - HALO:], 'seq', [(j, j + 1) for j in range(...  4.89 us
    ppermute x1, waiting for transfers between devices, local(): total_sq = total_sq + lax.ppermute(sumsq, 'head', shift_x(o))  3.73 us
    all_to_all x1, starting transfers between devices, local(): everything = lax.all_to_all(spread, 'seq', 0, 0, tiled=True).reshape(-1)  3.33 us
  transfers between devices with their start and end apart: 11, of which 9 were waited for; matrix products, arithmetic and copies ran while one was open for 15% of the time, Pallas kernels for 0%

profile of v1, /device:TPU:0, one launch (start us, length us, event | category | flops | bytes accessed | tf_op | source)
XLA Modules:
  0.0 82.6 jit_solution(5485509868523665183)
XLA Ops:
  1.4 4.9 %collective-permute-start = (bf16[8,2048]{1,0:T(8,128)(2,1)S(1)}, bf16[8,2048]{1,0:T(8,128)(2,1)S(1)}, u32[]{:S(2)}, u32[]{:S(2)}) collective-permute-start(bf16[8,2048]{1,0:T(8,128)(2,1)S(1)} %get-tuple-element.20), channel_id=1, source_target_pairs={{0,4},{4,8},{8,12},{12,16},{16,20},{20,24},{24,28},{1,5},{5,9},{9,... | collective-permute-start | bytes 98312 | tf_op jit(solution)/shard_map/ppermute | solution.py:63
  6.3 1.3 %collective-permute-start.1 = (bf16[8,2048]{1,0:T(8,128)(2,1)S(1)}, bf16[8,2048]{1,0:T(8,128)(2,1)S(1)}, u32[]{:S(2)}, u32[]{:S(2)}) collective-permute-start(bf16[8,2048]{1,0:T(8,128)(2,1)S(1)} %get-tuple-element.19), channel_id=1, source_target_pairs={{4,0},{8,4},{12,8},{16,12},{20,16},{24,20},{28,24},{5,1},{9,5},{13... | collective-permute-start | bytes 98312 | tf_op jit(solution)/shard_map/ppermute | solution.py:64
  7.9 1.8 %constant_dynamic-update-slice_fusion.1 = bf16[528,2048]{1,0:T(8,128)(2,1)S(1)} fusion(bf16[528,2048]{1,0:T(8,128)(2,1)S(1)} %constant_dynamic-update-slice_fusion.2, bf16[512,2048]{1,0:T(8,128)(2,1)} %param.8), kind=kLoop, calls=%fused_computation.64 | loop fusion | bytes 4194304
  9.7 2.4 %collective-permute-done.1 = bf16[8,2048]{1,0:T(8,128)(2,1)S(1)} collective-permute-done((bf16[8,2048]{1,0:T(8,128)(2,1)S(1)}, bf16[8,2048]{1,0:T(8,128)(2,1)S(1)}, u32[]{:S(2)}, u32[]{:S(2)}) %collective-permute-start.1) | collective-permute-done | bytes 32800 | tf_op jit(solution)/shard_map/ppermute | solution.py:64
  12.2 1.3 %constant_dynamic-slice_fusion.2 = (bf16[1024,128]{1,0:T(8,128)(2,1)S(1)}, bf16[1024,128]{1,0:T(8,128)(2,1)S(1)}, bf16[1024,128]{1,0:T(8,128)(2,1)S(1)}, bf16[1024,128]{1,0:T(8,128)(2,1)S(1)}) fusion(bf16[8192,128]{1,0:T(8,128)(2,1)} %param.11, s32[]{:T(128)S(6)} %select_n.172, s32[]{:T(128)S(6)} %select_n.178, bf16[8192,128]{1,0:T(8,128)(2,1)} %param.10), kind=kLoop, calls=%fused_computation.79 | loop fusion | bytes 2097160 | tf_op jit(solution)/shard_map/dynamic_slice | solution.py:46
  13.5 1.6 %collective-permute-start.3 = (bf16[1024,256]{1,0:T(8,128)(2,1)S(1)}, bf16[1024,256]{1,0:T(8,128)(2,1)}, u32[]{:S(2)}, u32[]{:S(2)}) collective-permute-start(bf16[1024,256]{1,0:T(8,128)(2,1)S(1)} %pad_maximum_fusion), channel_id=1, source_target_pairs={{0,2},{1,3},{2,0},{3,1},{4,6},{5,7},{6,4},{7,5},{8,10},{9,11},{10,... | collective-permute-start | bytes 1572872 | tf_op jit(solution)/shard_map/ppermute | solution.py:57
  17.3 1.7 %constant_dynamic-slice_fusion.6 = (bf16[2048,128]{1,0:T(8,128)(2,1)S(1)}, bf16[2048,128]{1,0:T(8,128)(2,1)S(1)}, bf16[2048,128]{1,0:T(8,128)(2,1)S(1)}, bf16[2048,128]{1,0:T(8,128)(2,1)S(1)}) fusion(bf16[8192,128]{1,0:T(8,128)(2,1)} %param.11, s32[]{:T(128)S(6)} %select_n.163, s32[]{:T(128)S(6)} %select_n.164, bf16[8192,128]{1,0:T(8,128)(2,1)} %param.10), kind=kLoop, calls=%fused_computation.84 | loop fusion | bytes 4194312 | tf_op jit(solution)/shard_map/dynamic_slice | solution.py:46
  19.7 8.8 %collective-permute-done.3 = bf16[1024,256]{1,0:T(8,128)(2,1)} collective-permute-done((bf16[1024,256]{1,0:T(8,128)(2,1)S(1)}, bf16[1024,256]{1,0:T(8,128)(2,1)}, u32[]{:S(2)}, u32[]{:S(2)}) %collective-permute-start.3) | collective-permute-done | bytes 524320 | tf_op jit(solution)/shard_map/ppermute | solution.py:57
  28.5 2.4 %collective-permute-start.4 = (bf16[1024,256]{1,0:T(8,128)(2,1)}, bf16[1024,256]{1,0:T(8,128)(2,1)S(1)}, u32[]{:S(2)}, u32[]{:S(2)}) collective-permute-start(bf16[1024,256]{1,0:T(8,128)(2,1)} %collective-permute-done.3), channel_id=1, source_target_pairs={{0,4},{4,0},{8,12},{12,8},{16,20},{20,16},{24,28},{28,24},{1,5},{5... | collective-permute-start | bytes 1572872 | tf_op jit(solution)/shard_map/ppermute | solution.py:59
  30.9 1.6 %collective-permute-start.5 = (bf16[1024,256]{1,0:T(8,128)(2,1)}, bf16[1024,256]{1,0:T(8,128)(2,1)S(1)}, u32[]{:S(2)}, u32[]{:S(2)}) collective-permute-start(bf16[1024,256]{1,0:T(8,128)(2,1)} %collective-permute-done.3), channel_id=1, source_target_pairs={{0,8},{4,12},{8,0},{12,4},{16,24},{20,28},{24,16},{28,20},{1,9},{5... | collective-permute-start | bytes 1572872 | tf_op jit(solution)/shard_map/ppermute | solution.py:60
  32.5 2.3 %fusion.3 = (f32[528]{0:T(1024)S(1)}, bf16[528,2048]{1,0:T(8,128)(2,1)S(1)}) fusion(bf16[528,2048]{1,0:T(8,128)(2,1)} %collective-permute-done.2, f32[2048]{0:T(1024)S(1)} %get-tuple-element.27), kind=kLoop, calls=%fused_computation.15 | loop fusion | flops 5406192 | bytes 4335680 | tf_op jit(solution)/shard_map/reduce_sum | solution.py:69
  34.8 1.6 %fusion.15 = f32[528,256]{1,0:T(8,128)S(1)} fusion(bf16[1024,256]{1,0:T(8,128)(2,1)} %collective-permute-done.3, s32[]{:T(128)S(6)} %select_n.166, bf16[528,2048]{1,0:T(8,128)(2,1)S(1)} %get-tuple-element.10, bf16[528,2048]{1,0:T(8,128)(2,1)S(1)} %get-tuple-element.8), kind=kOutput, calls=%fused_computation.31 | convolution fusion | flops 278986752 | bytes 5390340 | tf_op jit(solution)/shard_map/dot_general | solution.py:87
  36.4 2.8 %collective-permute-done.6 = bf16[1024,256]{1,0:T(8,128)(2,1)} collective-permute-done((bf16[1024,256]{1,0:T(8,128)(2,1)S(1)}, bf16[1024,256]{1,0:T(8,128)(2,1)}, u32[]{:S(2)}, u32[]{:S(2)}) %collective-permute-start.6) | collective-permute-done | bytes 524320 | tf_op jit(solution)/shard_map/ppermute | solution.py:58
  39.2 1.6 %fusion.17 = f32[528,256]{1,0:T(8,128)S(1)} fusion(bf16[1024,256]{1,0:T(8,128)(2,1)} %collective-permute-done.6, s32[]{:T(128)S(6)} %select_n.175, bf16[528,2048]{1,0:T(8,128)(2,1)S(1)} %get-tuple-element.10, bf16[528,2048]{1,0:T(8,128)(2,1)S(1)} %get-tuple-element.8), kind=kOutput, calls=%fused_computation.32 | convolution fusion | flops 278986752 | bytes 5390340 | tf_op jit(solution)/shard_map/dot_general | solution.py:87
  40.8 1.5 %collective-permute-done.4 = bf16[1024,256]{1,0:T(8,128)(2,1)S(1)} collective-permute-done((bf16[1024,256]{1,0:T(8,128)(2,1)}, bf16[1024,256]{1,0:T(8,128)(2,1)S(1)}, u32[]{:S(2)}, u32[]{:S(2)}) %collective-permute-start.4) | collective-permute-done | bytes 524320 | tf_op jit(solution)/shard_map/ppermute | solution.py:59
  44.4 1.6 %collective-permute-start.7 = (bf16[528,256]{1,0:T(8,128)(2,1)S(1)}, bf16[528,256]{1,0:T(8,128)(2,1)S(1)}, u32[]{:S(2)}, u32[]{:S(2)}) collective-permute-start(bf16[528,256]{1,0:T(8,128)(2,1)S(1)} %fusion.8), channel_id=1, source_target_pairs={{0,2},{1,3},{2,0},{3,1},{4,6},{5,7},{6,4},{7,5},{8,10},{9,11},{10,... | collective-permute-start | bytes 811016 | tf_op jit(solution)/shard_map/ppermute | solution.py:94
  47.2 3.7 %collective-permute-done.8 = f32[528]{0:T(1024)S(1)} collective-permute-done((f32[528]{0:T(1024)S(1)}, f32[528]{0:T(1024)S(1)}, u32[]{:S(2)}, u32[]{:S(2)}) %collective-permute-start.8) | collective-permute-done | bytes 2144 | tf_op jit(solution)/shard_map/ppermute | solution.py:72
  51.7 1.3 %fusion.31 = (bf16[528,64]{1,0:T(8,128)(2,1)S(1)}, bf16[528,64]{1,0:T(8,128)(2,1)S(1)}) fusion(f32[528,256]{1,0:T(8,128)S(1)} %fusion.7, f32[64]{0:T(128)S(1)} %multiply_power_fusion, f32[528]{0:T(1024)S(1)} %fusion.46), kind=kLoop, calls=%fused_computation.50 | loop fusion | flops 304128 | bytes 407872 | tf_op jit(solution)/shard_map/convert
  54.3 4.9 %all-to-all-start = ((f32[8,2,512]{2,1,0:T(2,128)}), f32[8,2,512]{2,1,0:T(2,128)S(1)}, u32[]{:S(2)}, u32[]{:S(2)}) async-start(f32[8,2,512]{2,1,0:T(2,128)} %broadcast_in_dim.14), calls=%async_computation | async-start | bytes 65536 | tf_op jit(solution)/shard_map/all_to_all | solution.py:122
  59.5 6.5 %all-to-all-done = f32[8,2,512]{2,1,0:T(2,128)S(1)} async-done(((f32[8,2,512]{2,1,0:T(2,128)}), f32[8,2,512]{2,1,0:T(2,128)S(1)}, u32[]{:S(2)}, u32[]{:S(2)}) %all-to-all-start) | async-done | bytes 32800 | tf_op jit(solution)/shard_map/all_to_all | solution.py:122
  66.1 1.0 %convolution_reduce_fusion = f32[528]{0:T(1024)S(1)} fusion(f32[512,1]{0,1:T(1,128)S(1)} %bitcast.103, f32[528,512]{1,0:T(8,128)S(1)} %subtract_exponential_fusion), kind=kOutput, calls=%fused_computation.25 | convolution fusion | flops 3244032 | bytes 1085504 | tf_op jit(solution)/shard_map/dot_general | solution.py:128
  67.9 3.3 %all-to-all-start.1 = ((f32[8,1,4]{2,1,0:T(1,128)}), f32[8,1,4]{2,1,0:T(1,128)S(1)}, u32[]{:S(2)}, u32[]{:S(2)}) async-start(f32[8,1,4]{2,1,0:T(1,128)} %broadcast_in_dim.16), calls=%async_computation.1 | async-start | bytes 8192 | tf_op jit(solution)/shard_map/all_to_all | solution.py:144
  71.9 5.8 %all-to-all-done.1 = f32[8,1,4]{2,1,0:T(1,128)S(1)} async-done(((f32[8,1,4]{2,1,0:T(1,128)}), f32[8,1,4]{2,1,0:T(1,128)S(1)}, u32[]{:S(2)}, u32[]{:S(2)}) %all-to-all-start.1) | async-done | bytes 160 | tf_op jit(solution)/shard_map/all_to_all | solution.py:144
  77.8 1.6 %sort.15 = (f32[32]{0:T(128)S(1)}, s32[32]{0:T(128)}) sort(f32[32]{0:T(128)S(1)} %neg.20, s32[32]{0:T(128)S(1)} %iota.31), dimensions={0}, to_apply=%region_8.9 | sort | flops 160 | bytes 512 | tf_op jit(solution)/shard_map/jit(sort)/sort | solution.py:145
  (48 shorter events, 9.9 us)
Async XLA Ops:
  1.4 6.5 %collective-permute-start = (bf16[8,2048]{1,0:T(8,128)(2,1)S(1)}, bf16[8,2048]{1,0:T(8,128)(2,1)S(1)}, u32[]{:S(2)}, u32[]{:S(2)}) collective-permute-start(bf16[8,2048]{1,0:T(8,128)(2,1)S(1)} %get-tuple-element.20), channel_id=1, source_target_pairs={{0,4},{4,8},{8,12},{12,16},{16,20},{20,24},{24,28},{1,5},{5,9},{9,... | collective-permute-start | bytes 98312 | tf_op jit(solution)/shard_map/ppermute | solution.py:63
  6.3 5.8 %collective-permute-start.1 = (bf16[8,2048]{1,0:T(8,128)(2,1)S(1)}, bf16[8,2048]{1,0:T(8,128)(2,1)S(1)}, u32[]{:S(2)}, u32[]{:S(2)}) collective-permute-start(bf16[8,2048]{1,0:T(8,128)(2,1)S(1)} %get-tuple-element.19), channel_id=1, source_target_pairs={{4,0},{8,4},{12,8},{16,12},{20,16},{24,20},{28,24},{5,1},{9,5},{13... | collective-permute-start | bytes 98312 | tf_op jit(solution)/shard_map/ppermute | solution.py:64
  12.1 20.4 %collective-permute-start.2 = (bf16[528,2048]{1,0:T(8,128)(2,1)S(1)}, bf16[528,2048]{1,0:T(8,128)(2,1)}, u32[]{:S(2)}, u32[]{:S(2)}) collective-permute-start(bf16[528,2048]{1,0:T(8,128)(2,1)S(1)} %constant_dynamic-update-slice_fusion), channel_id=1, source_target_pairs={{0,1},{1,0},{2,3},{3,2},{4,5},{5,4},{6,7},{7,6},{8,9},{9,8},{10,11... | collective-permute-start | bytes 6488072 | tf_op jit(solution)/shard_map/ppermute | solution.py:66
  12.1 4.3 %copy-start = (bf16[64,1024]{1,0:T(8,128)(2,1)S(1)}, bf16[64,1024]{1,0:T(8,128)(2,1)}, u32[]{:S(2)}) copy-start(bf16[64,1024]{1,0:T(8,128)(2,1)} %param.12) | copy-start | bytes 393220
  13.5 15.0 %collective-permute-start.3 = (bf16[1024,256]{1,0:T(8,128)(2,1)S(1)}, bf16[1024,256]{1,0:T(8,128)(2,1)}, u32[]{:S(2)}, u32[]{:S(2)}) collective-permute-start(bf16[1024,256]{1,0:T(8,128)(2,1)S(1)} %pad_maximum_fusion), channel_id=1, source_target_pairs={{0,2},{1,3},{2,0},{3,1},{4,6},{5,7},{6,4},{7,5},{8,10},{9,11},{10,... | collective-permute-start | bytes 1572872 | tf_op jit(solution)/shard_map/ppermute | solution.py:57
  15.1 24.1 %collective-permute-start.6 = (bf16[1024,256]{1,0:T(8,128)(2,1)S(1)}, bf16[1024,256]{1,0:T(8,128)(2,1)}, u32[]{:S(2)}, u32[]{:S(2)}) collective-permute-start(bf16[1024,256]{1,0:T(8,128)(2,1)S(1)} %pad_maximum_fusion.1), channel_id=1, source_target_pairs={{0,2},{1,3},{2,0},{3,1},{4,6},{5,7},{6,4},{7,5},{8,10},{9,11},{10,... | collective-permute-start | bytes 1572872 | tf_op jit(solution)/shard_map/ppermute | solution.py:58
  16.5 2.5 %copy-start.1 = (f32[8192]{0:T(1024)S(1)}, f32[8192]{0:T(1024)}, u32[]{:S(2)}) copy-start(f32[8192]{0:T(1024)} %param.9) | copy-start | bytes 98308
  28.5 13.9 %collective-permute-start.4 = (bf16[1024,256]{1,0:T(8,128)(2,1)}, bf16[1024,256]{1,0:T(8,128)(2,1)S(1)}, u32[]{:S(2)}, u32[]{:S(2)}) collective-permute-start(bf16[1024,256]{1,0:T(8,128)(2,1)} %collective-permute-done.3), channel_id=1, source_target_pairs={{0,4},{4,0},{8,12},{12,8},{16,20},{20,16},{24,28},{28,24},{1,5},{5... | collective-permute-start | bytes 1572872 | tf_op jit(solution)/shard_map/ppermute | solution.py:59
  30.9 12.9 %collective-permute-start.5 = (bf16[1024,256]{1,0:T(8,128)(2,1)}, bf16[1024,256]{1,0:T(8,128)(2,1)S(1)}, u32[]{:S(2)}, u32[]{:S(2)}) collective-permute-start(bf16[1024,256]{1,0:T(8,128)(2,1)} %collective-permute-done.3), channel_id=1, source_target_pairs={{0,8},{4,12},{8,0},{12,4},{16,24},{20,28},{24,16},{28,20},{1,9},{5... | collective-permute-start | bytes 1572872 | tf_op jit(solution)/shard_map/ppermute | solution.py:60
  44.4 6.6 %collective-permute-start.7 = (bf16[528,256]{1,0:T(8,128)(2,1)S(1)}, bf16[528,256]{1,0:T(8,128)(2,1)S(1)}, u32[]{:S(2)}, u32[]{:S(2)}) collective-permute-start(bf16[528,256]{1,0:T(8,128)(2,1)S(1)} %fusion.8), channel_id=1, source_target_pairs={{0,2},{1,3},{2,0},{3,1},{4,6},{5,7},{6,4},{7,5},{8,10},{9,11},{10,... | collective-permute-start | bytes 811016 | tf_op jit(solution)/shard_map/ppermute | solution.py:94
  45.9 5.0 %collective-permute-start.8 = (f32[528]{0:T(1024)S(1)}, f32[528]{0:T(1024)S(1)}, u32[]{:S(2)}, u32[]{:S(2)}) collective-permute-start(f32[528]{0:T(1024)S(1)} %add.153), channel_id=1, source_target_pairs={{0,2},{1,3},{2,0},{3,1},{4,6},{5,7},{6,4},{7,5},{8,10},{9,11},{10,... | collective-permute-start | bytes 6344 | tf_op jit(solution)/shard_map/ppermute | solution.py:72
  54.3 11.6 %all-to-all-start = ((f32[8,2,512]{2,1,0:T(2,128)}), f32[8,2,512]{2,1,0:T(2,128)S(1)}, u32[]{:S(2)}, u32[]{:S(2)}) async-start(f32[8,2,512]{2,1,0:T(2,128)} %broadcast_in_dim.14), calls=%async_computation | async-start | bytes 65536 | tf_op jit(solution)/shard_map/all_to_all | solution.py:122
  67.3 14.2 %copy-start.2 = (f32[4]{0:T(128)}, f32[4]{0:T(128)S(1)}, u32[]{:S(2)}) copy-start(f32[4]{0:T(128)S(1)} %fusion.53) | copy-start | bytes 52
  67.9 9.8 %all-to-all-start.1 = ((f32[8,1,4]{2,1,0:T(1,128)}), f32[8,1,4]{2,1,0:T(1,128)S(1)}, u32[]{:S(2)}, u32[]{:S(2)}) async-start(f32[8,1,4]{2,1,0:T(1,128)} %broadcast_in_dim.16), calls=%async_computation.1 | async-start | bytes 8192 | tf_op jit(solution)/shard_map/all_to_all | solution.py:144

commit v2 on v0

v2 whole, which is shorter than its diff:
```python
import functools

import jax
import jax.numpy as jnp
from jax import lax
from jax.experimental import pallas as pl
from jax.experimental.pallas import tpu as pltpu
from jax.sharding import PartitionSpec as P

BLK = 128
LANES = 128
KERNEL_LIMIT = 15
HALO = 8
CORES = 2
GROUP = 4
MASKED = -1e30

VMEM = pl.BlockSpec(memory_space=pltpu.VMEM)
SMEM = pl.BlockSpec(memory_space=pltpu.SMEM)
HBM = pl.BlockSpec(memory_space=pltpu.HBM)
F32, BF16 = jnp.float32, jnp.bfloat16


def sds(shape, dtype):
    return jax.ShapeDtypeStruct(shape, dtype)


def call(body, out, ins, scratch=(), outs=None, flops=1 << 20, limit=40 << 20):
    return pl.pallas_call(
        body,
        out_shape=out,
        in_specs=ins,
        out_specs=outs if outs is not None else jax.tree.map(lambda _: VMEM, out),
        scratch_shapes=list(scratch),
        cost_estimate=pl.CostEstimate(flops=flops, bytes_accessed=1 << 20, transcendentals=0),
        compiler_params=pltpu.CompilerParams(vmem_limit_bytes=limit),
    )


def iota(shape, dim):
    return lax.broadcasted_iota(jnp.int32, shape, dim)


def to_lanes(col):
    n = col.shape[0]
    here = iota((n, LANES), 0) == iota((n, LANES), 1)
    return jnp.sum(jnp.where(here, jnp.broadcast_to(col, (n, LANES)), 0.0), axis=0, keepdims=True)


def to_rows(row, n):
    here = iota((n, LANES), 0) == iota((n, LANES), 1)
    return jnp.sum(jnp.where(here, jnp.broadcast_to(row, (n, LANES)), 0.0), axis=1, keepdims=True)


def pack_kernel(chunks, at, km, vm, *refs):
    outs, sem = refs[:-1], refs[-1]
    head = km.shape[1]
    copies = []
    for which, (out_no, to, count) in enumerate(chunks):
        start = pl.multiple_of(at[which], 128)
        for side, src in enumerate((km, vm)):
            copies.append(
                pltpu.make_async_copy(
                    src.at[pl.ds(start, count)],
                    outs[out_no].at[pl.ds(to, count), pl.ds(side * head, head)],
                    sem.at[2 * which + side],
                )
            )
    for c in copies:
        c.start()
    for c in copies:
        c.wait()


def norm_kernel(
    at, hid, swp, halo, swp_halo, gain, km, vm, normed, sumsq, acc_k, acc_v, wbuf, total, sem
):
    tok, feats = hid.shape
    head = km.shape[1]
    copies = []
    for part in range(CORES):
        start = pl.multiple_of(at[part], 128)
        for side, src in enumerate((km, vm)):
            copies.append(
                pltpu.make_async_copy(
                    src.at[pl.ds(start, feats)],
                    wbuf.at[pl.ds(part * feats, feats), pl.ds(side * head, head)],
                    sem.at[2 * part + side],
                )
            )
    for c in copies:
        c.start()
    sumsq[...] = jnp.zeros_like(sumsq)
    pieces = [(b * LANES, LANES, b) for b in range(tok // LANES)] + [(tok, 2 * HALO, tok // LANES)]
    for row, count, line in pieces:
        folded = jnp.zeros((count, LANES), F32)
        for part, (main, edge) in enumerate(((hid, halo), (swp, swp_halo))):
            for t in range(feats // LANES):
                lanes = pl.ds(t * LANES, LANES)
                raw = (main[pl.ds(row, count), lanes] if row < tok else edge[:, lanes]).astype(F32)
                folded = folded + raw * raw
                g = gain[pl.ds(part, 1), lanes]
                normed[pl.ds(row, count), pl.ds(part * feats + t * LANES, LANES)] = (raw * g).astype(BF16)
        sumsq[pl.ds(line, 1), :] = to_lanes(jnp.sum(folded, axis=1, keepdims=True))
    for c in copies:
        c.wait()
    total[...] = jnp.zeros_like(total)
    step = min(1024, feats)

    def body(k, carry):
        at_k = pl.multiple_of(k * step, 128)
        total[...] += jnp.dot(
            normed[:, pl.ds(at_k, step)], wbuf[pl.ds(at_k, step), :], preferred_element_type=F32
        )
        return carry

    lax.fori_loop(0, CORES * feats // step, body, 0)
    acc_k[...] = total[:, :head]
    acc_v[...] = total[:, head:]


def partial_kernel(r, hw, at, normed, b0, b1, b2, b3, out_k, out_v):
    head = out_k.shape[1]
    total = None
    for k, blk in enumerate((b0, b1, b2, b3)):
        col = pl.multiple_of(at[k], 128)
        p = jnp.dot(normed[:, pl.ds(col, r)], blk[:r, :], preferred_element_type=F32)
        total = p if total is None else total + p
    d2 = hw - 2 * r
    if d2:
        for part in range(CORES):
            total = total + jnp.dot(
                normed[:, pl.ds(part * hw + 2 * r, d2)],
                b3[r + part * d2 : r + (part + 1) * d2, :],
                preferred_element_type=F32,
            )
    out_k[...] = total[:, :head].astype(BF16)
    out_v[...] = total[:, head:].astype(BF16)


def row_scale(sumsq, tok, full_width):
    inv = lax.rsqrt(sumsq / full_width + 1e-05)
    parts = [to_rows(inv[b : b + 1, :], LANES) for b in range(tok // LANES)]
    parts.append(to_rows(inv[tok // LANES : tok // LANES + 1, :], 2 * HALO))
    return parts


def score_kernel(full_width, scale_by, first, *refs):
    n_off = (len(refs) - 9) // 2
    acc, parts, sqs = refs[0], refs[1 : 1 + n_off], refs[1 + n_off : 2 + 2 * n_off]
    cos, sin, q, limit, expo, stats, keys = refs[2 + 2 * n_off :]
    span, head = acc.shape
    tok = span - 2 * HALO
    sumsq = sqs[0][...]
    for sq in sqs[1:]:
        sumsq = sumsq + sq[...]
    row = 0
    for col in row_scale(sumsq, tok, full_width):
        n = col.shape[0]
        k = acc[row : row + n, :]
        for p in parts:
            k = k + p[row : row + n, :].astype(F32)
        k = k * col
        rot = k * cos[row : row + n, :] + pltpu.roll(k, head // 2, 1) * sin[row : row + n, :]
        keys[row : row + n, :] = rot.astype(BF16)
        row += n
    scores = lax.dot_general(
        keys[...], q[...], (((1,), (1,)), ((), ())), preferred_element_type=F32
    ) * scale_by
    idx = iota((span, 1), 0)
    token = jnp.where(idx < tok, first[0] + idx, jnp.where(idx < tok + HALO, first[0] - HALO + idx - tok, first[0] + idx - HALO))
    token = jnp.where(token < 0, jnp.int32(2**30), token)
    scores = jnp.where(token <= limit[...], scores, MASKED)
    top = jnp.max(scores, axis=0, keepdims=True)
    e = jnp.exp(scores - top)
    expo[...] = e
    own = jnp.sum(e[:tok, :], axis=0, keepdims=True)
    for d in range(stats.shape[0]):
        stats[d, 0:1, :] = top
        stats[d, 1:2, :] = own


def pool_kernel(full_width, window, sizes, got, mine, expo, *refs):
    n_off = (len(refs) - 5) // 2
    acc, parts, sqs = refs[0], refs[1 : 1 + n_off], refs[1 + n_off : 2 + 2 * n_off]
    win, blocks, spread = refs[2 + 2 * n_off :]
    span = expo.shape[0]
    tok = span - 2 * HALO
    nb = tok // LANES
    row_top = got[0, 0:1, :]
    for d in range(1, got.shape[0]):
        row_top = jnp.maximum(row_top, got[d, 0:1, :])
    row_total = jnp.zeros_like(row_top)
    for d in range(got.shape[0]):
        row_total = row_total + got[d, 1:2, :] * jnp.exp(got[d, 0:1, :] - row_top)
    weight = jnp.exp(mine[0, 0:1, :] - row_top) / row_total
    weight = jnp.where(win[...] >= window - sizes[0], weight, 0.0)
    sumsq = sqs[0][...]
    for sq in sqs[1:]:
        sumsq = sumsq + sq[...]
    scales = row_scale(sumsq, tok, full_width)
    lines = []
    row = 0
    for col in scales:
        n = col.shape[0]
        v = acc[row : row + n, :]
        for p in parts:
            v = v + p[row : row + n, :].astype(F32)
        vmag = jnp.sum(jnp.abs(v), axis=1, keepdims=True) * (1.0 / v.shape[1]) * col
        mass = jnp.sum(expo[row : row + n, :] * weight, axis=1, keepdims=True)
        lines.append(to_lanes(mass * vmag))
        row += n
    edge = pltpu.roll(lines[nb], LANES - HALO, 1)
    height = -(-(nb + 2) // 8) * 8
    line = iota((height, LANES), 0)
    lane = iota((height, LANES), 1)
    column = jnp.broadcast_to(edge, (height, LANES))
    for b in range(nb):
        column = jnp.where(line == b, jnp.broadcast_to(lines[b], (height, LANES)), column)
    below, above = pltpu.roll(column, height - 1, 0), pltpu.roll(column, 1, 0)
    halfspan = lax.shift_right_arithmetic(sizes[1] - 1, 1)
    pooled = column
    for shift in range(1, (KERNEL_LIMIT - 1) // 2 + 1):
        right = pltpu.roll(jnp.where(lane < shift, below, column), LANES - shift, 1)
        left = pltpu.roll(jnp.where(lane >= LANES - shift, above, column), shift, 1)
        wider = jnp.maximum(jnp.maximum(pooled, right), left)
        pooled = jnp.where(shift <= halfspan, wider, pooled)
    sums = jnp.sum(pooled, axis=1, keepdims=True)
    pick = (line == lax.rem(lane, nb)) & (line < nb)
    flat = jnp.sum(jnp.where(pick, jnp.broadcast_to(sums, (height, LANES)), 0.0), axis=0, keepdims=True)
    blocks[...] = flat[:, :nb]
    spread[...] = jnp.broadcast_to(flat, spread.shape)


def rank_kernel(nb, keep, everything, out):
    v = everything[...]
    n = v.shape[0]
    place = iota(v.shape, 0) * nb + lax.rem(iota(v.shape, 1), nb)
    rank = jnp.zeros(v.shape, jnp.int32)
    for a in range(nb):
        va = pltpu.roll(v, a, 1) if a else v
        pa = pltpu.roll(place, a, 1) if a else place
        for b in range(n):
            vb = pltpu.roll(va, b, 0) if b else va
            pb = pltpu.roll(pa, b, 0) if b else pa
            rank = rank + jnp.where((vb > v) | ((vb == v) & (pb < place)), 1, 0)
    once = iota(v.shape, 1) < nb
    kept = jnp.where(once & (rank < keep[0]), v, 0.0)
    whole = jnp.where(once, v, 0.0)

    def add(t):
        return jnp.sum(jnp.sum(t, axis=1, keepdims=True), axis=0, keepdims=True)

    out[...] = add(kept) / add(whole)


def local(
    hidden, gain, key_matrix, value_matrix, queries, window_len, kernel_width, kept_block_count
):
    tok, feats = hidden.shape
    full_width = gain.shape[0]
    head = key_matrix.shape[1]
    n_seq, n_head = lax.axis_size("seq"), lax.axis_size("head")
    n_x = n_head // CORES
    s, h = lax.axis_index("seq"), lax.axis_index("head")
    x, c = h // CORES, h % CORES
    i = s % GROUP
    r = feats * 7 // 16 // LANES * LANES
    spare = feats - 2 * r
    span = tok + 2 * HALO
    total_tokens = tok * n_seq

    def shift_x(offset):
        return [
            (a * CORES + b, (a + offset) % n_x * CORES + b) for a in range(n_x) for b in range(CORES)
        ]

    def flip(bit):
        return [(j, j ^ bit) for j in range(n_seq)]

    def half_at(chip, part):
        return (chip * CORES + jnp.where(part == 0, c, 1 - c)) * feats

    def block_at(chip, j):
        return half_at(chip, j // 2) + (j % 2) * r

    offsets = range(1, n_x)
    starts, chunks = [], []
    for o in offsets:
        chip = (x - o) % n_x
        starts += [block_at(chip, i), block_at(chip, 3 - i)]
        starts += [half_at(chip, part) + 2 * r for part in range(CORES)]
        a = 2 * (o - 1)
        chunks += [(a, 0, r), (a + 1, 0, r), (a + 1, r, spare), (a + 1, r + spare, spare)]
    rows = [r, r + CORES * spare] * len(offsets)
    packed = call(
        functools.partial(pack_kernel, tuple(chunks)),
        [sds((n, 2 * head), BF16) for n in rows],
        [SMEM, HBM, HBM],
        scratch=[pltpu.SemaphoreType.DMA((2 * len(chunks),))],
        limit=8 << 20,
    )(jnp.stack(starts), key_matrix, value_matrix)

    firsts, seconds = [], []
    for o in offsets:
        firsts.append(lax.ppermute(packed[2 * o - 2], "head", shift_x(-o)))
        seconds.append(lax.ppermute(packed[2 * o - 1], "head", shift_x(-o)))
    swapped = lax.ppermute(hidden, "head", [(j, j ^ 1) for j in range(n_head)])
    before = lax.ppermute(hidden[tok - HALO :], "seq", [(j, j + 1) for j in range(n_seq - 1)])
    after = lax.ppermute(hidden[:HALO], "seq", [(j + 1, j) for j in range(n_seq - 1)])
    halo = jnp.concatenate([before, after], axis=0)
    swapped_halo = lax.ppermute(halo, "head", [(j, j ^ 1) for j in range(n_head)])
    crossing = []
    for o in offsets:
        by_y = lax.ppermute(firsts[o - 1], "seq", flip(1))
        by_z = lax.ppermute(firsts[o - 1], "seq", flip(2))
        crossing.append((firsts[o - 1], by_y, by_z, seconds[o - 1]))

    gains = jnp.stack(
        [lax.dynamic_slice_in_dim(gain, p * feats, feats) for p in (h, h ^ 1)], axis=0
    )
    lines = -(-(tok // LANES + 1) // 8) * 8
    normed, sumsq, acc_k, acc_v = call(
        norm_kernel,
        [
            sds((span, CORES * feats), BF16),
            sds((lines, LANES), F32),
            sds((span, head), F32),
            sds((span, head), F32),
        ],
        [SMEM, VMEM, VMEM, VMEM, VMEM, VMEM, HBM, HBM],
        scratch=[
            pltpu.VMEM((CORES * feats, 2 * head), BF16),
            pltpu.VMEM((span, 2 * head), F32),
            pltpu.SemaphoreType.DMA((2 * CORES,)),
        ],
        flops=1 << 31,
    )(
        jnp.stack([h * feats, (h ^ 1) * feats]),
        hidden, swapped, halo, swapped_halo, gains, key_matrix, value_matrix,
    )
    sqs = [sumsq] + [lax.ppermute(sumsq, "head", shift_x(o)) for o in offsets]

    parts_k, parts_v = [], []
    slabs = jnp.stack([((i ^ k) // 2) * feats + ((i ^ k) % 2) * r for k in range(GROUP)])
    for o in offsets:
        part_k, part_v = call(
            functools.partial(partial_kernel, r, feats),
            [sds((span, head), BF16), sds((span, head), BF16)],
            [SMEM] + [VMEM] * 5,
            flops=1 << 31,
        )(slabs, normed, *crossing[o - 1])
        parts_k.append(lax.ppermute(part_k, "head", shift_x(o)))
        parts_v.append(lax.ppermute(part_v, "head", shift_x(o)))

    half = head // 2
    freq = 500000.0 ** (-(jnp.arange(half).astype(F32) * 2.0) / head)
    at = jnp.arange(span)
    token = s * tok + jnp.where(
        at < tok, at, jnp.where(at < tok + HALO, at - tok - HALO, at - HALO)
    )
    angle = token.astype(F32)[:, None] * freq[None, :]
    cos, sin = jnp.cos(angle), jnp.sin(angle)
    cos = jnp.concatenate([cos, cos], axis=1)
    sin = jnp.concatenate([-sin, sin], axis=1)

    window = queries.shape[0]
    group_heads = queries.shape[1] // head
    rows = window * group_heads
    query_rows = queries.reshape(rows, head)
    row_window = (jnp.arange(rows) // group_heads).astype(jnp.int32)[None, :]
    limit = total_tokens - window + row_window
    expo, stats = call(
        functools.partial(score_kernel, full_width, head ** (-0.5)),
        [sds((span, rows), F32), sds((n_seq, 2, rows), F32)],
        [SMEM] + [VMEM] * (6 + 2 * len(offsets)),
        scratch=[pltpu.VMEM((span, head), BF16)],
        flops=1 << 28,
    )((s * tok).reshape(1), acc_k, *parts_k, *sqs, cos, sin, query_rows, limit)
    got = lax.all_to_all(stats, "seq", 0, 0, tiled=True)
    nb = tok // BLK
    local_blocks, spread = call(
        functools.partial(pool_kernel, full_width, window),
        [sds((1, nb), F32), sds((n_seq, LANES), F32)],
        [SMEM] + [VMEM] * (6 + 2 * len(offsets)),
        flops=1 << 26,
    )(
        jnp.concatenate([window_len, kernel_width]),
        got, stats, expo, acc_v, *parts_v, *sqs, row_window,
    )
    everything = lax.all_to_all(spread, "seq", 0, 0, tiled=True)
    fraction = call(
        functools.partial(rank_kernel, nb), sds((1, 1), F32), [SMEM, VMEM], flops=1 << 20
    )(kept_block_count, everything)
    return (local_blocks, fraction.reshape(1))


def solution(mesh):
    return jax.shard_map(
        local,
        mesh=mesh,
        in_specs=(
            P("seq", "head"),
            P(),
            P(None, "head"),
            P(None, "head"),
            P(None, "head"),
            P("head"),
            P("head"),
            P("head"),
        ),
        out_specs=(P("head", "seq"), P("head")),
        check_vma=False,
    )
```

time: 157 us -> 77.4 us (0.49)
  blocking collectives: 66.9 us -> 0 us
  waiting for transfers between devices: 48.9 us -> 24.4 us
  starting transfers between devices: 5.88 us -> 26.1 us
  between operations: 19.3 us -> 2.88 us
  Pallas kernels: 0 us -> 14.6 us
  matrix products: 7.68 us -> 0 us
  local copies, waits for them, and re-layouts: 2.88 us -> 7.24 us
  other arithmetic: 5.53 us -> 1.59 us
    all_gather x1 -> x0, waiting for transfers between devices: 46.9 us -> none  [local(): lax.all_gather(hidden, 'head', axis=1, tiled=True).astype(jnp.float32)]
    psum x2 -> x0, blocking collectives: 25.5 us -> none  [the longest x1 17.1 us: local(): row_total = lax.psum(jnp.sum(expo, axis=1), 'seq')]
    pmax x1 -> x0, blocking collectives: 21.4 us -> none  [local(): row_top = lax.pmax(local_top, 'seq')]
    unnamed x1 -> x0, blocking collectives: 20 us -> none
    pallas_call x0 -> x6, Pallas kernels: none -> 14.6 us  [the longest x1 5.79 us: local(): call(norm_kernel, [sds((span, CORES * feats), BF16), sds((lines, LANES),...]
    all_to_all x0 -> x2, waiting for transfers between devices: none -> 12.4 us  [the longest x1 6.61 us: local(): got = lax.all_to_all(stats, 'seq', 0, 0, tiled=True)]
    ppermute x2 -> x11, waiting for transfers between devices: 1.27 us -> 12 us  [the longest x1 10 us: local(): firsts.append(lax.ppermute(packed[2 * o - 2], 'head', shift_x(-o)))]
    ppermute x2 -> x11, starting transfers between devices: 5.84 us -> 16.2 us  [the longest x1 4.41 us: local(): lax.ppermute(hidden[tok - HALO:], 'seq', [(j, j + 1) for j in range(n_seq...]
  transfers between devices with their start and end apart: 3 -> 13, of which waited for: 2 -> 6; matrix products, arithmetic and copies ran while one was open for 3% -> 3% of each run, Pallas kernels for 0% -> 12%
where the time goes in v2:
time: 77.4 us; the launch traced here: 76.8 us
  starting transfers between devices  26.1 us (34%)
  waiting for transfers between devices  24.4 us (32%)
  Pallas kernels  14.6 us (19%)
  local copies, waits for them, and re-layouts  7.24 us (9%)
  between operations  2.88 us (4%)
  other arithmetic  1.59 us (2%)
    ppermute x1, waiting for transfers between devices, local(): firsts.append(lax.ppermute(packed[2 * o - 2], 'head', shift_x(-o)))  10 us
    all_to_all x1, waiting for transfers between devices, local(): got = lax.all_to_all(stats, 'seq', 0, 0, tiled=True)  6.61 us
    all_to_all x1, starting transfers between devices, local(): got = lax.all_to_all(stats, 'seq', 0, 0, tiled=True)  6.6 us
    unnamed x15, local copies, waits for them, and re-layouts  6.38 us
    pallas_call x1, Pallas kernels, local(): call(norm_kernel, [sds((span, CORES * feats), BF16), sds((lines, LANES),...  5.79 us
    all_to_all x1, waiting for transfers between devices, local(): everything = lax.all_to_all(spread, 'seq', 0, 0, tiled=True)  5.78 us
    ppermute x1, starting transfers between devices, local(): lax.ppermute(hidden[tok - HALO:], 'seq', [(j, j + 1) for j in range(n_seq...  4.41 us
    all_to_all x1, starting transfers between devices, local(): everything = lax.all_to_all(spread, 'seq', 0, 0, tiled=True)  3.25 us
  transfers between devices with their start and end apart: 13, of which 6 were waited for; matrix products, arithmetic and copies ran while one was open for 3% of the time, Pallas kernels for 12%

profile of v2, /device:TPU:0, one launch (start us, length us, event | category | flops | bytes accessed | tf_op | source)
XLA Modules:
  0.0 76.8 jit_solution(888863239127227674)
XLA Ops:
  1.2 0.8 %fusion.4 = (bf16[8,2048]{1,0:T(8,128)(2,1)S(1)}, bf16[8,2048]{1,0:T(8,128)(2,1)S(1)}) fusion(bf16[512,2048]{1,0:T(8,128)(2,1)} %hid.1), kind=kLoop, calls=%fused_computation.26 | loop fusion | bytes 131072 | tf_op jit(solution)/shard_map/slice | solution.py:310
  2.0 4.4 %collective-permute-start.1 = (bf16[8,2048]{1,0:T(8,128)(2,1)S(1)}, bf16[8,2048]{1,0:T(8,128)(2,1)S(1)}, u32[]{:S(2)}, u32[]{:S(2)}) collective-permute-start(bf16[8,2048]{1,0:T(8,128)(2,1)S(1)} %get-tuple-element.27), channel_id=1, source_target_pairs={{0,4},{4,8},{8,12},{12,16},{16,20},{20,24},{24,28},{1,5},{5,9},{9,... | collective-permute-start | bytes 98312 | tf_op jit(solution)/shard_map/ppermute | solution.py:309
  6.4 1.3 %collective-permute-start.2 = (bf16[8,2048]{1,0:T(8,128)(2,1)S(1)}, bf16[8,2048]{1,0:T(8,128)(2,1)S(1)}, u32[]{:S(2)}, u32[]{:S(2)}) collective-permute-start(bf16[8,2048]{1,0:T(8,128)(2,1)S(1)} %get-tuple-element.26), channel_id=1, source_target_pairs={{4,0},{8,4},{12,8},{16,12},{20,16},{24,20},{28,24},{5,1},{9,5},{13... | collective-permute-start | bytes 98312 | tf_op jit(solution)/shard_map/ppermute | solution.py:310
  7.9 1.6 %copy-done = bf16[8192,128]{1,0:T(8,128)(2,1)S(1)} copy-done((bf16[8192,128]{1,0:T(8,128)(2,1)S(1)}, bf16[8192,128]{1,0:T(8,128)(2,1)}, u32[]{:S(2)}) %copy-start) | copy-done | bytes 2097176
  9.5 1.6 %copy-done.2 = bf16[8192,128]{1,0:T(8,128)(2,1)S(1)} copy-done((bf16[8192,128]{1,0:T(8,128)(2,1)S(1)}, bf16[8192,128]{1,0:T(8,128)(2,1)}, u32[]{:S(2)}) %copy-start.2) | copy-done | bytes 2097176
  11.1 1.7 %shard_map.96 = (bf16[896,256]{1,0:T(8,128)(2,1)S(1)}, bf16[1408,256]{1,0:T(8,128)(2,1)}) custom-call(s32[4]{0:T(128)S(1)} %pad_add_fusion.3.at, bf16[8192,128]{1,0:T(8,128)(2,1)S(1)} %copy-done, bf16[8192,128]{1,0:T(8,128)(2,1)S(1)} %copy-done.2), custom_call_target="tpu_custom_call" | custom-call | flops 1048576 | bytes 1048576 | tf_op jit(solution)/shard_map/pallas_call | solution.py:296
  12.8 1.6 %collective-permute-start.4 = (bf16[896,256]{1,0:T(8,128)(2,1)S(1)}, bf16[896,256]{1,0:T(8,128)(2,1)}, u32[]{:S(2)}, u32[]{:S(2)}) collective-permute-start(bf16[896,256]{1,0:T(8,128)(2,1)S(1)} %get-tuple-element.16), channel_id=1, source_target_pairs={{0,2},{1,3},{2,0},{3,1},{4,6},{5,7},{6,4},{7,5},{8,10},{9,11},{10,... | collective-permute-start | bytes 1376264 | tf_op jit(solution)/shard_map/ppermute | solution.py:306
  15.0 1.0 %fusion = (f32[528,64]{1,0:T(8,128)S(1)}, f32[528,64]{1,0:T(8,128)S(1)}, f32[528,64]{1,0:T(8,128)S(1)}) fusion(f32[64]{0:T(128)S(1)} %multiply_power_fusion, f32[528]{0:T(1024)S(1)} %fusion.3), kind=kLoop, calls=%fused_computation.4 | loop fusion | flops 67584 | bytes 407872 | tf_op jit(solution)/shard_map/neg | solution.py:365
  16.3 10.0 %collective-permute-done.4.b0 = bf16[896,256]{1,0:T(8,128)(2,1)} collective-permute-done((bf16[896,256]{1,0:T(8,128)(2,1)S(1)}, bf16[896,256]{1,0:T(8,128)(2,1)}, u32[]{:S(2)}, u32[]{:S(2)}) %collective-permute-start.4) | collective-permute-done | bytes 458784 | tf_op jit(solution)/shard_map/ppermute | solution.py:306
  26.4 2.6 %collective-permute-start.5 = (bf16[896,256]{1,0:T(8,128)(2,1)}, bf16[896,256]{1,0:T(8,128)(2,1)S(1)}, u32[]{:S(2)}, u32[]{:S(2)}) collective-permute-start(bf16[896,256]{1,0:T(8,128)(2,1)} %collective-permute-done.4.b0), channel_id=1, source_target_pairs={{0,4},{4,0},{8,12},{12,8},{16,20},{20,16},{24,28},{28,24},{1,5},{5... | collective-permute-start | bytes 1376264 | tf_op jit(solution)/shard_map/ppermute | solution.py:315
  29.0 1.6 %collective-permute-start.6 = (bf16[896,256]{1,0:T(8,128)(2,1)}, bf16[896,256]{1,0:T(8,128)(2,1)S(1)}, u32[]{:S(2)}, u32[]{:S(2)}) collective-permute-start(bf16[896,256]{1,0:T(8,128)(2,1)} %collective-permute-done.4.b0), channel_id=1, source_target_pairs={{0,8},{4,12},{8,0},{12,4},{16,24},{20,28},{24,16},{28,20},{1,9},{5... | collective-permute-start | bytes 1376264 | tf_op jit(solution)/shard_map/ppermute | solution.py:316
  30.7 1.2 %collective-permute-done.3.swp_halo = bf16[16,2048]{1,0:T(8,128)(2,1)S(1)} collective-permute-done((bf16[16,2048]{1,0:T(8,128)(2,1)S(1)}, bf16[16,2048]{1,0:T(8,128)(2,1)S(1)}, u32[]{:S(2)}, u32[]{:S(2)}) %collective-permute-start.3) | collective-permute-done | bytes 65568 | tf_op jit(solution)/shard_map/ppermute | solution.py:312
  31.9 1.6 %copy-done.3 = bf16[8192,128]{1,0:T(8,128)(2,1)S(1)} copy-done((bf16[8192,128]{1,0:T(8,128)(2,1)S(1)}, bf16[8192,128]{1,0:T(8,128)(2,1)}, u32[]{:S(2)}) %copy-start.3) | copy-done | bytes 2097176
  33.5 1.6 %copy-done.4 = bf16[512,2048]{1,0:T(8,128)(2,1)S(1)} copy-done((bf16[512,2048]{1,0:T(8,128)(2,1)S(1)}, bf16[512,2048]{1,0:T(8,128)(2,1)}, u32[]{:S(2)}) %copy-start.4) | copy-done | bytes 2097176
  35.0 5.8 %shard_map.95 = (bf16[528,4096]{1,0:T(8,128)(2,1)S(1)}, f32[8,128]{1,0:T(8,128)S(1)}, f32[528,128]{1,0:T(8,128)S(1)}, f32[528,128]{1,0:T(8,128)S(1)}) custom-call(s32[2]{0:T(128)S(1)} %pad_add_fusion.1.at, bf16[512,2048]{1,0:T(8,128)(2,1)S(1)} %copy-done.4, bf16[512,2048]{1,0:T(8,128)(2,1)} %collective-permute-done.swp, ...), custom_call_target="tpu_custom_call" | custom-call | flops 2147483648 | bytes 1048576 | tf_op jit(solution)/shard_map/pallas_call | solution.py:323
  41.1 2.7 %shard_map.97 = (bf16[528,128]{1,0:T(8,128)(2,1)S(1)}, bf16[528,128]{1,0:T(8,128)(2,1)S(1)}) custom-call(s32[4]{0:T(128)S(1)} %pad_add_fusion.2.at, bf16[528,4096]{1,0:T(8,128)(2,1)S(1)} %get-tuple-element.15.normed, bf16[896,256]{1,0:T(8,128)(2,1)} %collective-permute-done.4.b0, bf16[896,256]{1,0:T(8,128)(2,1)S(1)} %collective-permute-done.5.b1, ...), custom_call_target="tpu_custom_call" | custom-call | flops 2147483648 | bytes 1048576 | tf_op jit(solution)/shard_map/pallas_call | solution.py:347
  43.8 1.6 %collective-permute-start.8 = (bf16[528,128]{1,0:T(8,128)(2,1)S(1)}, bf16[528,128]{1,0:T(8,128)(2,1)S(1)}, u32[]{:S(2)}, u32[]{:S(2)}) collective-permute-start(bf16[528,128]{1,0:T(8,128)(2,1)S(1)} %get-tuple-element.18), channel_id=1, source_target_pairs={{0,2},{1,3},{2,0},{3,1},{4,6},{5,7},{6,4},{7,5},{8,10},{9,11},{10,... | collective-permute-start | bytes 405512 | tf_op jit(solution)/shard_map/ppermute | solution.py:353
  47.3 1.6 %collective-permute-start.10 = (bf16[528,128]{1,0:T(8,128)(2,1)S(1)}, bf16[528,128]{1,0:T(8,128)(2,1)S(1)}, u32[]{:S(2)}, u32[]{:S(2)}) collective-permute-start(bf16[528,128]{1,0:T(8,128)(2,1)S(1)} %get-tuple-element.23), channel_id=1, source_target_pairs={{0,2},{1,3},{2,0},{3,1},{4,6},{5,7},{6,4},{7,5},{8,10},{9,11},{10,... | collective-permute-start | bytes 405512 | tf_op jit(solution)/shard_map/ppermute | solution.py:354
  49.5 1.8 %shard_map.98 = (f32[528,512]{1,0:T(8,128)S(1)}, f32[8,2,512]{2,1,0:T(2,128)}) custom-call(s32[1]{0:T(128)} %bitcast.first, f32[528,128]{1,0:T(8,128)S(1)} %get-tuple-element.14.refs_0_, bf16[528,128]{1,0:T(8,128)(2,1)S(1)} %collective-permute-done.8.refs_1_, f32[8,128]{1,0:T(8,128)S(1)} %get-tuple-element.19.refs_2_, ...), custom_call_target="tpu_custom_call" | custom-call | flops 268435456 | bytes 1048576 | tf_op jit(solution)/shard_map/pallas_call | solution.py:373
  51.3 6.6 %all-to-all-start = ((f32[8,2,512]{2,1,0:T(2,128)}), f32[8,2,512]{2,1,0:T(2,128)S(1)}, u32[]{:S(2)}, u32[]{:S(2)}) async-start(f32[8,2,512]{2,1,0:T(2,128)} %get-tuple-element.20.mine), calls=%async_computation | async-start | bytes 65536 | tf_op jit(solution)/shard_map/all_to_all | solution.py:380
  58.0 6.6 %all-to-all-done.got = f32[8,2,512]{2,1,0:T(2,128)S(1)} async-done(((f32[8,2,512]{2,1,0:T(2,128)}), f32[8,2,512]{2,1,0:T(2,128)S(1)}, u32[]{:S(2)}, u32[]{:S(2)}) %all-to-all-start) | async-done | bytes 32800 | tf_op jit(solution)/shard_map/all_to_all | solution.py:380
  64.6 1.8 %shard_map.99 = (f32[1,4]{1,0:T(1,128)}, f32[8,128]{1,0:T(8,128)}) custom-call(s32[2]{0:T(128)S(1)} %pad_add_fusion.sizes, f32[8,2,512]{2,1,0:T(2,128)S(1)} %all-to-all-done.got, f32[8,2,512]{2,1,0:T(2,128)} %get-tuple-element.20.mine, f32[528,512]{1,0:T(8,128)S(1)} %get-tuple-element.21.expo, f32[528,128]{1,0:T(8,128)S(1)} %get-tuple-element.22.refs_0_, ...), custom_call_target="tpu_custom_call" | custom-call | flops 67108864 | bytes 1048576 | tf_op jit(solution)/shard_map/pallas_call | solution.py:382
  66.4 3.2 %all-to-all-start.1 = ((f32[8,1,128]{2,1,0:T(1,128)}), f32[8,1,128]{2,1,0:T(1,128)S(1)}, u32[]{:S(2)}, u32[]{:S(2)}) async-start(f32[8,1,128]{2,1,0:T(1,128)} %bitcast.14), calls=%async_computation.1 | async-start | bytes 8192 | tf_op jit(solution)/shard_map/all_to_all | solution.py:391
  70.3 5.8 %all-to-all-done.1 = f32[8,1,128]{2,1,0:T(1,128)S(1)} async-done(((f32[8,1,128]{2,1,0:T(1,128)}), f32[8,1,128]{2,1,0:T(1,128)S(1)}, u32[]{:S(2)}, u32[]{:S(2)}) %all-to-all-start.1) | async-done | bytes 4128 | tf_op jit(solution)/shard_map/all_to_all | solution.py:391
  (38 shorter events, 3.9 us)
Async XLA Ops:
  0.6 31.2 %collective-permute-start = (bf16[512,2048]{1,0:T(8,128)(2,1)}, bf16[512,2048]{1,0:T(8,128)(2,1)}, u32[]{:S(2)}, u32[]{:S(2)}) collective-permute-start(bf16[512,2048]{1,0:T(8,128)(2,1)} %hid.1), channel_id=1, source_target_pairs={{0,1},{1,0},{2,3},{3,2},{4,5},{5,4},{6,7},{7,6},{8,9},{9,8},{10,11... | collective-permute-start | bytes 6291464 | tf_op jit(solution)/shard_map/ppermute | solution.py:308
  2.0 14.4 %collective-permute-start.1 = (bf16[8,2048]{1,0:T(8,128)(2,1)S(1)}, bf16[8,2048]{1,0:T(8,128)(2,1)S(1)}, u32[]{:S(2)}, u32[]{:S(2)}) collective-permute-start(bf16[8,2048]{1,0:T(8,128)(2,1)S(1)} %get-tuple-element.27), channel_id=1, source_target_pairs={{0,4},{4,8},{8,12},{12,16},{16,20},{20,24},{24,28},{1,5},{5,9},{9,... | collective-permute-start | bytes 98312 | tf_op jit(solution)/shard_map/ppermute | solution.py:309
  6.4 24.2 %collective-permute-start.2 = (bf16[8,2048]{1,0:T(8,128)(2,1)S(1)}, bf16[8,2048]{1,0:T(8,128)(2,1)S(1)}, u32[]{:S(2)}, u32[]{:S(2)}) collective-permute-start(bf16[8,2048]{1,0:T(8,128)(2,1)S(1)} %get-tuple-element.26), channel_id=1, source_target_pairs={{4,0},{8,4},{12,8},{16,12},{20,16},{24,20},{28,24},{5,1},{9,5},{13... | collective-permute-start | bytes 98312 | tf_op jit(solution)/shard_map/ppermute | solution.py:310
  7.9 1.6 %copy-start = (bf16[8192,128]{1,0:T(8,128)(2,1)S(1)}, bf16[8192,128]{1,0:T(8,128)(2,1)}, u32[]{:S(2)}) copy-start(bf16[8192,128]{1,0:T(8,128)(2,1)} %km.3) | copy-start | bytes 6291460
  9.5 1.6 %copy-start.2 = (bf16[8192,128]{1,0:T(8,128)(2,1)S(1)}, bf16[8192,128]{1,0:T(8,128)(2,1)}, u32[]{:S(2)}) copy-start(bf16[8192,128]{1,0:T(8,128)(2,1)} %vm.3) | copy-start | bytes 6291460
  11.1 3.8 %copy-start.6 = (f32[8192]{0:T(1024)S(1)}, f32[8192]{0:T(1024)}, u32[]{:S(2)}) copy-start(f32[8192]{0:T(1024)} %param.9) | copy-start | bytes 98308
  12.8 19.1 %copy-start.1 = (bf16[8192,128]{1,0:T(8,128)(2,1)S(1)}, bf16[8192,128]{1,0:T(8,128)(2,1)}, u32[]{:S(2)}) copy-start(bf16[8192,128]{1,0:T(8,128)(2,1)} %km.3) | copy-start | bytes 6291460
  12.8 13.6 %collective-permute-start.4 = (bf16[896,256]{1,0:T(8,128)(2,1)S(1)}, bf16[896,256]{1,0:T(8,128)(2,1)}, u32[]{:S(2)}, u32[]{:S(2)}) collective-permute-start(bf16[896,256]{1,0:T(8,128)(2,1)S(1)} %get-tuple-element.16), channel_id=1, source_target_pairs={{0,2},{1,3},{2,0},{3,1},{4,6},{5,7},{6,4},{7,5},{8,10},{9,11},{10,... | collective-permute-start | bytes 1376264 | tf_op jit(solution)/shard_map/ppermute | solution.py:306
  14.4 26.7 %collective-permute-start.7 = (bf16[1408,256]{1,0:T(8,128)(2,1)}, bf16[1408,256]{1,0:T(8,128)(2,1)}, u32[]{:S(2)}, u32[]{:S(2)}) collective-permute-start(bf16[1408,256]{1,0:T(8,128)(2,1)} %get-tuple-element.17), channel_id=1, source_target_pairs={{0,2},{1,3},{2,0},{3,1},{4,6},{5,7},{6,4},{7,5},{8,10},{9,11},{10,... | collective-permute-start | bytes 2162696 | tf_op jit(solution)/shard_map/ppermute | solution.py:307
  26.4 14.7 %collective-permute-start.5 = (bf16[896,256]{1,0:T(8,128)(2,1)}, bf16[896,256]{1,0:T(8,128)(2,1)S(1)}, u32[]{:S(2)}, u32[]{:S(2)}) collective-permute-start(bf16[896,256]{1,0:T(8,128)(2,1)} %collective-permute-done.4.b0), channel_id=1, source_target_pairs={{0,4},{4,0},{8,12},{12,8},{16,20},{20,16},{24,28},{28,24},{1,5},{5... | collective-permute-start | bytes 1376264 | tf_op jit(solution)/shard_map/ppermute | solution.py:315
  29.0 12.1 %collective-permute-start.6 = (bf16[896,256]{1,0:T(8,128)(2,1)}, bf16[896,256]{1,0:T(8,128)(2,1)S(1)}, u32[]{:S(2)}, u32[]{:S(2)}) collective-permute-start(bf16[896,256]{1,0:T(8,128)(2,1)} %collective-permute-done.4.b0), channel_id=1, source_target_pairs={{0,8},{4,12},{8,0},{12,4},{16,24},{20,28},{24,16},{28,20},{1,9},{5... | collective-permute-start | bytes 1376264 | tf_op jit(solution)/shard_map/ppermute | solution.py:316
  30.6 1.3 %collective-permute-start.3 = (bf16[16,2048]{1,0:T(8,128)(2,1)S(1)}, bf16[16,2048]{1,0:T(8,128)(2,1)S(1)}, u32[]{:S(2)}, u32[]{:S(2)}) collective-permute-start(bf16[16,2048]{1,0:T(8,128)(2,1)S(1)} %constant_dynamic-update-slice_fusion.halo), channel_id=1, source_target_pairs={{0,1},{1,0},{2,3},{3,2},{4,5},{5,4},{6,7},{7,6},{8,9},{9,8},{10,11... | collective-permute-start | bytes 196616 | tf_op jit(solution)/shard_map/ppermute | solution.py:312
  31.9 1.6 %copy-start.3 = (bf16[8192,128]{1,0:T(8,128)(2,1)S(1)}, bf16[8192,128]{1,0:T(8,128)(2,1)}, u32[]{:S(2)}) copy-start(bf16[8192,128]{1,0:T(8,128)(2,1)} %vm.3) | copy-start | bytes 6291460
  33.5 1.6 %copy-start.4 = (bf16[512,2048]{1,0:T(8,128)(2,1)S(1)}, bf16[512,2048]{1,0:T(8,128)(2,1)}, u32[]{:S(2)}) copy-start(bf16[512,2048]{1,0:T(8,128)(2,1)} %hid.1) | copy-start | bytes 6291460
  41.1 6.2 %copy-start.5 = (bf16[64,1024]{1,0:T(8,128)(2,1)S(1)}, bf16[64,1024]{1,0:T(8,128)(2,1)}, u32[]{:S(2)}) copy-start(bf16[64,1024]{1,0:T(8,128)(2,1)} %param.12) | copy-start | bytes 393220
  43.8 5.7 %collective-permute-start.8 = (bf16[528,128]{1,0:T(8,128)(2,1)S(1)}, bf16[528,128]{1,0:T(8,128)(2,1)S(1)}, u32[]{:S(2)}, u32[]{:S(2)}) collective-permute-start(bf16[528,128]{1,0:T(8,128)(2,1)S(1)} %get-tuple-element.18), channel_id=1, source_target_pairs={{0,2},{1,3},{2,0},{3,1},{4,6},{5,7},{6,4},{7,5},{8,10},{9,11},{10,... | collective-permute-start | bytes 405512 | tf_op jit(solution)/shard_map/ppermute | solution.py:353
  45.4 4.1 %collective-permute-start.9 = (f32[8,128]{1,0:T(8,128)S(1)}, f32[8,128]{1,0:T(8,128)S(1)}, u32[]{:S(2)}, u32[]{:S(2)}) collective-permute-start(f32[8,128]{1,0:T(8,128)S(1)} %get-tuple-element.19.refs_2_), channel_id=1, source_target_pairs={{0,2},{1,3},{2,0},{3,1},{4,6},{5,7},{6,4},{7,5},{8,10},{9,11},{10,... | collective-permute-start | bytes 12296 | tf_op jit(solution)/shard_map/ppermute | solution.py:342
  47.3 10.7 %collective-permute-start.10 = (bf16[528,128]{1,0:T(8,128)(2,1)S(1)}, bf16[528,128]{1,0:T(8,128)(2,1)S(1)}, u32[]{:S(2)}, u32[]{:S(2)}) collective-permute-start(bf16[528,128]{1,0:T(8,128)(2,1)S(1)} %get-tuple-element.23), channel_id=1, source_target_pairs={{0,2},{1,3},{2,0},{3,1},{4,6},{5,7},{6,4},{7,5},{8,10},{9,11},{10,... | collective-permute-start | bytes 405512 | tf_op jit(solution)/shard_map/ppermute | solution.py:354
  51.3 13.3 %all-to-all-start = ((f32[8,2,512]{2,1,0:T(2,128)}), f32[8,2,512]{2,1,0:T(2,128)S(1)}, u32[]{:S(2)}, u32[]{:S(2)}) async-start(f32[8,2,512]{2,1,0:T(2,128)} %get-tuple-element.20.mine), calls=%async_computation | async-start | bytes 65536 | tf_op jit(solution)/shard_map/all_to_all | solution.py:380
  66.4 9.7 %all-to-all-start.1 = ((f32[8,1,128]{2,1,0:T(1,128)}), f32[8,1,128]{2,1,0:T(1,128)S(1)}, u32[]{:S(2)}, u32[]{:S(2)}) async-start(f32[8,1,128]{2,1,0:T(1,128)} %bitcast.14), calls=%async_computation.1 | async-start | bytes 8192 | tf_op jit(solution)/shard_map/all_to_all | solution.py:391

commit v3 on v0

v3 whole, which is shorter than its diff:
```python
import functools

import jax
import jax.numpy as jnp
from jax import lax
from jax.experimental import pallas as pl
from jax.experimental.pallas import tpu as pltpu
from jax.sharding import PartitionSpec as P

BLK = 128
LANES = 128
KERNEL_LIMIT = 15
REACH = (KERNEL_LIMIT - 1) // 2
EDGE = 16
CORES = 2
GROUP = 4
MASKED = -1e30

VMEM = pl.BlockSpec(memory_space=pltpu.VMEM)
SMEM = pl.BlockSpec(memory_space=pltpu.SMEM)
HBM = pl.BlockSpec(memory_space=pltpu.HBM)
F32, BF16 = jnp.float32, jnp.bfloat16


def sds(shape, dtype):
    return jax.ShapeDtypeStruct(shape, dtype)


def call(body, out, ins, scratch=(), outs=None, flops=1 << 20, limit=40 << 20):
    return pl.pallas_call(
        body,
        out_shape=out,
        in_specs=ins,
        out_specs=outs if outs is not None else jax.tree.map(lambda _: VMEM, out),
        scratch_shapes=list(scratch),
        cost_estimate=pl.CostEstimate(flops=flops, bytes_accessed=1 << 20, transcendentals=0),
        compiler_params=pltpu.CompilerParams(vmem_limit_bytes=limit),
    )


def iota(shape, dim):
    return lax.broadcasted_iota(jnp.int32, shape, dim)


def to_lanes(col):
    n = col.shape[0]
    here = iota((n, LANES), 0) == iota((n, LANES), 1)
    return jnp.sum(jnp.where(here, jnp.broadcast_to(col, (n, LANES)), 0.0), axis=0, keepdims=True)


def to_rows(row, n):
    here = iota((n, LANES), 0) == iota((n, LANES), 1)
    return jnp.sum(jnp.where(here, jnp.broadcast_to(row, (n, LANES)), 0.0), axis=1, keepdims=True)


def pack_kernel(chunks, at, km, vm, out, sem):
    head = km.shape[1]
    copies = []
    for which, (to, count) in enumerate(chunks):
        start = pl.multiple_of(at[which], LANES)
        for side, src in enumerate((km, vm)):
            copies.append(
                pltpu.make_async_copy(
                    src.at[pl.ds(start, count)],
                    out.at[pl.ds(to, count), pl.ds(side * head, head)],
                    sem.at[2 * which + side],
                )
            )
    for c in copies:
        c.start()
    for c in copies:
        c.wait()


def norm_kernel(at, hid, gain, weights, *refs):
    more = refs[:-3]
    normed, sumsq, acc = refs[-3:]
    tok, feats = hid.shape
    line = at[0] // LANES
    nb = tok // LANES
    sumsq[...] = more[0][...] if more else jnp.zeros_like(sumsq)
    for b in range(nb):
        rows = pl.ds(b * LANES, LANES)
        folded = None
        for t in range(feats // LANES):
            lanes = pl.ds(t * LANES, LANES)
            raw = hid[rows, lanes].astype(F32)
            folded = raw * raw if folded is None else folded + raw * raw
            normed[rows, lanes] = (raw * gain[pl.ds(line + t, 1), :]).astype(BF16)
        sumsq[b : b + 1, :] += to_lanes(jnp.sum(folded, axis=1, keepdims=True))
    out = jnp.dot(normed[...], weights[...], preferred_element_type=F32)
    acc[...] = out + more[1][...] if more else out


def part_of(q, at, mine, other, blk):
    a = mine[:, pl.ds(pl.multiple_of(at * q[0], LANES), q[0])]
    b = other[:, pl.ds(pl.multiple_of(at * q[1], LANES), q[1])]
    return jnp.dot(a, blk[: q[0], :], preferred_element_type=F32) + jnp.dot(
        b, blk[q[0] : q[0] + q[1], :], preferred_element_type=F32
    )


def early_kernel(q, at, mine, other, b0, out):
    out[...] = part_of(q, at[0], mine, other, b0)


def late_kernel(q, at, mine, other, early, b1, b2, b3, out_k, out_v):
    head = out_k.shape[1]
    total = early[...]
    for k, blk in enumerate((b1, b2, b3)):
        total = total + part_of(q, at[k + 1], mine, other, blk)
    total = total + jnp.dot(
        other[:, GROUP * q[1] :], b3[q[0] + q[1] :, :], preferred_element_type=F32
    )
    out_k[...] = total[:, :head].astype(BF16)
    out_v[...] = total[:, head:].astype(BF16)


def row_scale(sqs, tok, full_width):
    sumsq = sqs[0][...]
    for sq in sqs[1:]:
        sumsq = sumsq + sq[...]
    inv = lax.rsqrt(sumsq / full_width + 1e-05)
    return [to_rows(inv[b : b + 1, :], LANES) for b in range(tok // LANES)]


def score_kernel(full_width, scale_by, first, *refs):
    n_off = (len(refs) - 9) // 2
    acc, parts, sqs = refs[0], refs[1 : 1 + n_off], refs[1 + n_off : 2 + 2 * n_off]
    cos, sin, q, limit, expo, stats, keys = refs[2 + 2 * n_off :]
    tok, head = keys.shape
    for b, col in enumerate(row_scale(sqs, tok, full_width)):
        rows = pl.ds(b * LANES, LANES)
        k = acc[rows, :head]
        for p in parts:
            k = k + p[rows, :].astype(F32)
        k = k * col
        keys[rows, :] = (k * cos[rows, :] + pltpu.roll(k, head // 2, 1) * sin[rows, :]).astype(BF16)
    scores = lax.dot_general(
        keys[...], q[...], (((1,), (1,)), ((), ())), preferred_element_type=F32
    ) * scale_by
    token = first[0] + iota((tok, 1), 0)
    scores = jnp.where(token <= limit[...], scores, MASKED)
    top = jnp.max(scores, axis=0, keepdims=True)
    e = jnp.exp(scores - top)
    expo[...] = e
    own = jnp.sum(e, axis=0, keepdims=True)
    for d in range(stats.shape[0]):
        stats[d, 0:1, :] = top
        stats[d, 1:2, :] = own


def widen(column, below, above, lane, halfspan):
    pooled = column
    for shift in range(1, REACH + 1):
        right = pltpu.roll(jnp.where(lane < shift, below, column), LANES - shift, 1)
        left = pltpu.roll(jnp.where(lane >= LANES - shift, above, column), shift, 1)
        pooled = jnp.where(
            shift <= halfspan, jnp.maximum(jnp.maximum(pooled, right), left), pooled
        )
    return pooled


def pool_kernel(full_width, window, sizes, got, mine, expo, *refs):
    n_off = (len(refs) - 4) // 2
    acc, parts, sqs = refs[0], refs[1 : 1 + n_off], refs[1 + n_off : 2 + 2 * n_off]
    win, spread = refs[2 + 2 * n_off :]
    tok = expo.shape[0]
    head = acc.shape[1] // 2
    nb = tok // LANES
    row_top = got[0, 0:1, :]
    for d in range(1, got.shape[0]):
        row_top = jnp.maximum(row_top, got[d, 0:1, :])
    row_total = jnp.zeros_like(row_top)
    for d in range(got.shape[0]):
        row_total = row_total + got[d, 1:2, :] * jnp.exp(got[d, 0:1, :] - row_top)
    weight = jnp.exp(mine[0, 0:1, :] - row_top) / row_total
    weight = jnp.where(win[...] >= window - sizes[0], weight, 0.0)
    height = -(-nb // 8) * 8
    line = iota((height, LANES), 0)
    lane = iota((height, LANES), 1)
    column = jnp.zeros((height, LANES), F32)
    for b, col in enumerate(row_scale(sqs, tok, full_width)):
        rows = pl.ds(b * LANES, LANES)
        v = acc[rows, head:]
        for p in parts:
            v = v + p[rows, :].astype(F32)
        vmag = jnp.sum(jnp.abs(v), axis=1, keepdims=True) * (1.0 / head) * col
        mass = jnp.sum(expo[rows, :] * weight, axis=1, keepdims=True)
        here = jnp.broadcast_to(to_lanes(mass * vmag), (height, LANES))
        column = jnp.where(line == b, here, column)
    below, above = pltpu.roll(column, height - 1, 0), pltpu.roll(column, 1, 0)
    halfspan = lax.shift_right_arithmetic(sizes[1] - 1, 1)
    pooled = widen(column, below, above, lane, halfspan)
    place = line * LANES + lane
    inner = (place >= REACH) & (place < tok - REACH)
    sums = to_lanes(jnp.sum(jnp.where(inner, pooled, 0.0), axis=1, keepdims=True))
    flat = lane[0:1, :]
    last = pltpu.roll(column[nb - 1 : nb, :], 2 * EDGE, 1)
    said = jnp.where(flat < EDGE, column[0:1, :], jnp.where(flat < 2 * EDGE, last, pltpu.roll(sums, 2 * EDGE, 1)))
    spread[...] = jnp.broadcast_to(said, spread.shape)


def rank_kernel(nb, sizes, said, blocks, share):
    v = said[...]
    n = v.shape[0]
    line, lane = iota(v.shape, 0), iota(v.shape, 1)
    following = pltpu.roll(v, n - 1, 0)
    seam = jnp.where(lane < EDGE, pltpu.roll(v, LANES - EDGE, 1), pltpu.roll(following, EDGE, 1))
    seam = jnp.where(lane < 2 * EDGE, seam, 0.0)
    end = line == n - 1
    zero = jnp.zeros_like(seam)
    halfspan = lax.shift_right_arithmetic(sizes[1] - 1, 1)
    tail = widen(jnp.where(end & (lane >= EDGE), 0.0, seam), zero, zero, lane, halfspan)
    lead = widen(jnp.where(end & (lane < EDGE), 0.0, seam), zero, zero, lane, halfspan)
    tail = jnp.sum(jnp.where((lane >= EDGE - REACH) & (lane < EDGE), tail, 0.0), axis=1, keepdims=True)
    lead = jnp.sum(jnp.where((lane >= EDGE) & (lane < EDGE + REACH), lead, 0.0), axis=1, keepdims=True)
    lead = pltpu.roll(jnp.broadcast_to(lead, v.shape), 1, 0)
    b = pltpu.roll(v, LANES - 2 * EDGE, 1)
    b = b + jnp.where(lane == 0, lead, 0.0) + jnp.where(lane == nb - 1, tail, 0.0)
    b = jnp.where(lane < nb, b, 0.0)
    own = jnp.sum(jnp.where(line == sizes[2], b, 0.0), axis=0, keepdims=True)
    blocks[...] = own[:, :nb]
    place = line * nb + lane
    rank = jnp.zeros(v.shape, jnp.int32)

    def turned(t, k):
        return jnp.where(lane >= k, pltpu.roll(t, k, 1), pltpu.roll(t, LANES + k - nb, 1)) if k else t

    for k in range(nb):
        bk, pk = turned(b, k), turned(place, k)
        for m in range(n):
            bm, pm = (pltpu.roll(bk, m, 0), pltpu.roll(pk, m, 0)) if m else (bk, pk)
            rank = rank + jnp.where((bm > b) | ((bm == b) & (pm < place)), 1, 0)

    def add(t):
        return jnp.sum(jnp.sum(t, axis=1, keepdims=True), axis=0, keepdims=True)

    kept = jnp.where((lane < nb) & (rank < sizes[0]), b, 0.0)
    share[...] = add(kept) / add(b)


def local(
    hidden, gain, key_matrix, value_matrix, queries, window_len, kernel_width, kept_block_count
):
    tok, feats = hidden.shape
    full_width = gain.shape[0]
    head = key_matrix.shape[1]
    n_seq, n_head = lax.axis_size("seq"), lax.axis_size("head")
    n_x = n_head // CORES
    s, h = lax.axis_index("seq"), lax.axis_index("head")
    x, c = h // CORES, h % CORES
    i = s % GROUP
    q = (feats // GROUP, feats // GROUP - LANES)
    spare = feats - GROUP * q[1]
    total_tokens = tok * n_seq
    offsets = range(1, n_x)

    def shift_x(offset):
        return [
            (a * CORES + b, (a + offset) % n_x * CORES + b) for a in range(n_x) for b in range(CORES)
        ]

    def flip(bit):
        return [(j, j ^ bit) for j in range(n_seq)]

    def pack(starts, counts):
        to = [sum(counts[:k]) for k in range(len(counts))]
        return call(
            functools.partial(pack_kernel, tuple(zip(to, counts))),
            sds((sum(counts), 2 * head), BF16),
            [SMEM, HBM, HBM],
            scratch=[pltpu.SemaphoreType.DMA((2 * len(counts),))],
            limit=62 << 20,
        )(jnp.stack(starts), key_matrix, value_matrix)

    firsts, seconds = [], []
    for o in offsets:
        chip = (x - o) % n_x
        at0, at1 = (chip * CORES + c) * feats, (chip * CORES + 1 - c) * feats
        first = pack([at0 + i * q[0], at1 + i * q[1]], [q[0], q[1]])
        firsts.append(lax.ppermute(first, "head", shift_x(-o)))
        second = pack(
            [at0 + (3 - i) * q[0], at1 + (3 - i) * q[1], at1 + GROUP * q[1]], [q[0], q[1], spare]
        )
        seconds.append(lax.ppermute(second, "head", shift_x(-o)))
    swapped = lax.ppermute(hidden, "head", [(j, j ^ 1) for j in range(n_head)])
    trades = [[lax.ppermute(firsts[o - 1], "seq", flip(bit)) for bit in (1, 2)] for o in offsets]

    lines = -(-(tok // LANES) // 8) * 8
    gain_lines = gain.reshape(full_width // LANES, LANES)

    def norm(start, rows, more):
        weights = pack([start], [feats])
        return call(
            norm_kernel,
            [sds((tok, feats), BF16), sds((lines, LANES), F32), sds((tok, 2 * head), F32)],
            [SMEM] + [VMEM] * (3 + len(more)),
            flops=1 << 30,
        )(start.reshape(1), rows, gain_lines, weights, *more)

    mine, sumsq, acc = norm(h * feats, hidden, ())
    other, sumsq, acc = norm((h ^ 1) * feats, swapped, (sumsq, acc))
    sqs = [sumsq] + [lax.ppermute(sumsq, "head", shift_x(o)) for o in offsets]

    parts_k, parts_v = [], []
    slabs = jnp.stack([i ^ k for k in range(GROUP)])
    for o in offsets:
        early = call(
            functools.partial(early_kernel, q),
            sds((tok, 2 * head), F32),
            [SMEM] + [VMEM] * 3,
            flops=1 << 29,
        )(slabs, mine, other, firsts[o - 1])
        part_k, part_v = call(
            functools.partial(late_kernel, q),
            [sds((tok, head), BF16), sds((tok, head), BF16)],
            [SMEM] + [VMEM] * 6,
            flops=1 << 30,
        )(slabs, mine, other, early, *trades[o - 1], seconds[o - 1])
        parts_k.append(lax.ppermute(part_k, "head", shift_x(o)))
        parts_v.append(lax.ppermute(part_v, "head", shift_x(o)))

    half = head // 2
    freq = 500000.0 ** (-(jnp.arange(half).astype(F32) * 2.0) / head)
    token = s * tok + jnp.arange(tok)
    angle = token.astype(F32)[:, None] * freq[None, :]
    cos, sin = jnp.cos(angle), jnp.sin(angle)
    cos = jnp.concatenate([cos, cos], axis=1)
    sin = jnp.concatenate([-sin, sin], axis=1)

    window = queries.shape[0]
    group_heads = queries.shape[1] // head
    rows = window * group_heads
    query_rows = queries.reshape(rows, head)
    row_window = (jnp.arange(rows) // group_heads).astype(jnp.int32)[None, :]
    limit = total_tokens - window + row_window
    expo, stats = call(
        functools.partial(score_kernel, full_width, head ** (-0.5)),
        [sds((tok, rows), F32), sds((n_seq, 2, rows), F32)],
        [SMEM] + [VMEM] * (6 + 2 * len(offsets)),
        scratch=[pltpu.VMEM((tok, head), BF16)],
        flops=1 << 28,
    )((s * tok).reshape(1), acc, *parts_k, *sqs, cos, sin, query_rows, limit)
    got = lax.all_to_all(stats, "seq", 0, 0, tiled=True)
    nb = tok // BLK
    spread = call(
        functools.partial(pool_kernel, full_width, window),
        sds((n_seq, LANES), F32),
        [SMEM] + [VMEM] * (6 + 2 * len(offsets)),
        flops=1 << 26,
    )(
        jnp.concatenate([window_len, kernel_width]),
        got, stats, expo, acc, *parts_v, *sqs, row_window,
    )
    said = lax.all_to_all(spread, "seq", 0, 0, tiled=True)
    local_blocks, fraction = call(
        functools.partial(rank_kernel, nb),
        [sds((1, nb), F32), sds((1, 1), F32)],
        [SMEM, VMEM],
        flops=1 << 20,
    )(jnp.concatenate([kept_block_count, kernel_width, s.reshape(1)]), said)
    return (local_blocks, fraction.reshape(1))


def solution(mesh):
    return jax.shard_map(
        local,
        mesh=mesh,
        in_specs=(
            P("seq", "head"),
            P(),
            P(None, "head"),
            P(None, "head"),
            P(None, "head"),
            P("head"),
            P("head"),
            P("head"),
        ),
        out_specs=(P("head", "seq"), P("head")),
        check_vma=False,
    )
```

time: 157 us -> 69.4 us (0.44)
  blocking collectives: 66.9 us -> 0 us
  waiting for transfers between devices: 48.9 us -> 19.1 us
  Pallas kernels: 0 us -> 21.4 us
  between operations: 19.3 us -> 2.74 us
  starting transfers between devices: 5.88 us -> 20 us
  matrix products: 7.68 us -> 0 us
  other arithmetic: 5.53 us -> 2.73 us
    all_gather x1 -> x0, waiting for transfers between devices: 46.9 us -> none  [local(): lax.all_gather(hidden, 'head', axis=1, tiled=True).astype(jnp.float32)]
    psum x2 -> x0, blocking collectives: 25.5 us -> none  [the longest x1 17.1 us: local(): row_total = lax.psum(jnp.sum(expo, axis=1), 'seq')]
    pmax x1 -> x0, blocking collectives: 21.4 us -> none  [local(): row_top = lax.pmax(local_top, 'seq')]
    pallas_call x0 -> x11, Pallas kernels: none -> 21.4 us  [the longest x4 9.71 us: pack(): call(functools.partial(pack_kernel, tuple(zip(to, counts))), sds((sum(cou...]
    unnamed x1 -> x0, blocking collectives: 20 us -> none
    all_to_all x0 -> x2, waiting for transfers between devices: none -> 13 us  [the longest x1 6.61 us: local(): got = lax.all_to_all(stats, 'seq', 0, 0, tiled=True)]
    all_to_all x0 -> x2, starting transfers between devices: none -> 9.15 us  [the longest x1 5.82 us: local(): got = lax.all_to_all(stats, 'seq', 0, 0, tiled=True)]
    dot_general x3 -> x0, matrix products: 7.68 us -> none  [the longest x1 6.35 us: local(): projected = jnp.dot(normed, joined, preferred_element_type=jnp.float32)]
  transfers between devices with their start and end apart: 3 -> 10, of which waited for: 2 -> 3; matrix products, arithmetic and copies ran while one was open for 3% -> 4% of each run, Pallas kernels for 0% -> 24%
where the time goes in v3:
time: 69.4 us; the launch traced here: 68.8 us
  Pallas kernels  21.4 us (31%)
  starting transfers between devices  20 us (29%)
  waiting for transfers between devices  19.1 us (28%)
  local copies, waits for them, and re-layouts  2.89 us (4%)
  between operations  2.74 us (4%)
  other arithmetic  2.73 us (4%)
    pallas_call x4, Pallas kernels, pack(): call(functools.partial(pack_kernel, tuple(zip(to, counts))), sds((sum(cou...  9.71 us
    all_to_all x1, waiting for transfers between devices, local(): got = lax.all_to_all(stats, 'seq', 0, 0, tiled=True)  6.61 us
    all_to_all x1, waiting for transfers between devices, local(): said = lax.all_to_all(spread, 'seq', 0, 0, tiled=True)  6.35 us
    ppermute x1, waiting for transfers between devices, local(): seconds.append(lax.ppermute(second, 'head', shift_x(-o)))  6.12 us
    all_to_all x1, starting transfers between devices, local(): got = lax.all_to_all(stats, 'seq', 0, 0, tiled=True)  5.82 us
    pallas_call x2, Pallas kernels, norm(): call(norm_kernel, [sds((tok, feats), BF16), sds((lines, LANES), F32), sds...  3.9 us
    ppermute x2, starting transfers between devices, local(): lax.ppermute(firsts[o - 1], 'seq', flip(bit))  3.67 us
    all_to_all x1, starting transfers between devices, local(): said = lax.all_to_all(spread, 'seq', 0, 0, tiled=True)  3.33 us
  transfers between devices with their start and end apart: 10, of which 3 were waited for; matrix products, arithmetic and copies ran while one was open for 4% of the time, Pallas kernels for 24%

profile of v3, /device:TPU:0, one launch (start us, length us, event | category | flops | bytes accessed | tf_op | source)
XLA Modules:
  0.0 68.8 jit_solution(13257571141114076271)
XLA Ops:
  1.8 2.5 %shard_map.99 = bf16[896,256]{1,0:T(8,128)(2,1)} custom-call(s32[2]{0:T(128)} %pad_add_fusion.3.at, bf16[8192,128]{1,0:T(8,128)(2,1)} %km.7, bf16[8192,128]{1,0:T(8,128)(2,1)} %vm.7), custom_call_target="tpu_custom_call" | custom-call | flops 1048576 | bytes 1048576 | tf_op jit(solution)/shard_map/pallas_call | solution.py:269
  4.4 2.6 %collective-permute-start.1 = (bf16[896,256]{1,0:T(8,128)(2,1)}, bf16[896,256]{1,0:T(8,128)(2,1)S(1)}, u32[]{:S(2)}, u32[]{:S(2)}) collective-permute-start(bf16[896,256]{1,0:T(8,128)(2,1)} %shard_map.99), channel_id=1, source_target_pairs={{0,2},{1,3},{2,0},{3,1},{4,6},{5,7},{6,4},{7,5},{8,10},{9,11},{10,... | collective-permute-start | bytes 1376264 | tf_op jit(solution)/shard_map/ppermute | solution.py:282
  7.6 2.8 %shard_map.101 = bf16[1408,256]{1,0:T(8,128)(2,1)} custom-call(s32[3]{0:T(128)} %pad_add_fusion.4.at, bf16[8192,128]{1,0:T(8,128)(2,1)} %km.7, bf16[8192,128]{1,0:T(8,128)(2,1)} %vm.7), custom_call_target="tpu_custom_call" | custom-call | flops 1048576 | bytes 1048576 | tf_op jit(solution)/shard_map/pallas_call | solution.py:269
  10.5 2.2 %shard_map.95.weights = bf16[2048,256]{1,0:T(8,128)(2,1)} custom-call(s32[1]{0:T(128)} %bitcast.2.at, bf16[8192,128]{1,0:T(8,128)(2,1)} %km.7, bf16[8192,128]{1,0:T(8,128)(2,1)} %vm.7), custom_call_target="tpu_custom_call" | custom-call | flops 1048576 | bytes 1048576 | tf_op jit(solution)/shard_map/pallas_call | solution.py:269
  12.7 2.2 %shard_map.96.weights = bf16[2048,256]{1,0:T(8,128)(2,1)} custom-call(s32[1]{0:T(128)} %bitcast.4.at, bf16[8192,128]{1,0:T(8,128)(2,1)} %km.7, bf16[8192,128]{1,0:T(8,128)(2,1)} %vm.7), custom_call_target="tpu_custom_call" | custom-call | flops 1048576 | bytes 1048576 | tf_op jit(solution)/shard_map/pallas_call | solution.py:269
  15.0 1.2 %copy-done.1 = bf16[2048,256]{1,0:T(8,128)(2,1)S(1)} copy-done((bf16[2048,256]{1,0:T(8,128)(2,1)S(1)}, bf16[2048,256]{1,0:T(8,128)(2,1)}, u32[]{:S(2)}) %copy-start.1) | copy-done | bytes 1048600
  16.2 1.6 %copy-done.2 = bf16[512,2048]{1,0:T(8,128)(2,1)S(1)} copy-done((bf16[512,2048]{1,0:T(8,128)(2,1)S(1)}, bf16[512,2048]{1,0:T(8,128)(2,1)}, u32[]{:S(2)}) %copy-start.2) | copy-done | bytes 2097176
  17.8 1.1 %shard_map.97 = (bf16[512,2048]{1,0:T(8,128)(2,1)S(1)}, f32[8,128]{1,0:T(8,128)S(1)}, f32[512,256]{1,0:T(8,128)S(1)}) custom-call(s32[1]{0:T(128)} %bitcast.4.at, bf16[512,2048]{1,0:T(8,128)(2,1)S(1)} %copy-done.2, f32[64,128]{1,0:T(8,128)S(1)} %bitcast.20, bf16[2048,256]{1,0:T(8,128)(2,1)S(1)} %copy-done.1), custom_call_target="tpu_custom_call" | custom-call | flops 1073741824 | bytes 1048576 | tf_op jit(solution)/shard_map/pallas_call | solution.py:295
  19.0 2.1 %collective-permute-start.2 = (bf16[896,256]{1,0:T(8,128)(2,1)S(1)}, bf16[896,256]{1,0:T(8,128)(2,1)S(1)}, u32[]{:S(2)}, u32[]{:S(2)}) collective-permute-start(bf16[896,256]{1,0:T(8,128)(2,1)S(1)} %collective-permute-done.1.b0), channel_id=1, source_target_pairs={{0,4},{4,0},{8,12},{12,8},{16,20},{20,16},{24,28},{28,24},{1,5},{5... | collective-permute-start | bytes 1376264 | tf_op jit(solution)/shard_map/ppermute | solution.py:288
  21.1 1.6 %collective-permute-start.3 = (bf16[896,256]{1,0:T(8,128)(2,1)S(1)}, bf16[896,256]{1,0:T(8,128)(2,1)S(1)}, u32[]{:S(2)}, u32[]{:S(2)}) collective-permute-start(bf16[896,256]{1,0:T(8,128)(2,1)S(1)} %collective-permute-done.1.b0), channel_id=1, source_target_pairs={{0,8},{4,12},{8,0},{12,4},{16,24},{20,28},{24,16},{28,20},{1,9},{5... | collective-permute-start | bytes 1376264 | tf_op jit(solution)/shard_map/ppermute | solution.py:288
  22.7 1.0 %fusion = (f32[512,64]{1,0:T(8,128)S(1)}, f32[512,64]{1,0:T(8,128)S(1)}, f32[512,64]{1,0:T(8,128)S(1)}) fusion(f32[64]{0:T(128)S(1)} %multiply_power_fusion, f32[512]{0:T(512)S(1)} %add_convert_fusion), kind=kLoop, calls=%fused_computation.4 | loop fusion | flops 65536 | bytes 395520 | tf_op jit(solution)/shard_map/neg | solution.py:330
  23.9 2.8 %shard_map.98 = (bf16[512,2048]{1,0:T(8,128)(2,1)S(1)}, f32[8,128]{1,0:T(8,128)S(1)}, f32[512,256]{1,0:T(8,128)S(1)}) custom-call(s32[1]{0:T(128)} %bitcast.2.at, bf16[512,2048]{1,0:T(8,128)(2,1)} %collective-permute-done.hid, f32[64,128]{1,0:T(8,128)S(1)} %bitcast.21, bf16[2048,256]{1,0:T(8,128)(2,1)S(1)} %copy-done, ...), custom_call_target="tpu_custom_call" | custom-call | flops 1073741824 | bytes 1048576 | tf_op jit(solution)/shard_map/pallas_call | solution.py:295
  26.7 1.0 %shard_map.100.early = f32[512,256]{1,0:T(8,128)S(1)} custom-call(s32[4]{0:T(128)S(1)} %pad_add_fusion.2.at, bf16[512,2048]{1,0:T(8,128)(2,1)S(1)} %get-tuple-element.17.mine, bf16[512,2048]{1,0:T(8,128)(2,1)S(1)} %get-tuple-element.18.other, bf16[896,256]{1,0:T(8,128)(2,1)S(1)} %collective-permute-done.1.b0), custom_call_target="tpu_custom_call" | custom-call | flops 536870912 | bytes 1048576 | tf_op jit(solution)/shard_map/pallas_call | solution.py:309
  27.7 6.1 %collective-permute-done.4.b3 = bf16[1408,256]{1,0:T(8,128)(2,1)S(1)} collective-permute-done((bf16[1408,256]{1,0:T(8,128)(2,1)}, bf16[1408,256]{1,0:T(8,128)(2,1)S(1)}, u32[]{:S(2)}, u32[]{:S(2)}) %collective-permute-start.4) | collective-permute-done | bytes 720928 | tf_op jit(solution)/shard_map/ppermute | solution.py:286
  33.8 1.7 %shard_map.102 = (bf16[512,128]{1,0:T(8,128)(2,1)S(1)}, bf16[512,128]{1,0:T(8,128)(2,1)S(1)}) custom-call(s32[4]{0:T(128)S(1)} %pad_add_fusion.2.at, bf16[512,2048]{1,0:T(8,128)(2,1)S(1)} %get-tuple-element.17.mine, bf16[512,2048]{1,0:T(8,128)(2,1)S(1)} %get-tuple-element.18.other, f32[512,256]{1,0:T(8,128)S(1)} %shard_map.100.early, ...), custom_call_target="tpu_custom_call" | custom-call | flops 1073741824 | bytes 1048576 | tf_op jit(solution)/shard_map/pallas_call | solution.py:315
  35.5 1.8 %collective-permute-start.5 = (bf16[512,128]{1,0:T(8,128)(2,1)S(1)}, bf16[512,128]{1,0:T(8,128)(2,1)S(1)}, u32[]{:S(2)}, u32[]{:S(2)}) collective-permute-start(bf16[512,128]{1,0:T(8,128)(2,1)S(1)} %get-tuple-element.19), channel_id=1, source_target_pairs={{0,2},{1,3},{2,0},{3,1},{4,6},{5,7},{6,4},{7,5},{8,10},{9,11},{10,... | collective-permute-start | bytes 393224 | tf_op jit(solution)/shard_map/ppermute | solution.py:321
  39.6 1.8 %collective-permute-start.7 = (bf16[512,128]{1,0:T(8,128)(2,1)S(1)}, bf16[512,128]{1,0:T(8,128)(2,1)S(1)}, u32[]{:S(2)}, u32[]{:S(2)}) collective-permute-start(bf16[512,128]{1,0:T(8,128)(2,1)S(1)} %get-tuple-element.23), channel_id=1, source_target_pairs={{0,2},{1,3},{2,0},{3,1},{4,6},{5,7},{6,4},{7,5},{8,10},{9,11},{10,... | collective-permute-start | bytes 393224 | tf_op jit(solution)/shard_map/ppermute | solution.py:322
  41.4 1.8 %shard_map.103 = (f32[512,512]{1,0:T(8,128)S(1)}, f32[8,2,512]{2,1,0:T(2,128)}) custom-call(s32[1]{0:T(128)} %bitcast.1.first, f32[512,256]{1,0:T(8,128)S(1)} %get-tuple-element.16.refs_0_, bf16[512,128]{1,0:T(8,128)(2,1)S(1)} %collective-permute-done.5.refs_1_, f32[8,128]{1,0:T(8,128)S(1)} %get-tuple-element.20.refs_2_, ...), custom_call_target="tpu_custom_call" | custom-call | flops 268435456 | bytes 1048576 | tf_op jit(solution)/shard_map/pallas_call | solution.py:338
  43.2 5.8 %all-to-all-start = ((f32[8,2,512]{2,1,0:T(2,128)}), f32[8,2,512]{2,1,0:T(2,128)S(1)}, u32[]{:S(2)}, u32[]{:S(2)}) async-start(f32[8,2,512]{2,1,0:T(2,128)} %get-tuple-element.21.mine), calls=%async_computation | async-start | bytes 65536 | tf_op jit(solution)/shard_map/all_to_all | solution.py:345
  49.1 6.6 %all-to-all-done.got = f32[8,2,512]{2,1,0:T(2,128)S(1)} async-done(((f32[8,2,512]{2,1,0:T(2,128)}), f32[8,2,512]{2,1,0:T(2,128)S(1)}, u32[]{:S(2)}, u32[]{:S(2)}) %all-to-all-start) | async-done | bytes 32800 | tf_op jit(solution)/shard_map/all_to_all | solution.py:345
  55.7 1.9 %shard_map.104 = f32[8,128]{1,0:T(8,128)} custom-call(s32[2]{0:T(128)S(1)} %pad_add_fusion.1.sizes, f32[8,2,512]{2,1,0:T(2,128)S(1)} %all-to-all-done.got, f32[8,2,512]{2,1,0:T(2,128)} %get-tuple-element.21.mine, f32[512,512]{1,0:T(8,128)S(1)} %get-tuple-element.22.expo, f32[512,256]{1,0:T(8,128)S(1)} %get-tuple-element.16.refs_0_, ...), custom_call_target="tpu_custom_call" | custom-call | flops 67108864 | bytes 1048576 | tf_op jit(solution)/shard_map/pallas_call | solution.py:347
  57.6 3.3 %all-to-all-start.1 = ((f32[8,1,128]{2,1,0:T(1,128)}), f32[8,1,128]{2,1,0:T(1,128)S(1)}, u32[]{:S(2)}, u32[]{:S(2)}) async-start(f32[8,1,128]{2,1,0:T(1,128)} %bitcast.15), calls=%async_computation.1 | async-start | bytes 8192 | tf_op jit(solution)/shard_map/all_to_all | solution.py:356
  61.0 6.4 %all-to-all-done.1 = f32[8,1,128]{2,1,0:T(1,128)S(1)} async-done(((f32[8,1,128]{2,1,0:T(1,128)}), f32[8,1,128]{2,1,0:T(1,128)S(1)}, u32[]{:S(2)}, u32[]{:S(2)}) %all-to-all-start.1) | async-done | bytes 4128 | tf_op jit(solution)/shard_map/all_to_all | solution.py:356
  67.4 1.5 %shard_map.105 = (f32[1,4]{1,0:T(1,128)}, f32[1,1]{1,0:T(1,128)}) custom-call(s32[3]{0:T(128)S(1)} %pad_add_fusion.sizes, f32[8,128]{1,0:T(8,128)S(1)} %bitcast.19), custom_call_target="tpu_custom_call" | custom-call | flops 1048576 | bytes 1048576 | tf_op jit(solution)/shard_map/pallas_call | solution.py:357
  (29 shorter events, 2.8 us)
Async XLA Ops:
  0.6 23.3 %collective-permute-start = (bf16[512,2048]{1,0:T(8,128)(2,1)}, bf16[512,2048]{1,0:T(8,128)(2,1)}, u32[]{:S(2)}, u32[]{:S(2)}) collective-permute-start(bf16[512,2048]{1,0:T(8,128)(2,1)} %hid.1), channel_id=1, source_target_pairs={{0,1},{1,0},{2,3},{3,2},{4,5},{5,4},{6,7},{7,6},{8,9},{9,8},{10,11... | collective-permute-start | bytes 6291464 | tf_op jit(solution)/shard_map/ppermute | solution.py:287
  4.4 14.6 %collective-permute-start.1 = (bf16[896,256]{1,0:T(8,128)(2,1)}, bf16[896,256]{1,0:T(8,128)(2,1)S(1)}, u32[]{:S(2)}, u32[]{:S(2)}) collective-permute-start(bf16[896,256]{1,0:T(8,128)(2,1)} %shard_map.99), channel_id=1, source_target_pairs={{0,2},{1,3},{2,0},{3,1},{4,6},{5,7},{6,4},{7,5},{8,10},{9,11},{10,... | collective-permute-start | bytes 1376264 | tf_op jit(solution)/shard_map/ppermute | solution.py:282
  10.4 23.4 %collective-permute-start.4 = (bf16[1408,256]{1,0:T(8,128)(2,1)}, bf16[1408,256]{1,0:T(8,128)(2,1)S(1)}, u32[]{:S(2)}, u32[]{:S(2)}) collective-permute-start(bf16[1408,256]{1,0:T(8,128)(2,1)} %shard_map.101), channel_id=1, source_target_pairs={{0,2},{1,3},{2,0},{3,1},{4,6},{5,7},{6,4},{7,5},{8,10},{9,11},{10,... | collective-permute-start | bytes 2162696 | tf_op jit(solution)/shard_map/ppermute | solution.py:286
  12.7 2.3 %copy-start.3 = (f32[8192]{0:T(1024)S(1)}, f32[8192]{0:T(1024)}, u32[]{:S(2)}) copy-start(f32[8192]{0:T(1024)} %param.9) | copy-start | bytes 98308
  15.0 1.2 %copy-start.1 = (bf16[2048,256]{1,0:T(8,128)(2,1)S(1)}, bf16[2048,256]{1,0:T(8,128)(2,1)}, u32[]{:S(2)}) copy-start(bf16[2048,256]{1,0:T(8,128)(2,1)} %shard_map.96.weights) | copy-start | bytes 3145732
  16.2 1.6 %copy-start.2 = (bf16[512,2048]{1,0:T(8,128)(2,1)S(1)}, bf16[512,2048]{1,0:T(8,128)(2,1)}, u32[]{:S(2)}) copy-start(bf16[512,2048]{1,0:T(8,128)(2,1)} %hid.1) | copy-start | bytes 6291460
  17.8 6.1 %copy-start = (bf16[2048,256]{1,0:T(8,128)(2,1)S(1)}, bf16[2048,256]{1,0:T(8,128)(2,1)}, u32[]{:S(2)}) copy-start(bf16[2048,256]{1,0:T(8,128)(2,1)} %shard_map.95.weights) | copy-start | bytes 3145732
  19.0 14.8 %collective-permute-start.2 = (bf16[896,256]{1,0:T(8,128)(2,1)S(1)}, bf16[896,256]{1,0:T(8,128)(2,1)S(1)}, u32[]{:S(2)}, u32[]{:S(2)}) collective-permute-start(bf16[896,256]{1,0:T(8,128)(2,1)S(1)} %collective-permute-done.1.b0), channel_id=1, source_target_pairs={{0,4},{4,0},{8,12},{12,8},{16,20},{20,16},{24,28},{28,24},{1,5},{5... | collective-permute-start | bytes 1376264 | tf_op jit(solution)/shard_map/ppermute | solution.py:288
  21.1 12.7 %collective-permute-start.3 = (bf16[896,256]{1,0:T(8,128)(2,1)S(1)}, bf16[896,256]{1,0:T(8,128)(2,1)S(1)}, u32[]{:S(2)}, u32[]{:S(2)}) collective-permute-start(bf16[896,256]{1,0:T(8,128)(2,1)S(1)} %collective-permute-done.1.b0), channel_id=1, source_target_pairs={{0,8},{4,12},{8,0},{12,4},{16,24},{20,28},{24,16},{28,20},{1,9},{5... | collective-permute-start | bytes 1376264 | tf_op jit(solution)/shard_map/ppermute | solution.py:288
  27.6 11.9 %copy-start.4 = (bf16[64,1024]{1,0:T(8,128)(2,1)S(1)}, bf16[64,1024]{1,0:T(8,128)(2,1)}, u32[]{:S(2)}) copy-start(bf16[64,1024]{1,0:T(8,128)(2,1)} %param.12) | copy-start | bytes 393220
  35.5 5.9 %collective-permute-start.5 = (bf16[512,128]{1,0:T(8,128)(2,1)S(1)}, bf16[512,128]{1,0:T(8,128)(2,1)S(1)}, u32[]{:S(2)}, u32[]{:S(2)}) collective-permute-start(bf16[512,128]{1,0:T(8,128)(2,1)S(1)} %get-tuple-element.19), channel_id=1, source_target_pairs={{0,2},{1,3},{2,0},{3,1},{4,6},{5,7},{6,4},{7,5},{8,10},{9,11},{10,... | collective-permute-start | bytes 393224 | tf_op jit(solution)/shard_map/ppermute | solution.py:321
  37.3 4.1 %collective-permute-start.6 = (f32[8,128]{1,0:T(8,128)S(1)}, f32[8,128]{1,0:T(8,128)S(1)}, u32[]{:S(2)}, u32[]{:S(2)}) collective-permute-start(f32[8,128]{1,0:T(8,128)S(1)} %get-tuple-element.20.refs_2_), channel_id=1, source_target_pairs={{0,2},{1,3},{2,0},{3,1},{4,6},{5,7},{6,4},{7,5},{8,10},{9,11},{10,... | collective-permute-start | bytes 12296 | tf_op jit(solution)/shard_map/ppermute | solution.py:304
  39.6 9.5 %collective-permute-start.7 = (bf16[512,128]{1,0:T(8,128)(2,1)S(1)}, bf16[512,128]{1,0:T(8,128)(2,1)S(1)}, u32[]{:S(2)}, u32[]{:S(2)}) collective-permute-start(bf16[512,128]{1,0:T(8,128)(2,1)S(1)} %get-tuple-element.23), channel_id=1, source_target_pairs={{0,2},{1,3},{2,0},{3,1},{4,6},{5,7},{6,4},{7,5},{8,10},{9,11},{10,... | collective-permute-start | bytes 393224 | tf_op jit(solution)/shard_map/ppermute | solution.py:322
  43.2 12.5 %all-to-all-start = ((f32[8,2,512]{2,1,0:T(2,128)}), f32[8,2,512]{2,1,0:T(2,128)S(1)}, u32[]{:S(2)}, u32[]{:S(2)}) async-start(f32[8,2,512]{2,1,0:T(2,128)} %get-tuple-element.21.mine), calls=%async_computation | async-start | bytes 65536 | tf_op jit(solution)/shard_map/all_to_all | solution.py:345
  57.6 9.8 %all-to-all-start.1 = ((f32[8,1,128]{2,1,0:T(1,128)}), f32[8,1,128]{2,1,0:T(1,128)S(1)}, u32[]{:S(2)}, u32[]{:S(2)}) async-start(f32[8,1,128]{2,1,0:T(1,128)} %bitcast.15), calls=%async_computation.1 | async-start | bytes 8192 | tf_op jit(solution)/shard_map/all_to_all | solution.py:356

commit v4 on v3

v4 whole, which is shorter than its diff:
```python
import functools

import jax
import jax.numpy as jnp
from jax import lax
from jax.experimental import pallas as pl
from jax.experimental.pallas import tpu as pltpu
from jax.sharding import PartitionSpec as P

BLK = 128
LANES = 128
KERNEL_LIMIT = 15
REACH = (KERNEL_LIMIT - 1) // 2
EDGE = 16
CORES = 2
GROUP = 4
MASKED = -1e30

VMEM = pl.BlockSpec(memory_space=pltpu.VMEM)
SMEM = pl.BlockSpec(memory_space=pltpu.SMEM)
F32, BF16 = jnp.float32, jnp.bfloat16


def sds(shape, dtype):
    return jax.ShapeDtypeStruct(shape, dtype)


def call(body, out, ins, scratch=(), outs=None, flops=1 << 20, limit=40 << 20):
    return pl.pallas_call(
        body,
        out_shape=out,
        in_specs=ins,
        out_specs=outs if outs is not None else jax.tree.map(lambda _: VMEM, out),
        scratch_shapes=list(scratch),
        cost_estimate=pl.CostEstimate(flops=flops, bytes_accessed=1 << 20, transcendentals=0),
        compiler_params=pltpu.CompilerParams(vmem_limit_bytes=limit),
    )


def iota(shape, dim):
    return lax.broadcasted_iota(jnp.int32, shape, dim)


def to_lanes(col):
    n = col.shape[0]
    here = iota((n, LANES), 0) == iota((n, LANES), 1)
    return jnp.sum(jnp.where(here, jnp.broadcast_to(col, (n, LANES)), 0.0), axis=0, keepdims=True)


def to_rows(row, n):
    here = iota((n, LANES), 0) == iota((n, LANES), 1)
    return jnp.sum(jnp.where(here, jnp.broadcast_to(row, (n, LANES)), 0.0), axis=1, keepdims=True)


def norm_kernel(at, hid, gain, weights, *refs):
    more = refs[:-3]
    normed, sumsq, acc = refs[-3:]
    tok, feats = hid.shape
    line = at[0] // LANES
    nb = tok // LANES
    sumsq[...] = more[0][...] if more else jnp.zeros_like(sumsq)
    for b in range(nb):
        rows = pl.ds(b * LANES, LANES)
        folded = None
        for t in range(feats // LANES):
            lanes = pl.ds(t * LANES, LANES)
            raw = hid[rows, lanes].astype(F32)
            folded = raw * raw if folded is None else folded + raw * raw
            normed[rows, lanes] = (raw * gain[pl.ds(line + t, 1), :]).astype(BF16)
        sumsq[b : b + 1, :] += to_lanes(jnp.sum(folded, axis=1, keepdims=True))
    out = jnp.dot(normed[...], weights[...], preferred_element_type=F32)
    acc[...] = out + more[1][...] if more else out


def part_of(at, rows, blk):
    q = blk.shape[0]
    cols = pl.ds(pl.multiple_of(at * q, LANES), q)
    return jnp.dot(rows[:, cols], blk[...], preferred_element_type=F32)


def early_kernel(at, mine, other, a0, b0, out):
    out[...] = part_of(at[0], mine, a0) + part_of(at[0], other, b0)


def middle_kernel(at, mine, total, a1, a2, a3, out):
    acc = total[...]
    for k, blk in enumerate((a1, a2, a3)):
        acc = acc + part_of(at[k + 1], mine, blk)
    out[...] = acc


def late_kernel(at, other, total, b1, b2, b3, out_k, out_v):
    head = out_k.shape[1]
    acc = total[...]
    for k, blk in enumerate((b1, b2, b3)):
        acc = acc + part_of(at[k + 1], other, blk)
    out_k[...] = acc[:, :head].astype(BF16)
    out_v[...] = acc[:, head:].astype(BF16)


def inverse_rms(sqs, full_width):
    sumsq = sqs[0][...]
    for sq in sqs[1:]:
        sumsq = sumsq + sq[...]
    return lax.rsqrt(sumsq / full_width + 1e-05)


def score_kernel(full_width, scale_by, first, *refs):
    n_off = (len(refs) - 10) // 2
    acc, parts, sqs = refs[0], refs[1 : 1 + n_off], refs[1 + n_off : 2 + 2 * n_off]
    cos, sin, q, limit, expo, stats, keys, rows_of = refs[2 + 2 * n_off :]
    tok, head = keys.shape
    window = q.shape[0]
    for j in range(q.shape[1] // head):
        rows_of[j * window : (j + 1) * window, :] = q[:, j * head : (j + 1) * head]
    inv = inverse_rms(sqs, full_width)
    for b in range(tok // LANES):
        rows = pl.ds(b * LANES, LANES)
        k = acc[rows, :head]
        for p in parts:
            k = k + p[rows, :].astype(F32)
        k = k * to_rows(inv[b : b + 1, :], LANES)
        keys[rows, :] = (k * cos[rows, :] + pltpu.roll(k, head // 2, 1) * sin[rows, :]).astype(BF16)
    scores = lax.dot_general(
        keys[...], rows_of[...], (((1,), (1,)), ((), ())), preferred_element_type=F32
    ) * scale_by
    open_to = tok - window
    token = first[0] + open_to + iota((window, 1), 0)
    tail = jnp.where(token <= limit[...], scores[open_to:, :], MASKED)
    body = scores[:open_to, :]
    top = jnp.maximum(
        jnp.max(body, axis=0, keepdims=True), jnp.max(tail, axis=0, keepdims=True)
    )
    body, tail = jnp.exp(body - top), jnp.exp(tail - top)
    expo[:open_to, :] = body
    expo[open_to:, :] = tail
    own = jnp.sum(body, axis=0, keepdims=True) + jnp.sum(tail, axis=0, keepdims=True)
    for d in range(stats.shape[0]):
        stats[d, 0:1, :] = top
        stats[d, 1:2, :] = own


def value_kernel(full_width, *refs):
    n_off = (len(refs) - 3) // 2
    acc, parts, sqs, out = refs[0], refs[1 : 1 + n_off], refs[1 + n_off : 2 + 2 * n_off], refs[-1]
    head = acc.shape[1] // 2
    inv = inverse_rms(sqs, full_width)
    out[...] = jnp.zeros_like(out)
    for b in range(acc.shape[0] // LANES):
        rows = pl.ds(b * LANES, LANES)
        v = acc[rows, head:]
        for p in parts:
            v = v + p[rows, :].astype(F32)
        total = to_lanes(jnp.sum(jnp.abs(v), axis=1, keepdims=True))
        out[b : b + 1, :] = total * (1.0 / head) * inv[b : b + 1, :]


def widen(column, below, above, lane, halfspan):
    pooled = column
    for shift in range(1, REACH + 1):
        right = pltpu.roll(jnp.where(lane < shift, below, column), LANES - shift, 1)
        left = pltpu.roll(jnp.where(lane >= LANES - shift, above, column), shift, 1)
        pooled = jnp.where(
            shift <= halfspan, jnp.maximum(jnp.maximum(pooled, right), left), pooled
        )
    return pooled


def pool_kernel(window, sizes, got, mine, expo, vmag, win, spread):
    tok = expo.shape[0]
    nb = tok // LANES
    row_top = got[0, 0:1, :]
    for d in range(1, got.shape[0]):
        row_top = jnp.maximum(row_top, got[d, 0:1, :])
    row_total = jnp.zeros_like(row_top)
    for d in range(got.shape[0]):
        row_total = row_total + got[d, 1:2, :] * jnp.exp(got[d, 0:1, :] - row_top)
    weight = jnp.exp(mine[0, 0:1, :] - row_top) / row_total
    weight = jnp.where(win[...] >= window - sizes[0], weight, 0.0)
    height = vmag.shape[0]
    line = iota((height, LANES), 0)
    lane = iota((height, LANES), 1)
    column = jnp.zeros((height, LANES), F32)
    for b in range(nb):
        mass = jnp.sum(expo[b * LANES : (b + 1) * LANES, :] * weight, axis=1, keepdims=True)
        column = jnp.where(line == b, jnp.broadcast_to(to_lanes(mass), (height, LANES)), column)
    column = column * vmag[...]
    below, above = pltpu.roll(column, height - 1, 0), pltpu.roll(column, 1, 0)
    halfspan = lax.shift_right_arithmetic(sizes[1] - 1, 1)
    pooled = widen(column, below, above, lane, halfspan)
    place = line * LANES + lane
    inner = (place >= REACH) & (place < tok - REACH)
    sums = to_lanes(jnp.sum(jnp.where(inner, pooled, 0.0), axis=1, keepdims=True))
    flat = lane[0:1, :]
    last = pltpu.roll(column[nb - 1 : nb, :], 2 * EDGE, 1)
    said = jnp.where(flat < EDGE, column[0:1, :], jnp.where(flat < 2 * EDGE, last, pltpu.roll(sums, 2 * EDGE, 1)))
    spread[...] = jnp.broadcast_to(said, spread.shape)


def rank_kernel(nb, sizes, said, blocks, share):
    v = said[...]
    n = v.shape[0]
    line, lane = iota(v.shape, 0), iota(v.shape, 1)
    following = pltpu.roll(v, n - 1, 0)
    seam = jnp.where(lane < EDGE, pltpu.roll(v, LANES - EDGE, 1), pltpu.roll(following, EDGE, 1))
    seam = jnp.where(lane < 2 * EDGE, seam, 0.0)
    end = line == n - 1
    apart = LANES // 2
    halfspan = lax.shift_right_arithmetic(sizes[1] - 1, 1)
    both = jnp.where(end & (lane >= EDGE), 0.0, seam) + pltpu.roll(
        jnp.where(end & (lane < EDGE), 0.0, seam), apart, 1
    )
    pooled = both
    for shift in range(1, REACH + 1):
        near = jnp.maximum(pltpu.roll(both, shift, 1), pltpu.roll(both, LANES - shift, 1))
        pooled = jnp.where(shift <= halfspan, jnp.maximum(pooled, near), pooled)
    tail = (lane >= EDGE - REACH) & (lane < EDGE)
    lead = (lane >= apart + EDGE) & (lane < apart + EDGE + REACH)
    tail = jnp.sum(jnp.where(tail, pooled, 0.0), axis=1, keepdims=True)
    lead = jnp.sum(jnp.where(lead, pooled, 0.0), axis=1, keepdims=True)
    lead = pltpu.roll(jnp.broadcast_to(lead, v.shape), 1, 0)
    b = pltpu.roll(v, LANES - 2 * EDGE, 1)
    b = b + jnp.where(lane == 0, lead, 0.0) + jnp.where(lane == nb - 1, tail, 0.0)
    b = jnp.where(lane < nb, b, 0.0)
    own = jnp.sum(jnp.where(line == sizes[2], b, 0.0), axis=0, keepdims=True)
    blocks[...] = own[:, :nb]
    place = line * nb + lane
    rank = jnp.zeros(v.shape, jnp.int32)

    def turned(t, k):
        return jnp.where(lane >= k, pltpu.roll(t, k, 1), pltpu.roll(t, LANES + k - nb, 1)) if k else t

    for k in range(nb):
        bk, pk = turned(b, k), turned(place, k)
        for m in range(n):
            bm, pm = (pltpu.roll(bk, m, 0), pltpu.roll(pk, m, 0)) if m else (bk, pk)
            rank = rank + jnp.where((bm > b) | ((bm == b) & (pm < place)), 1, 0)

    def add(t):
        return jnp.sum(jnp.sum(t, axis=1, keepdims=True), axis=0, keepdims=True)

    kept = jnp.where((lane < nb) & (rank < sizes[0]), b, 0.0)
    share[...] = add(kept) / add(b)


def local(
    hidden, gain, key_matrix, value_matrix, queries, window_len, kernel_width, kept_block_count
):
    tok, feats = hidden.shape
    full_width = gain.shape[0]
    head = key_matrix.shape[1]
    n_seq, n_head = lax.axis_size("seq"), lax.axis_size("head")
    n_x = n_head // CORES
    s, h = lax.axis_index("seq"), lax.axis_index("head")
    x, c = h // CORES, h % CORES
    i = s % GROUP
    q = feats // GROUP
    total_tokens = tok * n_seq
    offsets = range(1, n_x)

    def shift_x(offset):
        return [
            (a * CORES + b, (a + offset) % n_x * CORES + b) for a in range(n_x) for b in range(CORES)
        ]

    def flip(bit):
        return [(j, j ^ bit) for j in range(n_seq)]

    def rows_at(start, count):
        return jnp.concatenate(
            [lax.dynamic_slice_in_dim(m, start, count) for m in (key_matrix, value_matrix)], axis=1
        )

    def cross(o, block):
        chip = (x - o) % n_x
        return [
            lax.ppermute(
                rows_at((chip * CORES + (c ^ part)) * feats + block * q, q), "head", shift_x(-o)
            )
            for part in range(CORES)
        ]

    firsts = [cross(o, i) for o in offsets]
    seconds = [cross(o, 3 - i) for o in offsets]
    swapped = lax.ppermute(hidden, "head", [(j, j ^ 1) for j in range(n_head)])
    blocks = [
        [
            [firsts[o - 1][part]]
            + [lax.ppermute(firsts[o - 1][part], "seq", flip(bit)) for bit in (1, 2)]
            + [seconds[o - 1][part]]
            for part in range(CORES)
        ]
        for o in offsets
    ]

    lines = -(-(tok // LANES) // 8) * 8
    gain_lines = gain.reshape(full_width // LANES, LANES)

    def norm(start, rows, more):
        weights = rows_at(start, feats)
        return call(
            norm_kernel,
            [sds((tok, feats), BF16), sds((lines, LANES), F32), sds((tok, 2 * head), F32)],
            [SMEM] + [VMEM] * (3 + len(more)),
            flops=1 << 30,
        )(start.reshape(1), rows, gain_lines, weights, *more)

    mine, sumsq, acc = norm(h * feats, hidden, ())
    other, sumsq, acc = norm((h ^ 1) * feats, swapped, (sumsq, acc))
    sqs = [sumsq] + [lax.ppermute(sumsq, "head", shift_x(o)) for o in offsets]

    parts_k, parts_v = [], []
    slabs = jnp.stack([i ^ k for k in range(GROUP)])
    wide, thin = sds((tok, 2 * head), F32), sds((tok, head), BF16)
    for o in offsets:
        half_0, half_1 = blocks[o - 1]
        part = call(early_kernel, wide, [SMEM] + [VMEM] * 4, flops=1 << 29)(
            slabs, mine, other, half_0[0], half_1[0]
        )
        part = call(middle_kernel, wide, [SMEM] + [VMEM] * 5, flops=1 << 29)(
            slabs, mine, part, *half_0[1:]
        )
        part_k, part_v = call(
            late_kernel, [thin, thin], [SMEM] + [VMEM] * 5, flops=1 << 29
        )(slabs, other, part, *half_1[1:])
        parts_k.append(lax.ppermute(part_k, "head", shift_x(o)))
        parts_v.append(lax.ppermute(part_v, "head", shift_x(o)))

    half = head // 2
    freq = 500000.0 ** (-(jnp.arange(half).astype(F32) * 2.0) / head)
    token = s * tok + jnp.arange(tok)
    angle = token.astype(F32)[:, None] * freq[None, :]
    cos, sin = jnp.cos(angle), jnp.sin(angle)
    cos = jnp.concatenate([cos, cos], axis=1)
    sin = jnp.concatenate([-sin, sin], axis=1)

    window = queries.shape[0]
    group_heads = queries.shape[1] // head
    rows = window * group_heads
    row_window = (jnp.arange(rows) % window).astype(jnp.int32)[None, :]
    limit = total_tokens - window + row_window
    expo, stats = call(
        functools.partial(score_kernel, full_width, head ** (-0.5)),
        [sds((tok, rows), F32), sds((n_seq, 2, rows), F32)],
        [SMEM] + [VMEM] * (6 + 2 * len(offsets)),
        scratch=[pltpu.VMEM((tok, head), BF16), pltpu.VMEM((rows, head), BF16)],
        flops=1 << 28,
    )((s * tok).reshape(1), acc, *parts_k, *sqs, cos, sin, queries, limit)
    got = lax.all_to_all(stats, "seq", 0, 0, tiled=True)
    nb = tok // BLK
    vmag = call(
        functools.partial(value_kernel, full_width),
        sds((lines, LANES), F32),
        [VMEM] * (2 + 2 * len(offsets)),
        flops=1 << 28,
    )(acc, *parts_v, *sqs)
    spread = call(
        functools.partial(pool_kernel, window),
        sds((n_seq, LANES), F32),
        [SMEM] + [VMEM] * 5,
        flops=1 << 26,
    )(jnp.concatenate([window_len, kernel_width]), got, stats, expo, vmag, row_window)
    said = lax.all_to_all(spread, "seq", 0, 0, tiled=True)
    local_blocks, fraction = call(
        functools.partial(rank_kernel, nb),
        [sds((1, nb), F32), sds((1, 1), F32)],
        [SMEM, VMEM],
        flops=1 << 20,
    )(jnp.concatenate([kept_block_count, kernel_width, s.reshape(1)]), said)
    return (local_blocks, fraction.reshape(1))


def solution(mesh):
    return jax.shard_map(
        local,
        mesh=mesh,
        in_specs=(
            P("seq", "head"),
            P(),
            P(None, "head"),
            P(None, "head"),
            P(None, "head"),
            P("head"),
            P("head"),
            P("head"),
        ),
        out_specs=(P("head", "seq"), P("head")),
        check_vma=False,
    )
```

time: 69.4 us -> 69.8 us (level)
  Pallas kernels: 21.4 us -> 12.5 us
  starting transfers between devices: 20 us -> 24.8 us
  other arithmetic: 2.73 us -> 6.44 us
  local copies, waits for them, and re-layouts: 2.89 us -> 5.35 us
  waiting for transfers between devices: 19.1 us -> 17.5 us
    pallas_call x7 -> x5, Pallas kernels: 14.2 us -> 5.17 us  [the longest x1 1.79 us: local(): call(functools.partial(pool_kernel, window), sds((n_seq, LANES), F32), [S...]
    ppermute x4 -> x8, starting transfers between devices: 6.37 us -> 13.4 us  [the longest x4 6.79 us: local(): lax.ppermute(firsts[o - 1][part], 'seq', flip(bit))]
    dynamic_slice x0 -> x2, local copies, waits for them, and re-layouts: none -> 3.74 us  [rows_at(): lax.dynamic_slice_in_dim(m, start, count)]
    concatenate x0 -> x6, other arithmetic: none -> 3.19 us  [rows_at(): jnp.concatenate([lax.dynamic_slice_in_dim(m, start, count) for m in (key_...]
    ppermute x4 -> x8, waiting for transfers between devices: 6.13 us -> 4.12 us  [the longest x4 4.11 us: cross(): lax.ppermute(rows_at((chip * CORES + (c ^ part)) * feats + block * q, q),...]
    all_to_all x1, starting transfers between devices: 5.82 us -> 3.88 us  [local(): got = lax.all_to_all(stats, 'seq', 0, 0, tiled=True)]
    another operation x2 -> x0, other arithmetic: 1.27 us -> none  [pack(): jnp.stack(starts)]
    ppermute x1, waiting for transfers between devices: 0.01 us -> 1.24 us  [local(): sqs = [sumsq] + [lax.ppermute(sumsq, 'head', shift_x(o)) for o in offsets]]
  transfers between devices with their start and end apart: 10 -> 14, of which waited for: 3 -> 5; matrix products, arithmetic and copies ran while one was open for 4% -> 15% of each run, Pallas kernels for 24% -> 12%
where the time goes in v4:
time: 69.8 us; the launch traced here: 69.3 us
  starting transfers between devices  24.8 us (36%)
  waiting for transfers between devices  17.5 us (25%)
  Pallas kernels  12.5 us (18%)
  other arithmetic  6.44 us (9%)
  local copies, waits for them, and re-layouts  5.35 us (8%)
  between operations  2.75 us (4%)
    ppermute x4, starting transfers between devices, local(): lax.ppermute(firsts[o - 1][part], 'seq', flip(bit))  6.79 us
    ppermute x4, starting transfers between devices, cross(): lax.ppermute(rows_at((chip * CORES + (c ^ part)) * feats + block * q, q),...  6.62 us
    all_to_all x1, waiting for transfers between devices, local(): said = lax.all_to_all(spread, 'seq', 0, 0, tiled=True)  6.35 us
    all_to_all x1, waiting for transfers between devices, local(): got = lax.all_to_all(stats, 'seq', 0, 0, tiled=True)  5.78 us
    ppermute x4, waiting for transfers between devices, cross(): lax.ppermute(rows_at((chip * CORES + (c ^ part)) * feats + block * q, q),...  4.11 us
    pallas_call x2, Pallas kernels, norm(): call(norm_kernel, [sds((tok, feats), BF16), sds((lines, LANES), F32), sds...  3.95 us
    all_to_all x1, starting transfers between devices, local(): got = lax.all_to_all(stats, 'seq', 0, 0, tiled=True)  3.88 us
    dynamic_slice x2, local copies, waits for them, and re-layouts, rows_at(): lax.dynamic_slice_in_dim(m, start, count)  3.74 us
  transfers between devices with their start and end apart: 14, of which 5 were waited for; matrix products, arithmetic and copies ran while one was open for 15% of the time, Pallas kernels for 12%

profile of v4, /device:TPU:0, one launch (start us, length us, event | category | flops | bytes accessed | tf_op | source)
XLA Modules:
  0.0 69.3 jit_solution(4927275091433806553)
XLA Ops:
  1.2 2.1 %constant_dynamic-slice_fusion = (bf16[512,128]{1,0:T(8,128)(2,1)}, bf16[512,128]{1,0:T(8,128)(2,1)S(1)}, bf16[512,128]{1,0:T(8,128)(2,1)S(1)}, bf16[512,128]{1,...) fusion(bf16[8192,128]{1,0:T(8,128)(2,1)} %param.11, ...), kind=kLoop, calls=%fused_computation.12 | loop fusion | bytes 2097168 | tf_op jit(solution)/shard_map/dynamic_slice | solution.py:271
  4.0 2.6 %collective-permute-start.1 = (bf16[512,256]{1,0:T(8,128)(2,1)}, bf16[512,256]{1,0:T(8,128)(2,1)S(1)}, u32[]{:S(2)}, u32[]{:S(2)}) collective-permute-start(bf16[512,256]{1,0:T(8,128)(2,1)} %pad_maximum_fusion.2), channel_id=1, source_target_pairs={{0,2},{1,3},{2,0},{3,1},{4,6},{5,7},{6,4},{7,5},{8,10},{9,11},{10,... | collective-permute-start | bytes 786440 | tf_op jit(solution)/shard_map/ppermute | solution.py:277
  8.0 2.0 %collective-permute-start.5 = (bf16[512,256]{1,0:T(8,128)(2,1)}, bf16[512,256]{1,0:T(8,128)(2,1)S(1)}, u32[]{:S(2)}, u32[]{:S(2)}) collective-permute-start(bf16[512,256]{1,0:T(8,128)(2,1)} %pad_maximum_fusion.4), channel_id=1, source_target_pairs={{0,2},{1,3},{2,0},{3,1},{4,6},{5,7},{6,4},{7,5},{8,10},{9,11},{10,... | collective-permute-start | bytes 786440 | tf_op jit(solution)/shard_map/ppermute | solution.py:277
  10.1 1.7 %constant_dynamic-slice_fusion.8 = (bf16[2048,128]{1,0:T(8,128)(2,1)S(1)}, bf16[2048,128]{1,0:T(8,128)(2,1)S(1)}, bf16[2048,128]{1,0:T(8,128)(2,1)S(1)}, bf16[2048,128]{1,0:T(8,128)(2,1)S(1)}) fusion(bf16[8192,128]{1,0:T(8,128)(2,1)} %param.11, s32[]{:T(128)S(6)} %select_n.65, s32[]{:T(128)S(6)} %select_n.64, bf16[8192,128]{1,0:T(8,128)(2,1)} %param.10), kind=kLoop, calls=%fused_computation.20 | loop fusion | bytes 4194312 | tf_op jit(solution)/shard_map/dynamic_slice | solution.py:271
  12.0 1.8 %fusion = (f32[512,64]{1,0:T(8,128)S(1)}, f32[512,64]{1,0:T(8,128)S(1)}, f32[512,64]{1,0:T(8,128)}) fusion(f32[64]{0:T(128)S(1)} %multiply_power_fusion, f32[512]{0:T(512)S(1)} %add_convert_fusion), kind=kLoop, calls=%fused_computation.10 | loop fusion | flops 65536 | bytes 395520 | tf_op jit(solution)/shard_map/neg | solution.py:335
  14.6 1.2 %pad_maximum_fusion.6 = (f32[512,128]{1,0:T(8,128)S(1)}, f32[512,128]{1,0:T(8,128)S(1)}) fusion(f32[512,64]{1,0:T(8,128)} %get-tuple-element.40, f32[512,64]{1,0:T(8,128)S(1)} %get-tuple-element.39, f32[512,64]{1,0:T(8,128)S(1)} %get-tuple-element.38), kind=kLoop, calls=%fused_computation.8 | loop fusion | flops 131072 | bytes 917504 | tf_op jit(solution)/shard_map/concatenate | solution.py:334
  15.8 1.6 %collective-permute-start.3 = (bf16[512,256]{1,0:T(8,128)(2,1)S(1)}, bf16[512,256]{1,0:T(8,128)(2,1)S(1)}, u32[]{:S(2)}, u32[]{:S(2)}) collective-permute-start(bf16[512,256]{1,0:T(8,128)(2,1)S(1)} %collective-permute-done.1.a0), channel_id=1, source_target_pairs={{0,4},{4,0},{8,12},{12,8},{16,20},{20,16},{24,28},{28,24},{1,5},{5... | collective-permute-start | bytes 786440 | tf_op jit(solution)/shard_map/ppermute | solution.py:289
  17.4 1.6 %collective-permute-start.4 = (bf16[512,256]{1,0:T(8,128)(2,1)S(1)}, bf16[512,256]{1,0:T(8,128)(2,1)S(1)}, u32[]{:S(2)}, u32[]{:S(2)}) collective-permute-start(bf16[512,256]{1,0:T(8,128)(2,1)S(1)} %collective-permute-done.1.a0), channel_id=1, source_target_pairs={{0,8},{4,12},{8,0},{12,4},{16,24},{20,28},{24,16},{28,20},{1,9},{5... | collective-permute-start | bytes 786440 | tf_op jit(solution)/shard_map/ppermute | solution.py:289
  19.6 2.0 %collective-permute-start.8 = (bf16[512,256]{1,0:T(8,128)(2,1)}, bf16[512,256]{1,0:T(8,128)(2,1)S(1)}, u32[]{:S(2)}, u32[]{:S(2)}) collective-permute-start(bf16[512,256]{1,0:T(8,128)(2,1)} %pad_maximum_fusion.5), channel_id=1, source_target_pairs={{0,2},{1,3},{2,0},{3,1},{4,6},{5,7},{6,4},{7,5},{8,10},{9,11},{10,... | collective-permute-start | bytes 786440 | tf_op jit(solution)/shard_map/ppermute | solution.py:277
  21.6 3.6 %collective-permute-done.5.a3 = bf16[512,256]{1,0:T(8,128)(2,1)S(1)} collective-permute-done((bf16[512,256]{1,0:T(8,128)(2,1)}, bf16[512,256]{1,0:T(8,128)(2,1)S(1)}, u32[]{:S(2)}, u32[]{:S(2)}) %collective-permute-start.5) | collective-permute-done | bytes 262176 | tf_op jit(solution)/shard_map/ppermute | solution.py:277
  25.2 2.1 %collective-permute-start.6 = (bf16[512,256]{1,0:T(8,128)(2,1)S(1)}, bf16[512,256]{1,0:T(8,128)(2,1)S(1)}, u32[]{:S(2)}, u32[]{:S(2)}) collective-permute-start(bf16[512,256]{1,0:T(8,128)(2,1)S(1)} %collective-permute-done.2.b0), channel_id=1, source_target_pairs={{0,4},{4,0},{8,12},{12,8},{16,20},{20,16},{24,28},{28,24},{1,5},{5... | collective-permute-start | bytes 786440 | tf_op jit(solution)/shard_map/ppermute | solution.py:289
  27.2 1.6 %collective-permute-start.7 = (bf16[512,256]{1,0:T(8,128)(2,1)S(1)}, bf16[512,256]{1,0:T(8,128)(2,1)S(1)}, u32[]{:S(2)}, u32[]{:S(2)}) collective-permute-start(bf16[512,256]{1,0:T(8,128)(2,1)S(1)} %collective-permute-done.2.b0), channel_id=1, source_target_pairs={{0,8},{4,12},{8,0},{12,4},{16,24},{20,28},{24,16},{28,20},{1,9},{5... | collective-permute-start | bytes 786440 | tf_op jit(solution)/shard_map/ppermute | solution.py:289
  28.8 1.6 %copy-done.1 = bf16[512,2048]{1,0:T(8,128)(2,1)S(1)} copy-done((bf16[512,2048]{1,0:T(8,128)(2,1)S(1)}, bf16[512,2048]{1,0:T(8,128)(2,1)}, u32[]{:S(2)}) %copy-start.1) | copy-done | bytes 2097176
  31.6 2.8 %shard_map.96 = (bf16[512,2048]{1,0:T(8,128)(2,1)S(1)}, f32[8,128]{1,0:T(8,128)S(1)}, f32[512,256]{1,0:T(8,128)S(1)}) custom-call(s32[1]{0:T(128)} %bitcast.2.at, bf16[512,2048]{1,0:T(8,128)(2,1)} %collective-permute-done.hid, f32[64,128]{1,0:T(8,128)S(1)} %bitcast.16, bf16[2048,256]{1,0:T(8,128)(2,1)S(1)} %pad_maximum_fusion.weights, ...), custom_call_target="tpu_custom_call" | custom-call | flops 1073741824 | bytes 1048576 | tf_op jit(solution)/shard_map/pallas_call | solution.py:301
  37.7 1.6 %collective-permute-start.9 = (bf16[512,128]{1,0:T(8,128)(2,1)S(1)}, bf16[512,128]{1,0:T(8,128)(2,1)S(1)}, u32[]{:S(2)}, u32[]{:S(2)}) collective-permute-start(bf16[512,128]{1,0:T(8,128)(2,1)S(1)} %get-tuple-element.19), channel_id=1, source_target_pairs={{0,2},{1,3},{2,0},{3,1},{4,6},{5,7},{6,4},{7,5},{8,10},{9,11},{10,... | collective-permute-start | bytes 393224 | tf_op jit(solution)/shard_map/ppermute | solution.py:326
  41.1 1.6 %collective-permute-start.11 = (bf16[512,128]{1,0:T(8,128)(2,1)S(1)}, bf16[512,128]{1,0:T(8,128)(2,1)S(1)}, u32[]{:S(2)}, u32[]{:S(2)}) collective-permute-start(bf16[512,128]{1,0:T(8,128)(2,1)S(1)} %get-tuple-element.23), channel_id=1, source_target_pairs={{0,2},{1,3},{2,0},{3,1},{4,6},{5,7},{6,4},{7,5},{8,10},{9,11},{10,... | collective-permute-start | bytes 393224 | tf_op jit(solution)/shard_map/ppermute | solution.py:327
  42.6 1.2 %collective-permute-done.10.refs_3_ = f32[8,128]{1,0:T(8,128)S(1)} collective-permute-done((f32[8,128]{1,0:T(8,128)S(1)}, f32[8,128]{1,0:T(8,128)S(1)}, u32[]{:S(2)}, u32[]{:S(2)}) %collective-permute-start.10) | collective-permute-done | bytes 4128 | tf_op jit(solution)/shard_map/ppermute | solution.py:310
  43.9 1.8 %shard_map.100 = (f32[512,512]{1,0:T(8,128)S(1)}, f32[8,2,512]{2,1,0:T(2,128)}) custom-call(s32[1]{0:T(128)} %bitcast.1.first, f32[512,256]{1,0:T(8,128)S(1)} %get-tuple-element.16.refs_0_, bf16[512,128]{1,0:T(8,128)(2,1)S(1)} %collective-permute-done.9.refs_1_, f32[8,128]{1,0:T(8,128)S(1)} %get-tuple-element.20.refs_2_, ...), custom_call_target="tpu_custom_call" | custom-call | flops 268435456 | bytes 1048576 | tf_op jit(solution)/shard_map/pallas_call | solution.py:342
  45.7 3.9 %all-to-all-start = ((f32[8,2,512]{2,1,0:T(2,128)}), f32[8,2,512]{2,1,0:T(2,128)S(1)}, u32[]{:S(2)}, u32[]{:S(2)}) async-start(f32[8,2,512]{2,1,0:T(2,128)} %get-tuple-element.21.mine), calls=%async_computation | async-start | bytes 65536 | tf_op jit(solution)/shard_map/all_to_all | solution.py:349
  50.4 5.8 %all-to-all-done.got = f32[8,2,512]{2,1,0:T(2,128)S(1)} async-done(((f32[8,2,512]{2,1,0:T(2,128)}), f32[8,2,512]{2,1,0:T(2,128)S(1)}, u32[]{:S(2)}, u32[]{:S(2)}) %all-to-all-start) | async-done | bytes 32800 | tf_op jit(solution)/shard_map/all_to_all | solution.py:349
  56.2 1.8 %shard_map.102 = f32[8,128]{1,0:T(8,128)} custom-call(s32[2]{0:T(128)S(1)} %pad_add_fusion.1.sizes, f32[8,2,512]{2,1,0:T(2,128)S(1)} %all-to-all-done.got, f32[8,2,512]{2,1,0:T(2,128)} %get-tuple-element.21.mine, f32[512,512]{1,0:T(8,128)S(1)} %get-tuple-element.22.expo, f32[8,128]{1,0:T(8,128)S(1)} %shard_map.101.vmag, s32[1,512]{1,0:T(1,128)S(1)} %and_select_fusion.win), custom_call_target="tpu_custom_call" | custom-call | flops 67108864 | bytes 1048576 | tf_op jit(solution)/shard_map/pallas_call | solution.py:357
  58.0 3.3 %all-to-all-start.1 = ((f32[8,1,128]{2,1,0:T(1,128)}), f32[8,1,128]{2,1,0:T(1,128)S(1)}, u32[]{:S(2)}, u32[]{:S(2)}) async-start(f32[8,1,128]{2,1,0:T(1,128)} %bitcast.10), calls=%async_computation.1 | async-start | bytes 8192 | tf_op jit(solution)/shard_map/all_to_all | solution.py:363
  61.4 6.4 %all-to-all-done.1 = f32[8,1,128]{2,1,0:T(1,128)S(1)} async-done(((f32[8,1,128]{2,1,0:T(1,128)}), f32[8,1,128]{2,1,0:T(1,128)S(1)}, u32[]{:S(2)}, u32[]{:S(2)}) %all-to-all-start.1) | async-done | bytes 4128 | tf_op jit(solution)/shard_map/all_to_all | solution.py:363
  67.8 1.5 %shard_map.103 = (f32[1,4]{1,0:T(1,128)}, f32[1,1]{1,0:T(1,128)}) custom-call(s32[3]{0:T(128)S(1)} %pad_add_fusion.sizes, f32[8,128]{1,0:T(8,128)S(1)} %bitcast.14), custom_call_target="tpu_custom_call" | custom-call | flops 1048576 | bytes 1048576 | tf_op jit(solution)/shard_map/pallas_call | solution.py:364
  (40 shorter events, 9.7 us)
Async XLA Ops:
  0.6 26.6 %collective-permute-start = (bf16[512,2048]{1,0:T(8,128)(2,1)}, bf16[512,2048]{1,0:T(8,128)(2,1)}, u32[]{:S(2)}, u32[]{:S(2)}) collective-permute-start(bf16[512,2048]{1,0:T(8,128)(2,1)} %hid.1), channel_id=1, source_target_pairs={{0,1},{1,0},{2,3},{3,2},{4,5},{5,4},{6,7},{7,6},{8,9},{9,8},{10,11... | collective-permute-start | bytes 6291464 | tf_op jit(solution)/shard_map/ppermute | solution.py:285
  4.0 11.8 %collective-permute-start.1 = (bf16[512,256]{1,0:T(8,128)(2,1)}, bf16[512,256]{1,0:T(8,128)(2,1)S(1)}, u32[]{:S(2)}, u32[]{:S(2)}) collective-permute-start(bf16[512,256]{1,0:T(8,128)(2,1)} %pad_maximum_fusion.2), channel_id=1, source_target_pairs={{0,2},{1,3},{2,0},{3,1},{4,6},{5,7},{6,4},{7,5},{8,10},{9,11},{10,... | collective-permute-start | bytes 786440 | tf_op jit(solution)/shard_map/ppermute | solution.py:277
  7.3 12.3 %collective-permute-start.2 = (bf16[512,256]{1,0:T(8,128)(2,1)}, bf16[512,256]{1,0:T(8,128)(2,1)S(1)}, u32[]{:S(2)}, u32[]{:S(2)}) collective-permute-start(bf16[512,256]{1,0:T(8,128)(2,1)} %pad_maximum_fusion.3), channel_id=1, source_target_pairs={{0,2},{1,3},{2,0},{3,1},{4,6},{5,7},{6,4},{7,5},{8,10},{9,11},{10,... | collective-permute-start | bytes 786440 | tf_op jit(solution)/shard_map/ppermute | solution.py:277
  8.0 17.1 %collective-permute-start.5 = (bf16[512,256]{1,0:T(8,128)(2,1)}, bf16[512,256]{1,0:T(8,128)(2,1)S(1)}, u32[]{:S(2)}, u32[]{:S(2)}) collective-permute-start(bf16[512,256]{1,0:T(8,128)(2,1)} %pad_maximum_fusion.4), channel_id=1, source_target_pairs={{0,2},{1,3},{2,0},{3,1},{4,6},{5,7},{6,4},{7,5},{8,10},{9,11},{10,... | collective-permute-start | bytes 786440 | tf_op jit(solution)/shard_map/ppermute | solution.py:277
  11.7 2.1 %copy-start.3 = (bf16[512,128]{1,0:T(8,128)(2,1)S(1)}, bf16[512,128]{1,0:T(8,128)(2,1)}, u32[]{:S(2)}) copy-start(bf16[512,128]{1,0:T(8,128)(2,1)} %get-tuple-element.30) | copy-start | bytes 393220
  11.7 2.1 %copy-start.4 = (bf16[512,128]{1,0:T(8,128)(2,1)S(1)}, bf16[512,128]{1,0:T(8,128)(2,1)}, u32[]{:S(2)}) copy-start(bf16[512,128]{1,0:T(8,128)(2,1)} %get-tuple-element.46) | copy-start | bytes 393220
  11.9 16.9 %copy-start.2 = (f32[8192]{0:T(1024)S(1)}, f32[8192]{0:T(1024)}, u32[]{:S(2)}) copy-start(f32[8192]{0:T(1024)} %param.9) | copy-start | bytes 98308
  15.8 19.5 %collective-permute-start.3 = (bf16[512,256]{1,0:T(8,128)(2,1)S(1)}, bf16[512,256]{1,0:T(8,128)(2,1)S(1)}, u32[]{:S(2)}, u32[]{:S(2)}) collective-permute-start(bf16[512,256]{1,0:T(8,128)(2,1)S(1)} %collective-permute-done.1.a0), channel_id=1, source_target_pairs={{0,4},{4,0},{8,12},{12,8},{16,20},{20,16},{24,28},{28,24},{1,5},{5... | collective-permute-start | bytes 786440 | tf_op jit(solution)/shard_map/ppermute | solution.py:289
  17.4 18.0 %collective-permute-start.4 = (bf16[512,256]{1,0:T(8,128)(2,1)S(1)}, bf16[512,256]{1,0:T(8,128)(2,1)S(1)}, u32[]{:S(2)}, u32[]{:S(2)}) collective-permute-start(bf16[512,256]{1,0:T(8,128)(2,1)S(1)} %collective-permute-done.1.a0), channel_id=1, source_target_pairs={{0,8},{4,12},{8,0},{12,4},{16,24},{20,28},{24,16},{28,20},{1,9},{5... | collective-permute-start | bytes 786440 | tf_op jit(solution)/shard_map/ppermute | solution.py:289
  19.6 17.0 %collective-permute-start.8 = (bf16[512,256]{1,0:T(8,128)(2,1)}, bf16[512,256]{1,0:T(8,128)(2,1)S(1)}, u32[]{:S(2)}, u32[]{:S(2)}) collective-permute-start(bf16[512,256]{1,0:T(8,128)(2,1)} %pad_maximum_fusion.5), channel_id=1, source_target_pairs={{0,2},{1,3},{2,0},{3,1},{4,6},{5,7},{6,4},{7,5},{8,10},{9,11},{10,... | collective-permute-start | bytes 786440 | tf_op jit(solution)/shard_map/ppermute | solution.py:277
  25.2 11.3 %collective-permute-start.6 = (bf16[512,256]{1,0:T(8,128)(2,1)S(1)}, bf16[512,256]{1,0:T(8,128)(2,1)S(1)}, u32[]{:S(2)}, u32[]{:S(2)}) collective-permute-start(bf16[512,256]{1,0:T(8,128)(2,1)S(1)} %collective-permute-done.2.b0), channel_id=1, source_target_pairs={{0,4},{4,0},{8,12},{12,8},{16,20},{20,16},{24,28},{28,24},{1,5},{5... | collective-permute-start | bytes 786440 | tf_op jit(solution)/shard_map/ppermute | solution.py:289
  27.2 9.3 %collective-permute-start.7 = (bf16[512,256]{1,0:T(8,128)(2,1)S(1)}, bf16[512,256]{1,0:T(8,128)(2,1)S(1)}, u32[]{:S(2)}, u32[]{:S(2)}) collective-permute-start(bf16[512,256]{1,0:T(8,128)(2,1)S(1)} %collective-permute-done.2.b0), channel_id=1, source_target_pairs={{0,8},{4,12},{8,0},{12,4},{16,24},{20,28},{24,16},{28,20},{1,9},{5... | collective-permute-start | bytes 786440 | tf_op jit(solution)/shard_map/ppermute | solution.py:289
  28.8 1.6 %copy-start.1 = (bf16[512,2048]{1,0:T(8,128)(2,1)S(1)}, bf16[512,2048]{1,0:T(8,128)(2,1)}, u32[]{:S(2)}) copy-start(bf16[512,2048]{1,0:T(8,128)(2,1)} %hid.1) | copy-start | bytes 6291460
  36.5 7.4 %copy-start = (bf16[64,1024]{1,0:T(8,128)(2,1)S(1)}, bf16[64,1024]{1,0:T(8,128)(2,1)}, u32[]{:S(2)}) copy-start(bf16[64,1024]{1,0:T(8,128)(2,1)} %refs_6_.1) | copy-start | bytes 393220
  37.7 6.2 %collective-permute-start.9 = (bf16[512,128]{1,0:T(8,128)(2,1)S(1)}, bf16[512,128]{1,0:T(8,128)(2,1)S(1)}, u32[]{:S(2)}, u32[]{:S(2)}) collective-permute-start(bf16[512,128]{1,0:T(8,128)(2,1)S(1)} %get-tuple-element.19), channel_id=1, source_target_pairs={{0,2},{1,3},{2,0},{3,1},{4,6},{5,7},{6,4},{7,5},{8,10},{9,11},{10,... | collective-permute-start | bytes 393224 | tf_op jit(solution)/shard_map/ppermute | solution.py:326
  39.2 4.6 %collective-permute-start.10 = (f32[8,128]{1,0:T(8,128)S(1)}, f32[8,128]{1,0:T(8,128)S(1)}, u32[]{:S(2)}, u32[]{:S(2)}) collective-permute-start(f32[8,128]{1,0:T(8,128)S(1)} %get-tuple-element.20.refs_2_), channel_id=1, source_target_pairs={{0,2},{1,3},{2,0},{3,1},{4,6},{5,7},{6,4},{7,5},{8,10},{9,11},{10,... | collective-permute-start | bytes 12296 | tf_op jit(solution)/shard_map/ppermute | solution.py:310
  41.1 9.2 %collective-permute-start.11 = (bf16[512,128]{1,0:T(8,128)(2,1)S(1)}, bf16[512,128]{1,0:T(8,128)(2,1)S(1)}, u32[]{:S(2)}, u32[]{:S(2)}) collective-permute-start(bf16[512,128]{1,0:T(8,128)(2,1)S(1)} %get-tuple-element.23), channel_id=1, source_target_pairs={{0,2},{1,3},{2,0},{3,1},{4,6},{5,7},{6,4},{7,5},{8,10},{9,11},{10,... | collective-permute-start | bytes 393224 | tf_op jit(solution)/shard_map/ppermute | solution.py:327
  45.7 10.6 %all-to-all-start = ((f32[8,2,512]{2,1,0:T(2,128)}), f32[8,2,512]{2,1,0:T(2,128)S(1)}, u32[]{:S(2)}, u32[]{:S(2)}) async-start(f32[8,2,512]{2,1,0:T(2,128)} %get-tuple-element.21.mine), calls=%async_computation | async-start | bytes 65536 | tf_op jit(solution)/shard_map/all_to_all | solution.py:349
  58.0 9.8 %all-to-all-start.1 = ((f32[8,1,128]{2,1,0:T(1,128)}), f32[8,1,128]{2,1,0:T(1,128)S(1)}, u32[]{:S(2)}, u32[]{:S(2)}) async-start(f32[8,1,128]{2,1,0:T(1,128)} %bitcast.10), calls=%async_computation.1 | async-start | bytes 8192 | tf_op jit(solution)/shard_map/all_to_all | solution.py:363

commit v5 on v4

--- a/solution.py
+++ b/solution.py
@@ -266,10 +266,14 @@
     def flip(bit):
         return [(j, j ^ bit) for j in range(n_seq)]
 
+    weights = [key_matrix, value_matrix]
+
     def rows_at(start, count):
-        return jnp.concatenate(
-            [lax.dynamic_slice_in_dim(m, start, count) for m in (key_matrix, value_matrix)], axis=1
+        rows = jnp.concatenate(
+            [lax.dynamic_slice_in_dim(m, start, count) for m in weights], axis=1
         )
+        weights[0], weights[1], rows = lax.optimization_barrier((*weights, rows))
+        return rows
 
     def cross(o, block):
         chip = (x - o) % n_x
@@ -297,13 +301,13 @@
     gain_lines = gain.reshape(full_width // LANES, LANES)
 
     def norm(start, rows, more):
-        weights = rows_at(start, feats)
+        own = rows_at(start, feats)
         return call(
             norm_kernel,
             [sds((tok, feats), BF16), sds((lines, LANES), F32), sds((tok, 2 * head), F32)],
             [SMEM] + [VMEM] * (3 + len(more)),
             flops=1 << 30,
-        )(start.reshape(1), rows, gain_lines, weights, *more)
+        )(start.reshape(1), rows, gain_lines, own, *more)
 
     mine, sumsq, acc = norm(h * feats, hidden, ())
     other, sumsq, acc = norm((h ^ 1) * feats, swapped, (sumsq, acc))

time: 69.8 us -> 72.1 us (1.033)
  local copies, waits for them, and re-layouts: 5.35 us -> 12.4 us
  waiting for transfers between devices: 17.5 us -> 13.4 us
  starting transfers between devices: 24.8 us -> 23.9 us
    dynamic_slice x2 -> x11, local copies, waits for them, and re-layouts: 3.74 us -> 10.8 us  [rows_at(): lax.dynamic_slice_in_dim(m, start, count)]
    ppermute x4, waiting for transfers between devices: 4.11 us -> 0.01 us  [cross(): lax.ppermute(rows_at((chip * CORES + (c ^ part)) * feats + block * q, q),...]
    ppermute x4, starting transfers between devices: 6.62 us -> 5.13 us  [cross(): lax.ppermute(rows_at((chip * CORES + (c ^ part)) * feats + block * q, q),...]
    unnamed x10 -> x6, local copies, waits for them, and re-layouts: 1.61 us -> 1.6 us
  transfers between devices with their start and end apart: 14 -> 14, of which waited for: 5 -> 3; matrix products, arithmetic and copies ran while one was open for 15% -> 24% of each run, Pallas kernels for 12% -> 11%
where the time goes in v5:
time: 72.1 us; the launch traced here: 71.4 us
  starting transfers between devices  23.9 us (33%)
  waiting for transfers between devices  13.4 us (19%)
  Pallas kernels  12.5 us (17%)
  local copies, waits for them, and re-layouts  12.4 us (17%)
  other arithmetic  6.43 us (9%)
  between operations  2.79 us (4%)
    dynamic_slice x11, local copies, waits for them, and re-layouts, rows_at(): lax.dynamic_slice_in_dim(m, start, count)  10.8 us
    ppermute x4, starting transfers between devices, local(): lax.ppermute(firsts[o - 1][part], 'seq', flip(bit))  6.77 us
    all_to_all x1, waiting for transfers between devices, local(): said = lax.all_to_all(spread, 'seq', 0, 0, tiled=True)  6.35 us
    all_to_all x1, waiting for transfers between devices, local(): got = lax.all_to_all(stats, 'seq', 0, 0, tiled=True)  5.78 us
    ppermute x4, starting transfers between devices, cross(): lax.ppermute(rows_at((chip * CORES + (c ^ part)) * feats + block * q, q),...  5.13 us
    all_to_all x1, starting transfers between devices, local(): got = lax.all_to_all(stats, 'seq', 0, 0, tiled=True)  4.45 us
    pallas_call x2, Pallas kernels, norm(): call(norm_kernel, [sds((tok, feats), BF16), sds((lines, LANES), F32), sds...  3.95 us
    all_to_all x1, starting transfers between devices, local(): said = lax.all_to_all(spread, 'seq', 0, 0, tiled=True)  3.33 us
  transfers between devices with their start and end apart: 14, of which 3 were waited for; matrix products, arithmetic and copies ran while one was open for 24% of the time, Pallas kernels for 11%

profile of v5, /device:TPU:0, one launch (start us, length us, event | category | flops | bytes accessed | tf_op | source)
XLA Modules:
  0.0 71.4 jit_solution(11697456012047952944)
XLA Ops:
  5.5 2.6 %collective-permute-start.2 = (bf16[512,256]{1,0:T(8,128)(2,1)}, bf16[512,256]{1,0:T(8,128)(2,1)S(1)}, u32[]{:S(2)}, u32[]{:S(2)}) collective-permute-start(bf16[512,256]{1,0:T(8,128)(2,1)} %pad_maximum_fusion.3), channel_id=1, source_target_pairs={{0,2},{1,3},{2,0},{3,1},{4,6},{5,7},{6,4},{7,5},{8,10},{9,11},{10,... | collective-permute-start | bytes 786440 | tf_op jit(solution)/shard_map/ppermute | solution.py:281
  10.6 2.0 %collective-permute-start.5 = (bf16[512,256]{1,0:T(8,128)(2,1)}, bf16[512,256]{1,0:T(8,128)(2,1)S(1)}, u32[]{:S(2)}, u32[]{:S(2)}) collective-permute-start(bf16[512,256]{1,0:T(8,128)(2,1)} %pad_maximum_fusion.4), channel_id=1, source_target_pairs={{0,2},{1,3},{2,0},{3,1},{4,6},{5,7},{6,4},{7,5},{8,10},{9,11},{10,... | collective-permute-start | bytes 786440 | tf_op jit(solution)/shard_map/ppermute | solution.py:281
  16.3 1.1 %constant_dynamic-slice_fusion.2 = bf16[2048,128]{1,0:T(8,128)(2,1)S(1)} fusion(bf16[8192,128]{1,0:T(8,128)(2,1)} %param.11, s32[]{:T(128)S(6)} %select_n.72), kind=kLoop, calls=%fused_computation.14 | loop fusion | bytes 1048580 | tf_op jit(solution)/shard_map/dynamic_slice | solution.py:273
  19.8 1.8 %fusion = (f32[512,64]{1,0:T(8,128)S(1)}, f32[512,64]{1,0:T(8,128)S(1)}, f32[512,64]{1,0:T(8,128)}) fusion(f32[64]{0:T(128)S(1)} %multiply_power_fusion, f32[512]{0:T(512)S(1)} %add_convert_fusion), kind=kLoop, calls=%fused_computation.10 | loop fusion | flops 65536 | bytes 395520 | tf_op jit(solution)/shard_map/neg | solution.py:339
  21.6 1.2 %pad_maximum_fusion.6 = (f32[512,128]{1,0:T(8,128)S(1)}, f32[512,128]{1,0:T(8,128)S(1)}) fusion(f32[512,64]{1,0:T(8,128)} %get-tuple-element.60, f32[512,64]{1,0:T(8,128)S(1)} %get-tuple-element.59, f32[512,64]{1,0:T(8,128)S(1)} %get-tuple-element.58), kind=kLoop, calls=%fused_computation.8 | loop fusion | flops 131072 | bytes 917504 | tf_op jit(solution)/shard_map/concatenate | solution.py:338
  22.9 1.6 %collective-permute-start.3 = (bf16[512,256]{1,0:T(8,128)(2,1)S(1)}, bf16[512,256]{1,0:T(8,128)(2,1)S(1)}, u32[]{:S(2)}, u32[]{:S(2)}) collective-permute-start(bf16[512,256]{1,0:T(8,128)(2,1)S(1)} %collective-permute-done.1.a0), channel_id=1, source_target_pairs={{0,4},{4,0},{8,12},{12,8},{16,20},{20,16},{24,28},{28,24},{1,5},{5... | collective-permute-start | bytes 786440 | tf_op jit(solution)/shard_map/ppermute | solution.py:293
  24.4 1.6 %collective-permute-start.4 = (bf16[512,256]{1,0:T(8,128)(2,1)S(1)}, bf16[512,256]{1,0:T(8,128)(2,1)S(1)}, u32[]{:S(2)}, u32[]{:S(2)}) collective-permute-start(bf16[512,256]{1,0:T(8,128)(2,1)S(1)} %collective-permute-done.1.a0), channel_id=1, source_target_pairs={{0,8},{4,12},{8,0},{12,4},{16,24},{20,28},{24,16},{28,20},{1,9},{5... | collective-permute-start | bytes 786440 | tf_op jit(solution)/shard_map/ppermute | solution.py:293
  26.7 1.5 %collective-permute-start.6 = (bf16[512,256]{1,0:T(8,128)(2,1)S(1)}, bf16[512,256]{1,0:T(8,128)(2,1)S(1)}, u32[]{:S(2)}, u32[]{:S(2)}) collective-permute-start(bf16[512,256]{1,0:T(8,128)(2,1)S(1)} %collective-permute-done.2.b0), channel_id=1, source_target_pairs={{0,4},{4,0},{8,12},{12,8},{16,20},{20,16},{24,28},{28,24},{1,5},{5... | collective-permute-start | bytes 786440 | tf_op jit(solution)/shard_map/ppermute | solution.py:293
  28.1 2.1 %collective-permute-start.7 = (bf16[512,256]{1,0:T(8,128)(2,1)S(1)}, bf16[512,256]{1,0:T(8,128)(2,1)S(1)}, u32[]{:S(2)}, u32[]{:S(2)}) collective-permute-start(bf16[512,256]{1,0:T(8,128)(2,1)S(1)} %collective-permute-done.2.b0), channel_id=1, source_target_pairs={{0,8},{4,12},{8,0},{12,4},{16,24},{20,28},{24,16},{28,20},{1,9},{5... | collective-permute-start | bytes 786440 | tf_op jit(solution)/shard_map/ppermute | solution.py:293
  30.3 1.6 %copy-done.1 = bf16[512,2048]{1,0:T(8,128)(2,1)S(1)} copy-done((bf16[512,2048]{1,0:T(8,128)(2,1)S(1)}, bf16[512,2048]{1,0:T(8,128)(2,1)}, u32[]{:S(2)}) %copy-start.1) | copy-done | bytes 2097176
  31.9 1.2 %shard_map.95 = (bf16[512,2048]{1,0:T(8,128)(2,1)S(1)}, f32[8,128]{1,0:T(8,128)S(1)}, f32[512,256]{1,0:T(8,128)S(1)}) custom-call(s32[1]{0:T(128)} %bitcast.4.at, bf16[512,2048]{1,0:T(8,128)(2,1)S(1)} %copy-done.1, f32[64,128]{1,0:T(8,128)S(1)} %bitcast.15, bf16[2048,256]{1,0:T(8,128)(2,1)S(1)} %pad_maximum_fusion.weights), custom_call_target="tpu_custom_call" | custom-call | flops 1073741824 | bytes 1048576 | tf_op jit(solution)/shard_map/pallas_call | solution.py:305
  33.1 2.8 %shard_map.96 = (bf16[512,2048]{1,0:T(8,128)(2,1)S(1)}, f32[8,128]{1,0:T(8,128)S(1)}, f32[512,256]{1,0:T(8,128)S(1)}) custom-call(s32[1]{0:T(128)} %bitcast.2.at, bf16[512,2048]{1,0:T(8,128)(2,1)} %collective-permute-done.hid, f32[64,128]{1,0:T(8,128)S(1)} %bitcast.16, bf16[2048,256]{1,0:T(8,128)(2,1)S(1)} %pad_maximum_fusion.1.weights, ...), custom_call_target="tpu_custom_call" | custom-call | flops 1073741824 | bytes 1048576 | tf_op jit(solution)/shard_map/pallas_call | solution.py:305
  36.8 1.1 %shard_map.98.total = f32[512,256]{1,0:T(8,128)S(1)} custom-call(s32[4]{0:T(128)S(1)} %pad_add_fusion.2.at, bf16[512,2048]{1,0:T(8,128)(2,1)S(1)} %get-tuple-element.46.mine, f32[512,256]{1,0:T(8,128)S(1)} %shard_map.97.total, bf16[512,256]{1,0:T(8,128)(2,1)S(1)} %collective-permute-done.3.a1, bf16[512,256]{1,0:T(8,128)(2,1)S(1)} %collective-permute-done.4.a2, ...), custom_call_target="tpu_custom_call" | custom-call | flops 536870912 | bytes 1048576 | tf_op jit(solution)/shard_map/pallas_call | solution.py:324
  38.0 1.1 %shard_map.99 = (bf16[512,128]{1,0:T(8,128)(2,1)S(1)}, bf16[512,128]{1,0:T(8,128)(2,1)S(1)}) custom-call(s32[4]{0:T(128)S(1)} %pad_add_fusion.2.at, bf16[512,2048]{1,0:T(8,128)(2,1)S(1)} %get-tuple-element.45.other, f32[512,256]{1,0:T(8,128)S(1)} %shard_map.98.total, bf16[512,256]{1,0:T(8,128)(2,1)S(1)} %collective-permute-done.6.b1, ...), custom_call_target="tpu_custom_call" | custom-call | flops 536870912 | bytes 1048576 | tf_op jit(solution)/shard_map/pallas_call | solution.py:327
  39.1 1.6 %collective-permute-start.9 = (bf16[512,128]{1,0:T(8,128)(2,1)S(1)}, bf16[512,128]{1,0:T(8,128)(2,1)S(1)}, u32[]{:S(2)}, u32[]{:S(2)}) collective-permute-start(bf16[512,128]{1,0:T(8,128)(2,1)S(1)} %get-tuple-element.51), channel_id=1, source_target_pairs={{0,2},{1,3},{2,0},{3,1},{4,6},{5,7},{6,4},{7,5},{8,10},{9,11},{10,... | collective-permute-start | bytes 393224 | tf_op jit(solution)/shard_map/ppermute | solution.py:330
  42.5 1.6 %collective-permute-start.11 = (bf16[512,128]{1,0:T(8,128)(2,1)S(1)}, bf16[512,128]{1,0:T(8,128)(2,1)S(1)}, u32[]{:S(2)}, u32[]{:S(2)}) collective-permute-start(bf16[512,128]{1,0:T(8,128)(2,1)S(1)} %get-tuple-element.55), channel_id=1, source_target_pairs={{0,2},{1,3},{2,0},{3,1},{4,6},{5,7},{6,4},{7,5},{8,10},{9,11},{10,... | collective-permute-start | bytes 393224 | tf_op jit(solution)/shard_map/ppermute | solution.py:331
  44.1 1.2 %collective-permute-done.10.refs_3_ = f32[8,128]{1,0:T(8,128)S(1)} collective-permute-done((f32[8,128]{1,0:T(8,128)S(1)}, f32[8,128]{1,0:T(8,128)S(1)}, u32[]{:S(2)}, u32[]{:S(2)}) %collective-permute-start.10) | collective-permute-done | bytes 4128 | tf_op jit(solution)/shard_map/ppermute | solution.py:314
  45.3 1.8 %shard_map.100 = (f32[512,512]{1,0:T(8,128)S(1)}, f32[8,2,512]{2,1,0:T(2,128)}) custom-call(s32[1]{0:T(128)} %bitcast.1.first, f32[512,256]{1,0:T(8,128)S(1)} %get-tuple-element.44.refs_0_, bf16[512,128]{1,0:T(8,128)(2,1)S(1)} %collective-permute-done.9.refs_1_, f32[8,128]{1,0:T(8,128)S(1)} %get-tuple-element.52.refs_2_, ...), custom_call_target="tpu_custom_call" | custom-call | flops 268435456 | bytes 1048576 | tf_op jit(solution)/shard_map/pallas_call | solution.py:346
  47.2 4.5 %all-to-all-start = ((f32[8,2,512]{2,1,0:T(2,128)}), f32[8,2,512]{2,1,0:T(2,128)S(1)}, u32[]{:S(2)}, u32[]{:S(2)}) async-start(f32[8,2,512]{2,1,0:T(2,128)} %get-tuple-element.53.mine), calls=%async_computation | async-start | bytes 65536 | tf_op jit(solution)/shard_map/all_to_all | solution.py:353
  52.5 5.8 %all-to-all-done.got = f32[8,2,512]{2,1,0:T(2,128)S(1)} async-done(((f32[8,2,512]{2,1,0:T(2,128)}), f32[8,2,512]{2,1,0:T(2,128)S(1)}, u32[]{:S(2)}, u32[]{:S(2)}) %all-to-all-start) | async-done | bytes 32800 | tf_op jit(solution)/shard_map/all_to_all | solution.py:353
  58.3 1.8 %shard_map.102 = f32[8,128]{1,0:T(8,128)} custom-call(s32[2]{0:T(128)S(1)} %pad_add_fusion.1.sizes, f32[8,2,512]{2,1,0:T(2,128)S(1)} %all-to-all-done.got, f32[8,2,512]{2,1,0:T(2,128)} %get-tuple-element.53.mine, f32[512,512]{1,0:T(8,128)S(1)} %get-tuple-element.54.expo, f32[8,128]{1,0:T(8,128)S(1)} %shard_map.101.vmag, s32[1,512]{1,0:T(1,128)S(1)} %and_select_fusion.win), custom_call_target="tpu_custom_call" | custom-call | flops 67108864 | bytes 1048576 | tf_op jit(solution)/shard_map/pallas_call | solution.py:361
  60.1 3.3 %all-to-all-start.1 = ((f32[8,1,128]{2,1,0:T(1,128)}), f32[8,1,128]{2,1,0:T(1,128)S(1)}, u32[]{:S(2)}, u32[]{:S(2)}) async-start(f32[8,1,128]{2,1,0:T(1,128)} %bitcast.10), calls=%async_computation.1 | async-start | bytes 8192 | tf_op jit(solution)/shard_map/all_to_all | solution.py:367
  63.5 6.4 %all-to-all-done.1 = f32[8,1,128]{2,1,0:T(1,128)S(1)} async-done(((f32[8,1,128]{2,1,0:T(1,128)}), f32[8,1,128]{2,1,0:T(1,128)S(1)}, u32[]{:S(2)}, u32[]{:S(2)}) %all-to-all-start.1) | async-done | bytes 4128 | tf_op jit(solution)/shard_map/all_to_all | solution.py:367
  69.8 1.5 %shard_map.103 = (f32[1,4]{1,0:T(1,128)}, f32[1,1]{1,0:T(1,128)}) custom-call(s32[3]{0:T(128)S(1)} %pad_add_fusion.sizes, f32[8,128]{1,0:T(8,128)S(1)} %bitcast.14), custom_call_target="tpu_custom_call" | custom-call | flops 1048576 | bytes 1048576 | tf_op jit(solution)/shard_map/pallas_call | solution.py:368
  (45 shorter events, 16.0 us)
Async XLA Ops:
  0.6 27.5 %collective-permute-start = (bf16[512,2048]{1,0:T(8,128)(2,1)}, bf16[512,2048]{1,0:T(8,128)(2,1)}, u32[]{:S(2)}, u32[]{:S(2)}) collective-permute-start(bf16[512,2048]{1,0:T(8,128)(2,1)} %hid.1), channel_id=1, source_target_pairs={{0,1},{1,0},{2,3},{3,2},{4,5},{5,4},{6,7},{7,6},{8,9},{9,8},{10,11... | collective-permute-start | bytes 6291464 | tf_op jit(solution)/shard_map/ppermute | solution.py:289
  5.5 20.6 %collective-permute-start.2 = (bf16[512,256]{1,0:T(8,128)(2,1)}, bf16[512,256]{1,0:T(8,128)(2,1)S(1)}, u32[]{:S(2)}, u32[]{:S(2)}) collective-permute-start(bf16[512,256]{1,0:T(8,128)(2,1)} %pad_maximum_fusion.3), channel_id=1, source_target_pairs={{0,2},{1,3},{2,0},{3,1},{4,6},{5,7},{6,4},{7,5},{8,10},{9,11},{10,... | collective-permute-start | bytes 786440 | tf_op jit(solution)/shard_map/ppermute | solution.py:281
  8.0 14.8 %collective-permute-start.1 = (bf16[512,256]{1,0:T(8,128)(2,1)}, bf16[512,256]{1,0:T(8,128)(2,1)S(1)}, u32[]{:S(2)}, u32[]{:S(2)}) collective-permute-start(bf16[512,256]{1,0:T(8,128)(2,1)} %pad_maximum_fusion.2), channel_id=1, source_target_pairs={{0,2},{1,3},{2,0},{3,1},{4,6},{5,7},{6,4},{7,5},{8,10},{9,11},{10,... | collective-permute-start | bytes 786440 | tf_op jit(solution)/shard_map/ppermute | solution.py:281
  10.6 16.0 %collective-permute-start.5 = (bf16[512,256]{1,0:T(8,128)(2,1)}, bf16[512,256]{1,0:T(8,128)(2,1)S(1)}, u32[]{:S(2)}, u32[]{:S(2)}) collective-permute-start(bf16[512,256]{1,0:T(8,128)(2,1)} %pad_maximum_fusion.4), channel_id=1, source_target_pairs={{0,2},{1,3},{2,0},{3,1},{4,6},{5,7},{6,4},{7,5},{8,10},{9,11},{10,... | collective-permute-start | bytes 786440 | tf_op jit(solution)/shard_map/ppermute | solution.py:281
  19.7 10.6 %copy-start.2 = (f32[8192]{0:T(1024)S(1)}, f32[8192]{0:T(1024)}, u32[]{:S(2)}) copy-start(f32[8192]{0:T(1024)} %param.9) | copy-start | bytes 98308
  22.9 14.0 %collective-permute-start.3 = (bf16[512,256]{1,0:T(8,128)(2,1)S(1)}, bf16[512,256]{1,0:T(8,128)(2,1)S(1)}, u32[]{:S(2)}, u32[]{:S(2)}) collective-permute-start(bf16[512,256]{1,0:T(8,128)(2,1)S(1)} %collective-permute-done.1.a0), channel_id=1, source_target_pairs={{0,4},{4,0},{8,12},{12,8},{16,20},{20,16},{24,28},{28,24},{1,5},{5... | collective-permute-start | bytes 786440 | tf_op jit(solution)/shard_map/ppermute | solution.py:293
  24.4 12.4 %collective-permute-start.4 = (bf16[512,256]{1,0:T(8,128)(2,1)S(1)}, bf16[512,256]{1,0:T(8,128)(2,1)S(1)}, u32[]{:S(2)}, u32[]{:S(2)}) collective-permute-start(bf16[512,256]{1,0:T(8,128)(2,1)S(1)} %collective-permute-done.1.a0), channel_id=1, source_target_pairs={{0,8},{4,12},{8,0},{12,4},{16,24},{20,28},{24,16},{28,20},{1,9},{5... | collective-permute-start | bytes 786440 | tf_op jit(solution)/shard_map/ppermute | solution.py:293
  26.1 11.9 %collective-permute-start.8 = (bf16[512,256]{1,0:T(8,128)(2,1)}, bf16[512,256]{1,0:T(8,128)(2,1)S(1)}, u32[]{:S(2)}, u32[]{:S(2)}) collective-permute-start(bf16[512,256]{1,0:T(8,128)(2,1)} %pad_maximum_fusion.5), channel_id=1, source_target_pairs={{0,2},{1,3},{2,0},{3,1},{4,6},{5,7},{6,4},{7,5},{8,10},{9,11},{10,... | collective-permute-start | bytes 786440 | tf_op jit(solution)/shard_map/ppermute | solution.py:281
  26.7 11.3 %collective-permute-start.6 = (bf16[512,256]{1,0:T(8,128)(2,1)S(1)}, bf16[512,256]{1,0:T(8,128)(2,1)S(1)}, u32[]{:S(2)}, u32[]{:S(2)}) collective-permute-start(bf16[512,256]{1,0:T(8,128)(2,1)S(1)} %collective-permute-done.2.b0), channel_id=1, source_target_pairs={{0,4},{4,0},{8,12},{12,8},{16,20},{20,16},{24,28},{28,24},{1,5},{5... | collective-permute-start | bytes 786440 | tf_op jit(solution)/shard_map/ppermute | solution.py:293
  28.1 9.9 %collective-permute-start.7 = (bf16[512,256]{1,0:T(8,128)(2,1)S(1)}, bf16[512,256]{1,0:T(8,128)(2,1)S(1)}, u32[]{:S(2)}, u32[]{:S(2)}) collective-permute-start(bf16[512,256]{1,0:T(8,128)(2,1)S(1)} %collective-permute-done.2.b0), channel_id=1, source_target_pairs={{0,8},{4,12},{8,0},{12,4},{16,24},{20,28},{24,16},{28,20},{1,9},{5... | collective-permute-start | bytes 786440 | tf_op jit(solution)/shard_map/ppermute | solution.py:293
  30.3 1.6 %copy-start.1 = (bf16[512,2048]{1,0:T(8,128)(2,1)S(1)}, bf16[512,2048]{1,0:T(8,128)(2,1)}, u32[]{:S(2)}) copy-start(bf16[512,2048]{1,0:T(8,128)(2,1)} %hid.1) | copy-start | bytes 6291460
  38.0 7.4 %copy-start = (bf16[64,1024]{1,0:T(8,128)(2,1)S(1)}, bf16[64,1024]{1,0:T(8,128)(2,1)}, u32[]{:S(2)}) copy-start(bf16[64,1024]{1,0:T(8,128)(2,1)} %refs_6_.1) | copy-start | bytes 393220
  39.1 6.2 %collective-permute-start.9 = (bf16[512,128]{1,0:T(8,128)(2,1)S(1)}, bf16[512,128]{1,0:T(8,128)(2,1)S(1)}, u32[]{:S(2)}, u32[]{:S(2)}) collective-permute-start(bf16[512,128]{1,0:T(8,128)(2,1)S(1)} %get-tuple-element.51), channel_id=1, source_target_pairs={{0,2},{1,3},{2,0},{3,1},{4,6},{5,7},{6,4},{7,5},{8,10},{9,11},{10,... | collective-permute-start | bytes 393224 | tf_op jit(solution)/shard_map/ppermute | solution.py:330
  40.7 4.6 %collective-permute-start.10 = (f32[8,128]{1,0:T(8,128)S(1)}, f32[8,128]{1,0:T(8,128)S(1)}, u32[]{:S(2)}, u32[]{:S(2)}) collective-permute-start(f32[8,128]{1,0:T(8,128)S(1)} %get-tuple-element.52.refs_2_), channel_id=1, source_target_pairs={{0,2},{1,3},{2,0},{3,1},{4,6},{5,7},{6,4},{7,5},{8,10},{9,11},{10,... | collective-permute-start | bytes 12296 | tf_op jit(solution)/shard_map/ppermute | solution.py:314
  42.5 9.8 %collective-permute-start.11 = (bf16[512,128]{1,0:T(8,128)(2,1)S(1)}, bf16[512,128]{1,0:T(8,128)(2,1)S(1)}, u32[]{:S(2)}, u32[]{:S(2)}) collective-permute-start(bf16[512,128]{1,0:T(8,128)(2,1)S(1)} %get-tuple-element.55), channel_id=1, source_target_pairs={{0,2},{1,3},{2,0},{3,1},{4,6},{5,7},{6,4},{7,5},{8,10},{9,11},{10,... | collective-permute-start | bytes 393224 | tf_op jit(solution)/shard_map/ppermute | solution.py:331
  47.2 11.1 %all-to-all-start = ((f32[8,2,512]{2,1,0:T(2,128)}), f32[8,2,512]{2,1,0:T(2,128)S(1)}, u32[]{:S(2)}, u32[]{:S(2)}) async-start(f32[8,2,512]{2,1,0:T(2,128)} %get-tuple-element.53.mine), calls=%async_computation | async-start | bytes 65536 | tf_op jit(solution)/shard_map/all_to_all | solution.py:353
  60.1 9.8 %all-to-all-start.1 = ((f32[8,1,128]{2,1,0:T(1,128)}), f32[8,1,128]{2,1,0:T(1,128)S(1)}, u32[]{:S(2)}, u32[]{:S(2)}) async-start(f32[8,1,128]{2,1,0:T(1,128)} %bitcast.10), calls=%async_computation.1 | async-start | bytes 8192 | tf_op jit(solution)/shard_map/all_to_all | solution.py:367

commit v6 on v4

--- a/solution.py
+++ b/solution.py
@@ -55,19 +55,20 @@
 def norm_kernel(at, hid, gain, weights, *refs):
     more = refs[:-3]
     normed, sumsq, acc = refs[-3:]
-    tok, feats = hid.shape
-    line = at[0] // LANES
-    nb = tok // LANES
-    sumsq[...] = more[0][...] if more else jnp.zeros_like(sumsq)
-    for b in range(nb):
-        rows = pl.ds(b * LANES, LANES)
-        folded = None
-        for t in range(feats // LANES):
-            lanes = pl.ds(t * LANES, LANES)
-            raw = hid[rows, lanes].astype(F32)
-            folded = raw * raw if folded is None else folded + raw * raw
-            normed[rows, lanes] = (raw * gain[pl.ds(line + t, 1), :]).astype(BF16)
-        sumsq[b : b + 1, :] += to_lanes(jnp.sum(folded, axis=1, keepdims=True))
+    b = pl.program_id(0)
+    line = at[0]
+
+    @pl.when(b == 0)
+    def _():
+        sumsq[...] = more[0][...] if more else jnp.zeros_like(sumsq)
+
+    folded = None
+    for t in range(hid.shape[1] // LANES):
+        lanes = pl.ds(t * LANES, LANES)
+        raw = hid[:, lanes].astype(F32)
+        folded = raw * raw if folded is None else folded + raw * raw
+        normed[:, lanes] = (raw * gain[pl.ds(line + t, 1), :]).astype(BF16)
+    sumsq[pl.ds(b, 1), :] += to_lanes(jnp.sum(folded, axis=1, keepdims=True))
     out = jnp.dot(normed[...], weights[...], preferred_element_type=F32)
     acc[...] = out + more[1][...] if more else out
 
@@ -271,17 +272,24 @@
             [lax.dynamic_slice_in_dim(m, start, count) for m in (key_matrix, value_matrix)], axis=1
         )
 
-    def cross(o, block):
-        chip = (x - o) % n_x
+    def crossing(block):
         return [
-            lax.ppermute(
-                rows_at((chip * CORES + (c ^ part)) * feats + block * q, q), "head", shift_x(-o)
-            )
-            for part in range(CORES)
+            [
+                rows_at(((x - o) % n_x * CORES + (c ^ part)) * feats + block * q, q)
+                for part in range(CORES)
+            ]
+            for o in offsets
         ]
 
-    firsts = [cross(o, i) for o in offsets]
-    seconds = [cross(o, 3 - i) for o in offsets]
+    def cross(rows):
+        return [
+            [lax.ppermute(rows[o - 1][part], "head", shift_x(-o)) for part in range(CORES)]
+            for o in offsets
+        ]
+
+    firsts = cross(crossing(i))
+    seconds = cross(crossing(3 - i))
+    own = [rows_at(start * feats, feats) for start in (h, h ^ 1)]
     swapped = lax.ppermute(hidden, "head", [(j, j ^ 1) for j in range(n_head)])
     blocks = [
         [
@@ -296,17 +304,24 @@
     lines = -(-(tok // LANES) // 8) * 8
     gain_lines = gain.reshape(full_width // LANES, LANES)
 
-    def norm(start, rows, more):
-        weights = rows_at(start, feats)
-        return call(
+    def norm(core, rows, own, more):
+        line = pl.BlockSpec((LANES, feats), lambda b: (b, 0))
+        product = pl.BlockSpec((LANES, 2 * head), lambda b: (b, 0))
+        sums = pl.BlockSpec((lines, LANES), lambda b: (0, 0))
+        return pl.pallas_call(
             norm_kernel,
-            [sds((tok, feats), BF16), sds((lines, LANES), F32), sds((tok, 2 * head), F32)],
-            [SMEM] + [VMEM] * (3 + len(more)),
-            flops=1 << 30,
-        )(start.reshape(1), rows, gain_lines, weights, *more)
-
-    mine, sumsq, acc = norm(h * feats, hidden, ())
-    other, sumsq, acc = norm((h ^ 1) * feats, swapped, (sumsq, acc))
+            grid=(tok // LANES,),
+            out_shape=[
+                sds((tok, feats), BF16), sds((lines, LANES), F32), sds((tok, 2 * head), F32)
+            ],
+            in_specs=[SMEM, line, VMEM, VMEM] + ([sums, product] if more else []),
+            out_specs=[line, sums, product],
+            cost_estimate=pl.CostEstimate(flops=1 << 30, bytes_accessed=1 << 20, transcendentals=0),
+            compiler_params=pltpu.CompilerParams(vmem_limit_bytes=40 << 20),
+        )((core * (feats // LANES)).reshape(1), rows, gain_lines, own, *more)
+
+    mine, sumsq, acc = norm(h, hidden, own[0], ())
+    other, sumsq, acc = norm(h ^ 1, swapped, own[1], (sumsq, acc))
     sqs = [sumsq] + [lax.ppermute(sumsq, "head", shift_x(o)) for o in offsets]
 
     parts_k, parts_v = [], []

time: 69.8 us -> 70.6 us (1.011)
  Pallas kernels: 12.5 us -> 13.9 us
  local copies, waits for them, and re-layouts: 5.35 us -> 4.62 us
    pallas_call x2, Pallas kernels: 3.95 us -> 4.93 us  [norm(): pl.pallas_call(norm_kernel, grid=(tok // LANES,), out_shape=[sds((tok, fe...]
    dynamic_slice x2, local copies, waits for them, and re-layouts: 3.74 us -> 3.01 us  [rows_at(): lax.dynamic_slice_in_dim(m, start, count)]
    unnamed x10 -> x6, local copies, waits for them, and re-layouts: 1.61 us -> 1.6 us
  transfers between devices with their start and end apart: 14 -> 14, of which waited for: 5 -> 5; matrix products, arithmetic and copies ran while one was open for 15% -> 14% of each run, Pallas kernels for 12% -> 14%
where the time goes in v6:
time: 70.6 us; the launch traced here: 70 us
  starting transfers between devices  24.8 us (35%)
  waiting for transfers between devices  17.4 us (25%)
  Pallas kernels  13.9 us (20%)
  other arithmetic  6.53 us (9%)
  local copies, waits for them, and re-layouts  4.62 us (7%)
  between operations  2.75 us (4%)
    ppermute x4, starting transfers between devices, local(): lax.ppermute(firsts[o - 1][part], 'seq', flip(bit))  6.79 us
    ppermute x4, starting transfers between devices, cross(): lax.ppermute(rows[o - 1][part], 'head', shift_x(-o))  6.62 us
    all_to_all x1, waiting for transfers between devices, local(): said = lax.all_to_all(spread, 'seq', 0, 0, tiled=True)  6.35 us
    all_to_all x1, waiting for transfers between devices, local(): got = lax.all_to_all(stats, 'seq', 0, 0, tiled=True)  5.78 us
    pallas_call x2, Pallas kernels, norm(): pl.pallas_call(norm_kernel, grid=(tok // LANES,), out_shape=[sds((tok, fe...  4.93 us
    ppermute x4, waiting for transfers between devices, cross(): lax.ppermute(rows[o - 1][part], 'head', shift_x(-o))  4.06 us
    all_to_all x1, starting transfers between devices, local(): got = lax.all_to_all(stats, 'seq', 0, 0, tiled=True)  3.87 us
    all_to_all x1, starting transfers between devices, local(): said = lax.all_to_all(spread, 'seq', 0, 0, tiled=True)  3.27 us
  transfers between devices with their start and end apart: 14, of which 5 were waited for; matrix products, arithmetic and copies ran while one was open for 14% of the time, Pallas kernels for 14%

profile of v6, /device:TPU:0, one launch (start us, length us, event | category | flops | bytes accessed | tf_op | source)
XLA Modules:
  0.0 70.0 jit_solution(16183577090231705045)
XLA Ops:
  1.2 1.4 %constant_dynamic-slice_fusion = (bf16[512,128]{1,0:T(8,128)(2,1)S(1)}, bf16[512,128]{1,0:T(8,128)(2,1)S(1)}, bf16[512,128]{1,0:T(8,128)(2,1)S(1)}, bf16[512,128...) fusion(bf16[8192,128]{1,0:T(8,128)(2,1)} %param.11, ...), kind=kLoop, calls=%fused_computation.12 | loop fusion | bytes 2097168 | tf_op jit(solution)/shard_map/dynamic_slice | solution.py:272
  3.3 2.6 %collective-permute-start.1 = (bf16[512,256]{1,0:T(8,128)(2,1)}, bf16[512,256]{1,0:T(8,128)(2,1)}, u32[]{:S(2)}, u32[]{:S(2)}) collective-permute-start(bf16[512,256]{1,0:T(8,128)(2,1)} %pad_maximum_fusion.2), channel_id=1, source_target_pairs={{0,2},{1,3},{2,0},{3,1},{4,6},{5,7},{6,4},{7,5},{8,10},{9,11},{10,... | collective-permute-start | bytes 786440 | tf_op jit(solution)/shard_map/ppermute | solution.py:286
  7.4 2.0 %collective-permute-start.5 = (bf16[512,256]{1,0:T(8,128)(2,1)}, bf16[512,256]{1,0:T(8,128)(2,1)S(1)}, u32[]{:S(2)}, u32[]{:S(2)}) collective-permute-start(bf16[512,256]{1,0:T(8,128)(2,1)} %pad_maximum_fusion.4), channel_id=1, source_target_pairs={{0,2},{1,3},{2,0},{3,1},{4,6},{5,7},{6,4},{7,5},{8,10},{9,11},{10,... | collective-permute-start | bytes 786440 | tf_op jit(solution)/shard_map/ppermute | solution.py:286
  9.4 1.7 %constant_dynamic-slice_fusion.8 = (bf16[2048,128]{1,0:T(8,128)(2,1)S(1)}, bf16[2048,128]{1,0:T(8,128)(2,1)S(1)}, bf16[2048,128]{1,0:T(8,128)(2,1)S(1)}, bf16[2048,128]{1,0:T(8,128)(2,1)S(1)}) fusion(bf16[8192,128]{1,0:T(8,128)(2,1)} %param.11, s32[]{:T(128)S(6)} %select_n.69, s32[]{:T(128)S(6)} %select_n.68, bf16[8192,128]{1,0:T(8,128)(2,1)} %param.10), kind=kLoop, calls=%fused_computation.20 | loop fusion | bytes 4194312 | tf_op jit(solution)/shard_map/dynamic_slice | solution.py:272
  11.3 1.8 %fusion = (f32[512,64]{1,0:T(8,128)S(1)}, f32[512,64]{1,0:T(8,128)S(1)}, f32[512,64]{1,0:T(8,128)}) fusion(f32[64]{0:T(128)S(1)} %multiply_power_fusion, f32[512]{0:T(512)S(1)} %add_convert_fusion), kind=kLoop, calls=%fused_computation.10 | loop fusion | flops 65536 | bytes 395520 | tf_op jit(solution)/shard_map/neg | solution.py:350
  15.1 1.6 %collective-permute-start.3 = (bf16[512,256]{1,0:T(8,128)(2,1)}, bf16[512,256]{1,0:T(8,128)(2,1)S(1)}, u32[]{:S(2)}, u32[]{:S(2)}) collective-permute-start(bf16[512,256]{1,0:T(8,128)(2,1)} %collective-permute-done.1.a0), channel_id=1, source_target_pairs={{0,4},{4,0},{8,12},{12,8},{16,20},{20,16},{24,28},{28,24},{1,5},{5... | collective-permute-start | bytes 786440 | tf_op jit(solution)/shard_map/ppermute | solution.py:297
  16.7 1.6 %collective-permute-start.4 = (bf16[512,256]{1,0:T(8,128)(2,1)}, bf16[512,256]{1,0:T(8,128)(2,1)S(1)}, u32[]{:S(2)}, u32[]{:S(2)}) collective-permute-start(bf16[512,256]{1,0:T(8,128)(2,1)} %collective-permute-done.1.a0), channel_id=1, source_target_pairs={{0,8},{4,12},{8,0},{12,4},{16,24},{20,28},{24,16},{28,20},{1,9},{5... | collective-permute-start | bytes 786440 | tf_op jit(solution)/shard_map/ppermute | solution.py:297
  18.9 2.0 %collective-permute-start.8 = (bf16[512,256]{1,0:T(8,128)(2,1)}, bf16[512,256]{1,0:T(8,128)(2,1)S(1)}, u32[]{:S(2)}, u32[]{:S(2)}) collective-permute-start(bf16[512,256]{1,0:T(8,128)(2,1)} %pad_maximum_fusion.5), channel_id=1, source_target_pairs={{0,2},{1,3},{2,0},{3,1},{4,6},{5,7},{6,4},{7,5},{8,10},{9,11},{10,... | collective-permute-start | bytes 786440 | tf_op jit(solution)/shard_map/ppermute | solution.py:286
  21.0 3.5 %collective-permute-done.5.a3 = bf16[512,256]{1,0:T(8,128)(2,1)S(1)} collective-permute-done((bf16[512,256]{1,0:T(8,128)(2,1)}, bf16[512,256]{1,0:T(8,128)(2,1)S(1)}, u32[]{:S(2)}, u32[]{:S(2)}) %collective-permute-start.5) | collective-permute-done | bytes 262176 | tf_op jit(solution)/shard_map/ppermute | solution.py:286
  24.5 2.1 %collective-permute-start.6 = (bf16[512,256]{1,0:T(8,128)(2,1)}, bf16[512,256]{1,0:T(8,128)(2,1)S(1)}, u32[]{:S(2)}, u32[]{:S(2)}) collective-permute-start(bf16[512,256]{1,0:T(8,128)(2,1)} %collective-permute-done.2.b0), channel_id=1, source_target_pairs={{0,4},{4,0},{8,12},{12,8},{16,20},{20,16},{24,28},{28,24},{1,5},{5... | collective-permute-start | bytes 786440 | tf_op jit(solution)/shard_map/ppermute | solution.py:297
  26.5 1.6 %collective-permute-start.7 = (bf16[512,256]{1,0:T(8,128)(2,1)}, bf16[512,256]{1,0:T(8,128)(2,1)S(1)}, u32[]{:S(2)}, u32[]{:S(2)}) collective-permute-start(bf16[512,256]{1,0:T(8,128)(2,1)} %collective-permute-done.2.b0), channel_id=1, source_target_pairs={{0,8},{4,12},{8,0},{12,4},{16,24},{20,28},{24,16},{28,20},{1,9},{5... | collective-permute-start | bytes 786440 | tf_op jit(solution)/shard_map/ppermute | solution.py:297
  28.1 1.6 %copy-done.1 = bf16[512,2048]{1,0:T(8,128)(2,1)S(1)} copy-done((bf16[512,2048]{1,0:T(8,128)(2,1)S(1)}, bf16[512,2048]{1,0:T(8,128)(2,1)}, u32[]{:S(2)}) %copy-start.1) | copy-done | bytes 2097176
  29.7 1.6 %shard_map.95 = (bf16[512,2048]{1,0:T(8,128)(2,1)S(1)}, f32[8,128]{1,0:T(8,128)S(1)}, f32[512,256]{1,0:T(8,128)S(1)}) custom-call(s32[1]{0:T(128)} %bitcast.4.at, bf16[512,2048]{1,0:T(8,128)(2,1)S(1)} %copy-done.1, f32[64,128]{1,0:T(8,128)S(1)} %bitcast.15, bf16[2048,256]{1,0:T(8,128)(2,1)S(1)} %pad_maximum_fusion.1.weights), custom_call_target="tpu_custom_call" | custom-call | flops 1073741824 | bytes 1048576 | tf_op jit(solution)/shard_map/pallas_call | solution.py:311
  31.3 3.3 %shard_map.96 = (bf16[512,2048]{1,0:T(8,128)(2,1)S(1)}, f32[8,128]{1,0:T(8,128)S(1)}, f32[512,256]{1,0:T(8,128)S(1)}) custom-call(s32[1]{0:T(128)} %bitcast.2.at, bf16[512,2048]{1,0:T(8,128)(2,1)} %collective-permute-done.hid, f32[64,128]{1,0:T(8,128)S(1)} %bitcast.16, bf16[2048,256]{1,0:T(8,128)(2,1)S(1)} %pad_maximum_fusion.weights, ...), custom_call_target="tpu_custom_call" | custom-call | flops 1073741824 | bytes 1048576 | tf_op jit(solution)/shard_map/pallas_call | solution.py:311
  34.6 1.5 %shard_map.97.total = f32[512,256]{1,0:T(8,128)S(1)} custom-call(s32[4]{0:T(128)S(1)} %pad_add_fusion.2.at, bf16[512,2048]{1,0:T(8,128)(2,1)S(1)} %get-tuple-element.18.mine, bf16[512,2048]{1,0:T(8,128)(2,1)S(1)} %get-tuple-element.17.other, bf16[512,256]{1,0:T(8,128)(2,1)} %collective-permute-done.1.a0, bf16[512,256]{1,0:T(8,128)(2,1)} %collective-permute-done.2.b0), custom_call_target="tpu_custom_call" | custom-call | flops 536870912 | bytes 1048576 | tf_op jit(solution)/shard_map/pallas_call | solution.py:332
  38.5 1.6 %collective-permute-start.9 = (bf16[512,128]{1,0:T(8,128)(2,1)S(1)}, bf16[512,128]{1,0:T(8,128)(2,1)S(1)}, u32[]{:S(2)}, u32[]{:S(2)}) collective-permute-start(bf16[512,128]{1,0:T(8,128)(2,1)S(1)} %get-tuple-element.19), channel_id=1, source_target_pairs={{0,2},{1,3},{2,0},{3,1},{4,6},{5,7},{6,4},{7,5},{8,10},{9,11},{10,... | collective-permute-start | bytes 393224 | tf_op jit(solution)/shard_map/ppermute | solution.py:341
  41.9 1.6 %collective-permute-start.11 = (bf16[512,128]{1,0:T(8,128)(2,1)S(1)}, bf16[512,128]{1,0:T(8,128)(2,1)S(1)}, u32[]{:S(2)}, u32[]{:S(2)}) collective-permute-start(bf16[512,128]{1,0:T(8,128)(2,1)S(1)} %get-tuple-element.23), channel_id=1, source_target_pairs={{0,2},{1,3},{2,0},{3,1},{4,6},{5,7},{6,4},{7,5},{8,10},{9,11},{10,... | collective-permute-start | bytes 393224 | tf_op jit(solution)/shard_map/ppermute | solution.py:342
  44.7 1.8 %shard_map.100 = (f32[512,512]{1,0:T(8,128)S(1)}, f32[8,2,512]{2,1,0:T(2,128)}) custom-call(s32[1]{0:T(128)} %bitcast.1.first, f32[512,256]{1,0:T(8,128)S(1)} %get-tuple-element.16.refs_0_, bf16[512,128]{1,0:T(8,128)(2,1)S(1)} %collective-permute-done.9.refs_1_, f32[8,128]{1,0:T(8,128)S(1)} %get-tuple-element.20.refs_2_, ...), custom_call_target="tpu_custom_call" | custom-call | flops 268435456 | bytes 1048576 | tf_op jit(solution)/shard_map/pallas_call | solution.py:357
  46.5 3.9 %all-to-all-start = ((f32[8,2,512]{2,1,0:T(2,128)}), f32[8,2,512]{2,1,0:T(2,128)S(1)}, u32[]{:S(2)}, u32[]{:S(2)}) async-start(f32[8,2,512]{2,1,0:T(2,128)} %get-tuple-element.21.mine), calls=%async_computation | async-start | bytes 65536 | tf_op jit(solution)/shard_map/all_to_all | solution.py:364
  51.2 5.8 %all-to-all-done.got = f32[8,2,512]{2,1,0:T(2,128)S(1)} async-done(((f32[8,2,512]{2,1,0:T(2,128)}), f32[8,2,512]{2,1,0:T(2,128)S(1)}, u32[]{:S(2)}, u32[]{:S(2)}) %all-to-all-start) | async-done | bytes 32800 | tf_op jit(solution)/shard_map/all_to_all | solution.py:364
  57.0 1.8 %shard_map.102 = f32[8,128]{1,0:T(8,128)} custom-call(s32[2]{0:T(128)S(1)} %pad_add_fusion.1.sizes, f32[8,2,512]{2,1,0:T(2,128)S(1)} %all-to-all-done.got, f32[8,2,512]{2,1,0:T(2,128)} %get-tuple-element.21.mine, f32[512,512]{1,0:T(8,128)S(1)} %get-tuple-element.22.expo, f32[8,128]{1,0:T(8,128)S(1)} %shard_map.101.vmag, s32[1,512]{1,0:T(1,128)S(1)} %and_select_fusion.win), custom_call_target="tpu_custom_call" | custom-call | flops 67108864 | bytes 1048576 | tf_op jit(solution)/shard_map/pallas_call | solution.py:372
  58.8 3.3 %all-to-all-start.1 = ((f32[8,1,128]{2,1,0:T(1,128)}), f32[8,1,128]{2,1,0:T(1,128)S(1)}, u32[]{:S(2)}, u32[]{:S(2)}) async-start(f32[8,1,128]{2,1,0:T(1,128)} %bitcast.10), calls=%async_computation.1 | async-start | bytes 8192 | tf_op jit(solution)/shard_map/all_to_all | solution.py:378
  62.2 6.3 %all-to-all-done.1 = f32[8,1,128]{2,1,0:T(1,128)S(1)} async-done(((f32[8,1,128]{2,1,0:T(1,128)}), f32[8,1,128]{2,1,0:T(1,128)S(1)}, u32[]{:S(2)}, u32[]{:S(2)}) %all-to-all-start.1) | async-done | bytes 4128 | tf_op jit(solution)/shard_map/all_to_all | solution.py:378
  68.5 1.5 %shard_map.103 = (f32[1,4]{1,0:T(1,128)}, f32[1,1]{1,0:T(1,128)}) custom-call(s32[3]{0:T(128)S(1)} %pad_add_fusion.sizes, f32[8,128]{1,0:T(8,128)S(1)} %bitcast.14), custom_call_target="tpu_custom_call" | custom-call | flops 1048576 | bytes 1048576 | tf_op jit(solution)/shard_map/pallas_call | solution.py:379
  (36 shorter events, 10.1 us)
Async XLA Ops:
  0.6 25.9 %collective-permute-start = (bf16[512,2048]{1,0:T(8,128)(2,1)}, bf16[512,2048]{1,0:T(8,128)(2,1)}, u32[]{:S(2)}, u32[]{:S(2)}) collective-permute-start(bf16[512,2048]{1,0:T(8,128)(2,1)} %hid.1), channel_id=1, source_target_pairs={{0,1},{1,0},{2,3},{3,2},{4,5},{5,4},{6,7},{7,6},{8,9},{9,8},{10,11... | collective-permute-start | bytes 6291464 | tf_op jit(solution)/shard_map/ppermute | solution.py:293
  3.3 11.8 %collective-permute-start.1 = (bf16[512,256]{1,0:T(8,128)(2,1)}, bf16[512,256]{1,0:T(8,128)(2,1)}, u32[]{:S(2)}, u32[]{:S(2)}) collective-permute-start(bf16[512,256]{1,0:T(8,128)(2,1)} %pad_maximum_fusion.2), channel_id=1, source_target_pairs={{0,2},{1,3},{2,0},{3,1},{4,6},{5,7},{6,4},{7,5},{8,10},{9,11},{10,... | collective-permute-start | bytes 786440 | tf_op jit(solution)/shard_map/ppermute | solution.py:286
  6.6 12.3 %collective-permute-start.2 = (bf16[512,256]{1,0:T(8,128)(2,1)}, bf16[512,256]{1,0:T(8,128)(2,1)}, u32[]{:S(2)}, u32[]{:S(2)}) collective-permute-start(bf16[512,256]{1,0:T(8,128)(2,1)} %pad_maximum_fusion.3), channel_id=1, source_target_pairs={{0,2},{1,3},{2,0},{3,1},{4,6},{5,7},{6,4},{7,5},{8,10},{9,11},{10,... | collective-permute-start | bytes 786440 | tf_op jit(solution)/shard_map/ppermute | solution.py:286
  7.4 17.1 %collective-permute-start.5 = (bf16[512,256]{1,0:T(8,128)(2,1)}, bf16[512,256]{1,0:T(8,128)(2,1)S(1)}, u32[]{:S(2)}, u32[]{:S(2)}) collective-permute-start(bf16[512,256]{1,0:T(8,128)(2,1)} %pad_maximum_fusion.4), channel_id=1, source_target_pairs={{0,2},{1,3},{2,0},{3,1},{4,6},{5,7},{6,4},{7,5},{8,10},{9,11},{10,... | collective-permute-start | bytes 786440 | tf_op jit(solution)/shard_map/ppermute | solution.py:286
  11.2 16.9 %copy-start.2 = (f32[8192]{0:T(1024)S(1)}, f32[8192]{0:T(1024)}, u32[]{:S(2)}) copy-start(f32[8192]{0:T(1024)} %param.9) | copy-start | bytes 98308
  15.1 21.0 %collective-permute-start.3 = (bf16[512,256]{1,0:T(8,128)(2,1)}, bf16[512,256]{1,0:T(8,128)(2,1)S(1)}, u32[]{:S(2)}, u32[]{:S(2)}) collective-permute-start(bf16[512,256]{1,0:T(8,128)(2,1)} %collective-permute-done.1.a0), channel_id=1, source_target_pairs={{0,4},{4,0},{8,12},{12,8},{16,20},{20,16},{24,28},{28,24},{1,5},{5... | collective-permute-start | bytes 786440 | tf_op jit(solution)/shard_map/ppermute | solution.py:297
  16.7 19.4 %collective-permute-start.4 = (bf16[512,256]{1,0:T(8,128)(2,1)}, bf16[512,256]{1,0:T(8,128)(2,1)S(1)}, u32[]{:S(2)}, u32[]{:S(2)}) collective-permute-start(bf16[512,256]{1,0:T(8,128)(2,1)} %collective-permute-done.1.a0), channel_id=1, source_target_pairs={{0,8},{4,12},{8,0},{12,4},{16,24},{20,28},{24,16},{28,20},{1,9},{5... | collective-permute-start | bytes 786440 | tf_op jit(solution)/shard_map/ppermute | solution.py:297
  18.9 18.3 %collective-permute-start.8 = (bf16[512,256]{1,0:T(8,128)(2,1)}, bf16[512,256]{1,0:T(8,128)(2,1)S(1)}, u32[]{:S(2)}, u32[]{:S(2)}) collective-permute-start(bf16[512,256]{1,0:T(8,128)(2,1)} %pad_maximum_fusion.5), channel_id=1, source_target_pairs={{0,2},{1,3},{2,0},{3,1},{4,6},{5,7},{6,4},{7,5},{8,10},{9,11},{10,... | collective-permute-start | bytes 786440 | tf_op jit(solution)/shard_map/ppermute | solution.py:286
  24.5 12.8 %collective-permute-start.6 = (bf16[512,256]{1,0:T(8,128)(2,1)}, bf16[512,256]{1,0:T(8,128)(2,1)S(1)}, u32[]{:S(2)}, u32[]{:S(2)}) collective-permute-start(bf16[512,256]{1,0:T(8,128)(2,1)} %collective-permute-done.2.b0), channel_id=1, source_target_pairs={{0,4},{4,0},{8,12},{12,8},{16,20},{20,16},{24,28},{28,24},{1,5},{5... | collective-permute-start | bytes 786440 | tf_op jit(solution)/shard_map/ppermute | solution.py:297
  26.5 10.8 %collective-permute-start.7 = (bf16[512,256]{1,0:T(8,128)(2,1)}, bf16[512,256]{1,0:T(8,128)(2,1)S(1)}, u32[]{:S(2)}, u32[]{:S(2)}) collective-permute-start(bf16[512,256]{1,0:T(8,128)(2,1)} %collective-permute-done.2.b0), channel_id=1, source_target_pairs={{0,8},{4,12},{8,0},{12,4},{16,24},{20,28},{24,16},{28,20},{1,9},{5... | collective-permute-start | bytes 786440 | tf_op jit(solution)/shard_map/ppermute | solution.py:297
  28.1 1.6 %copy-start.1 = (bf16[512,2048]{1,0:T(8,128)(2,1)S(1)}, bf16[512,2048]{1,0:T(8,128)(2,1)}, u32[]{:S(2)}) copy-start(bf16[512,2048]{1,0:T(8,128)(2,1)} %hid.1) | copy-start | bytes 6291460
  37.3 7.4 %copy-start = (bf16[64,1024]{1,0:T(8,128)(2,1)S(1)}, bf16[64,1024]{1,0:T(8,128)(2,1)}, u32[]{:S(2)}) copy-start(bf16[64,1024]{1,0:T(8,128)(2,1)} %refs_6_.1) | copy-start | bytes 393220
  38.5 6.2 %collective-permute-start.9 = (bf16[512,128]{1,0:T(8,128)(2,1)S(1)}, bf16[512,128]{1,0:T(8,128)(2,1)S(1)}, u32[]{:S(2)}, u32[]{:S(2)}) collective-permute-start(bf16[512,128]{1,0:T(8,128)(2,1)S(1)} %get-tuple-element.19), channel_id=1, source_target_pairs={{0,2},{1,3},{2,0},{3,1},{4,6},{5,7},{6,4},{7,5},{8,10},{9,11},{10,... | collective-permute-start | bytes 393224 | tf_op jit(solution)/shard_map/ppermute | solution.py:341
  40.0 4.6 %collective-permute-start.10 = (f32[8,128]{1,0:T(8,128)S(1)}, f32[8,128]{1,0:T(8,128)S(1)}, u32[]{:S(2)}, u32[]{:S(2)}) collective-permute-start(f32[8,128]{1,0:T(8,128)S(1)} %get-tuple-element.20.refs_2_), channel_id=1, source_target_pairs={{0,2},{1,3},{2,0},{3,1},{4,6},{5,7},{6,4},{7,5},{8,10},{9,11},{10,... | collective-permute-start | bytes 12296 | tf_op jit(solution)/shard_map/ppermute | solution.py:325
  41.9 9.2 %collective-permute-start.11 = (bf16[512,128]{1,0:T(8,128)(2,1)S(1)}, bf16[512,128]{1,0:T(8,128)(2,1)S(1)}, u32[]{:S(2)}, u32[]{:S(2)}) collective-permute-start(bf16[512,128]{1,0:T(8,128)(2,1)S(1)} %get-tuple-element.23), channel_id=1, source_target_pairs={{0,2},{1,3},{2,0},{3,1},{4,6},{5,7},{6,4},{7,5},{8,10},{9,11},{10,... | collective-permute-start | bytes 393224 | tf_op jit(solution)/shard_map/ppermute | solution.py:342
  46.5 10.6 %all-to-all-start = ((f32[8,2,512]{2,1,0:T(2,128)}), f32[8,2,512]{2,1,0:T(2,128)S(1)}, u32[]{:S(2)}, u32[]{:S(2)}) async-start(f32[8,2,512]{2,1,0:T(2,128)} %get-tuple-element.21.mine), calls=%async_computation | async-start | bytes 65536 | tf_op jit(solution)/shard_map/all_to_all | solution.py:364
  58.8 9.7 %all-to-all-start.1 = ((f32[8,1,128]{2,1,0:T(1,128)}), f32[8,1,128]{2,1,0:T(1,128)S(1)}, u32[]{:S(2)}, u32[]{:S(2)}) async-start(f32[8,1,128]{2,1,0:T(1,128)} %bitcast.10), calls=%async_computation.1 | async-start | bytes 8192 | tf_op jit(solution)/shard_map/all_to_all | solution.py:378
